TPU v7x, 32 devices: a whole 2x2x4 slice. The times are simulated.
32 devices in a mesh: group: 4 (over z), patch: 8 (over y, x, core).
Axes of the slice: x: 2, y: 2, z: 4, core: 2. Of those that a mesh axis runs over, the one named last changes fastest.
Arguments:
- node_latent: bfloat16 [10240, 512], P(('group', 'patch')), may hold values from -6 to 6
- fine_latent: bfloat16 [65536, 512], P(('group', 'patch')), may hold values from -6 to 6
- coarse_latent: bfloat16 [16384, 512], P(('group', 'patch')), may hold values from -6 to 6
- fine_sender: int32 [65536], P(('group', 'patch')), may hold values from 0 to 447
- fine_receiver: int32 [65536], P(('group', 'patch')), may hold values from 0 to 319
- coarse_owner: int32 [16384, 1], P(('group', 'patch')), may hold values from 0 to 31; in each aligned block of 512 rows (0 to 511, 512 to 1023, ...) at most 32 rows name the same one
- coarse_row: int32 [16384], P(('group', 'patch')), may hold values from 0 to 15
- coarse_receiver: int32 [16384], P(('group', 'patch')), may hold values from 0 to 15
- edge_first: bfloat16 [2, 1536, 512], replicated, may hold values from -0.15625 to 0.15625
- edge_bias: float32 [2, 512], replicated, may hold values from -3 to 3
- edge_second: bfloat16 [2, 512, 512], replicated, may hold values from -0.25 to 0.25
- edge_gain: float32 [2, 512], replicated, may hold values from 0.25 to 1.75
- node_first: bfloat16 [2, 1024, 512], replicated, may hold values from -0.1875 to 0.1875
- node_bias: float32 [2, 512], replicated, may hold values from -3 to 3
- node_second: bfloat16 [2, 512, 512], replicated, may hold values from -0.25 to 0.25
- node_gain: float32 [2, 512], replicated, may hold values from 0.25 to 1.75
Outputs:
- node_out: bfloat16 [10240, 512], P(('group', 'patch'))
- fine_out: bfloat16 [65536, 512], P(('group', 'patch'))
- coarse_out: bfloat16 [16384, 512], P(('group', 'patch'))
Inputs may be any that keep to these rules, and one draw needn't show every extreme that they name: `fine_sender`: A fine edge's sender indexes the receiving device's patch extended by 64 nodes on each side: values below 64 are the last 64 nodes of the previous patch of the same group, values from 384 on the first 64 nodes of the next patch; patches of a group close into a loop. `coarse_owner`: among the 512 coarse edges of one device, at most 32 have their sender on any one device.
All inputs are finite; a program needn't handle non-finite values.
Results may differ from a plain program's by a relative error of at most 0.0095.
Values may be sent and summed in bfloat16 or wider, within the bound.
No kernel may reach another device: no remote copies, remote signals or barrier semaphores. Data moves between devices by JAX's collectives and lax.ppermute only.
A program may use at most 128 MiB of HBM per device.

v0:
```python
import functools

import jax
import jax.numpy as jnp
from jax import lax
from jax.experimental import pallas as pl
from jax.experimental.pallas import tpu as pltpu
from jax.sharding import PartitionSpec as P


HALO = 64
COARSE = 16
EPSILON = 1e-05
GP = ("group", "patch")
LIMIT = 20 << 20


def dot(a, b):
    return jnp.dot(a, b, preferred_element_type=jnp.float32)


def half_silu(half):
    return half * jnp.tanh(half) + half


def centred_columns(weight):
    wide = weight.astype(jnp.float32)
    return (wide - jnp.mean(wide, axis=-1, keepdims=True)).astype(jnp.bfloat16)


def scale_rows(centred, gain_row):
    variance = jnp.mean(centred * centred, axis=-1, keepdims=True)
    return centred * lax.rsqrt(variance + EPSILON) * gain_row


def column_of(row):
    return jnp.transpose(jnp.broadcast_to(row, (128, row.shape[1])))


def onehot_lanes(column, count):
    lanes = lax.broadcasted_iota(jnp.int32, column.shape, 1)
    parts = [
        jnp.where(column == lanes + start, 1.0, 0.0).astype(jnp.bfloat16)
        for start in range(0, count, 128)
    ]
    return jnp.concatenate(parts, axis=1)


def onehot_sublanes(row, count):
    places = lax.broadcasted_iota(jnp.int32, (count, row.shape[1]), 0)
    return jnp.where(places == row, 1.0, 0.0).astype(jnp.bfloat16)


def edge_rows(latent, ends, table, weight_edge, weight_second, gain_row):
    half = dot(latent, weight_edge) + dot(ends, table)
    hidden = half_silu(half).astype(jnp.bfloat16)
    message = scale_rows(dot(hidden, weight_second), gain_row)
    updated = (latent.astype(jnp.float32) + message).astype(jnp.bfloat16)
    return updated, message.astype(jnp.bfloat16)


def fine_kernel(
    layer, sub, e_ref, snd_ref, rcv_ref, h_ref, lo_ref, hi_ref, first_ref, bias_ref, second_ref, gain_ref,
    out_ref, agg_ref, table, w_edge, w_second,
):
    nodes, width = h_ref.shape
    senders = nodes + 2 * HALO
    steps, _, block = snd_ref.shape
    w_s = first_ref[layer, width : 2 * width, :]
    h = h_ref[...]
    table[0:HALO, :] = (dot(lo_ref[...], w_s) * 0.5).astype(jnp.bfloat16)
    table[HALO : HALO + nodes, :] = (dot(h, w_s) * 0.5).astype(jnp.bfloat16)
    table[HALO + nodes : senders, :] = (dot(hi_ref[...], w_s) * 0.5).astype(jnp.bfloat16)
    received = dot(h, first_ref[layer, 2 * width :, :]) + bias_ref[layer : layer + 1, :]
    table[senders:, :] = (received * 0.5).astype(jnp.bfloat16)
    w_edge[...] = (first_ref[layer, 0:width, :] * 0.5).astype(jnp.bfloat16)
    w_second[...] = centred_columns(second_ref[layer])
    agg_ref[...] = jnp.zeros_like(agg_ref)
    gain_row = gain_ref[layer : layer + 1, :]

    @pl.loop(0, steps)
    def _(step):
        total = agg_ref[...]
        base = pl.multiple_of(step * block, block)
        for start in range(0, block, sub):
            snd = snd_ref[step, :, start : start + sub]
            rcv = rcv_ref[step, :, start : start + sub]
            from_sender = column_of(snd)
            from_receiver = column_of(rcv) + senders
            lanes = lax.broadcasted_iota(jnp.int32, from_sender.shape, 1)
            parts = []
            for place in range(0, senders + nodes, 128):
                hit = None
                if place < senders:
                    hit = from_sender == lanes + place
                if place + 128 > senders:
                    other = from_receiver == lanes + place
                    hit = other if hit is None else hit | other
                parts.append(jnp.where(hit, 1.0, 0.0).astype(jnp.bfloat16))
            ends = jnp.concatenate(parts, axis=1)
            rows = pl.ds(base + start, sub)
            updated, message = edge_rows(e_ref[rows, :], ends, table[...], w_edge[...], w_second[...], gain_row)
            out_ref[rows, :] = updated
            total += dot(onehot_sublanes(rcv, nodes), message)
        agg_ref[...] = total


VMEM = pl.BlockSpec(memory_space=pltpu.VMEM)


def fine_call(layer, e, snd, rcv, h, lo, hi, first, bias, second, gain, block, sub):
    edges, width = e.shape
    nodes = h.shape[0]
    steps = edges // block
    table_rows = 2 * nodes + 2 * HALO
    return pl.pallas_call(
        functools.partial(fine_kernel, layer, sub),
        in_specs=[VMEM] * 10,
        out_specs=[VMEM] * 2,
        out_shape=[
            jax.ShapeDtypeStruct((edges, width), jnp.bfloat16),
            jax.ShapeDtypeStruct((nodes, width), jnp.float32),
        ],
        scratch_shapes=[
            pltpu.VMEM((table_rows, width), jnp.bfloat16),
            pltpu.VMEM((width, width), jnp.bfloat16),
            pltpu.VMEM((width, width), jnp.bfloat16),
        ],
        compiler_params=pltpu.CompilerParams(vmem_limit_bytes=LIMIT),
        cost_estimate=pl.CostEstimate(
            flops=2 * edges * width * (2 * width + 2 * table_rows), bytes_accessed=8 << 20, transcendentals=0
        ),
    )(e, snd.reshape(steps, 1, block), rcv.reshape(steps, 1, block), h, lo, hi, first, bias, second, gain)


def coarse_kernel(
    layer, sub, e_ref, own_ref, row_ref, rcv_ref, near_ref, far_ref, h_ref, agg_ref,
    first_ref, bias_ref, second_ref, gain_ref,
    node_first_ref, node_bias_ref, node_second_ref, node_gain_ref,
    out_ref, node_ref, *rest,
):
    slices, (table, total) = rest[:-2], rest[-2:]
    nodes, width = h_ref.shape
    near = near_ref.shape[0]
    count = near + far_ref.shape[0]
    w_s = first_ref[layer, width : 2 * width, :]
    table[0:near, :] = (dot(near_ref[...], w_s) * 0.5).astype(jnp.bfloat16)
    table[near:count, :] = (dot(far_ref[...], w_s) * 0.5).astype(jnp.bfloat16)
    received = dot(h_ref[0:COARSE, :], first_ref[layer, 2 * width :, :]) + bias_ref[layer : layer + 1, :]
    table[count : count + COARSE, :] = (received * 0.5).astype(jnp.bfloat16)
    table[count + COARSE :, :] = jnp.zeros((128 - COARSE, width), jnp.bfloat16)
    w_edge = (first_ref[layer, 0:width, :] * 0.5).astype(jnp.bfloat16)
    w_second = centred_columns(second_ref[layer])
    gain_row = gain_ref[layer : layer + 1, :]
    groups = lax.axis_size("group")
    patches = lax.axis_size("patch")
    my_group = lax.axis_index("group")
    my_patch = lax.axis_index("patch")
    heads = agg_ref[0:COARSE, :]
    for start in range(0, e_ref.shape[0], sub):
        rows = slice(start, start + sub)
        rcv = rcv_ref[:, rows]
        owner = own_ref[:, rows]
        patch_offset = (owner & (patches - 1)) ^ my_patch
        group_offset = (owner >> (patches.bit_length() - 1)) ^ my_group
        slot = ((patch_offset & 1) * (patches // 2) + (patch_offset >> 1)) * groups + group_offset
        place = slot * COARSE + row_ref[:, rows]
        ends = jnp.concatenate(
            [onehot_lanes(column_of(place), count), onehot_lanes(column_of(rcv), 128)], axis=1
        )
        updated, message = edge_rows(e_ref[rows, :], ends, table[...], w_edge, w_second, gain_row)
        out_ref[rows, :] = updated
        heads += dot(onehot_sublanes(rcv, COARSE), message)
    total[0:COARSE, :] = heads.astype(jnp.bfloat16)
    total[COARSE:, :] = agg_ref[COARSE:, :].astype(jnp.bfloat16)
    h = h_ref[...]
    pre = (
        dot(h, node_first_ref[layer, 0:width, :])
        + dot(total[...], node_first_ref[layer, width:, :])
        + node_bias_ref[layer : layer + 1, :]
    )
    hidden = half_silu(pre * 0.5).astype(jnp.bfloat16)
    change = scale_rows(dot(hidden, centred_columns(node_second_ref[layer])), node_gain_ref[layer : layer + 1, :])
    updated = (h.astype(jnp.float32) + change).astype(jnp.bfloat16)
    node_ref[...] = updated
    if slices:
        head, low, high = slices
        head[...] = updated[0:COARSE, :]
        low[...] = updated[0:HALO, :]
        high[...] = updated[nodes - HALO :, :]


def coarse_call(
    layer, e, owner, row, rcv, near, far, h, agg, first, bias, second, gain,
    node_first, node_bias, node_second, node_gain, sub, more,
):
    edges, width = e.shape
    nodes = h.shape[0]
    table_rows = near.shape[0] + far.shape[0] + 128
    flat = lambda a: a.reshape(1, edges)
    outs = [(edges, width), (nodes, width)]
    if more:
        outs += [(COARSE, width), (HALO, width), (HALO, width)]
    return pl.pallas_call(
        functools.partial(coarse_kernel, layer, sub),
        in_specs=[VMEM] * 16,
        out_specs=[VMEM] * len(outs),
        out_shape=[jax.ShapeDtypeStruct(s, jnp.bfloat16) for s in outs],
        scratch_shapes=[
            pltpu.VMEM((table_rows, width), jnp.bfloat16),
            pltpu.VMEM((nodes, width), jnp.bfloat16),
        ],
        compiler_params=pltpu.CompilerParams(vmem_limit_bytes=LIMIT),
        cost_estimate=pl.CostEstimate(
            flops=2 * edges * width * (3 * width + table_rows) + 6 * nodes * width * width,
            bytes_accessed=8 << 20,
            transcendentals=0,
        ),
    )(
        e, flat(owner), flat(row), flat(rcv), near, far, h, agg, first, bias, second, gain,
        node_first, node_bias, node_second, node_gain,
    )


def open_kernel(h_ref, head_ref, low_ref, high_ref, sems):
    nodes = h_ref.shape[0]
    copies = [
        pltpu.make_async_copy(h_ref.at[0:COARSE, :], head_ref, sems.at[0]),
        pltpu.make_async_copy(h_ref.at[0:HALO, :], low_ref, sems.at[1]),
        pltpu.make_async_copy(h_ref.at[nodes - HALO : nodes, :], high_ref, sems.at[2]),
    ]
    for copy in copies:
        copy.start()
    for copy in copies:
        copy.wait()


def open_call(h):
    width = h.shape[1]
    outs = [(COARSE, width), (HALO, width), (HALO, width)]
    return pl.pallas_call(
        open_kernel,
        in_specs=[pl.BlockSpec(memory_space=pl.ANY)],
        out_specs=[VMEM] * 3,
        out_shape=[jax.ShapeDtypeStruct(s, jnp.bfloat16) for s in outs],
        scratch_shapes=[pltpu.SemaphoreType.DMA((3,))],
        compiler_params=pltpu.CompilerParams(vmem_limit_bytes=1 << 20),
        cost_estimate=pl.CostEstimate(flops=10**10, bytes_accessed=1 << 20, transcendentals=0),
        name="open",
    )(h)


def swap(value, axis, bit):
    count = lax.axis_size(axis)
    return lax.ppermute(value, axis, [(i, i ^ bit) for i in range(count)])


def turn(value, axis, by):
    count = lax.axis_size(axis)
    return lax.ppermute(value, axis, [(i, (i + by) % count) for i in range(count)])


def exchange(head, low, high):
    groups = lax.axis_size("group")
    patches = lax.axis_size("patch")
    parts = [head] + [swap(head, "group", k) for k in range(1, groups)]
    below = turn(high, "patch", 1)
    above = turn(low, "patch", -1)
    line = jnp.concatenate(parts, axis=0)
    parts = [line] + [swap(line, "patch", k) for k in range(2, patches, 2)]
    near = jnp.concatenate(parts, axis=0)
    far = swap(near, "patch", 1)
    return below, above, near, far


def body(
    node_latent, fine_latent, coarse_latent, fine_sender, fine_receiver, coarse_owner, coarse_row, coarse_receiver,
    edge_first, edge_bias, edge_second, edge_gain, node_first, node_bias, node_second, node_gain,
):
    layers = edge_first.shape[0]
    h, fine, coarse = node_latent, fine_latent, coarse_latent
    head, low, high = open_call(h)
    edge_weights = (edge_first, edge_bias, edge_second, edge_gain)
    node_weights = (node_first, node_bias, node_second, node_gain)
    for layer in range(layers):
        below, above, near, far = exchange(head, low, high)
        fine, agg = fine_call(
            layer, fine, fine_sender, fine_receiver, h, below, above, *edge_weights, block=512, sub=256
        )
        last = layer == layers - 1
        out = coarse_call(
            layer, coarse, coarse_owner, coarse_row, coarse_receiver, near, far, h, agg,
            *edge_weights, *node_weights, sub=256, more=not last,
        )
        coarse, h = out[:2]
        if not last:
            head, low, high = out[2:]
    return h, fine, coarse


def solution(mesh):
    assert all(size & (size - 1) == 0 for size in mesh.shape.values())
    rows = P(GP, None)
    flat = P(GP)
    in_specs = (rows, rows, rows, flat, flat, rows, flat, flat) + (P(),) * 8
    return jax.shard_map(body, mesh=mesh, in_specs=in_specs, out_specs=(rows, rows, rows), check_vma=False)
```

profile of v0, /device:TPU:0, one launch (start us, length us, event | category | flops | bytes accessed | tf_op | source)
XLA Modules:
  0.0 65.7 jit_solution(7768614939819827470)
XLA Ops:
  0.7 1.1 %copy-done.5 = bf16[320,512]{1,0:T(8,128)(2,1)S(1)} copy-done((bf16[320,512]{1,0:T(8,128)(2,1)S(1)}, bf16[320,512]{1,0:T(8,128)(2,1)}, u32[]{:S(2)}) %copy-start.5) | copy-done | bytes 327704
  1.8 0.2 open.1
  2.0 3.1 %collective-permute-start = (bf16[16,512]{1,0:T(8,128)(2,1)S(1)}, bf16[16,512]{1,0:T(8,128)(2,1)S(1)}, u32[]{:S(2)}, u32[]{:S(2)}) collective-permute-start(bf16[16,512]{1,0:T(8,128)(2,1)S(1)} %get-tuple-element.17), channel_id=1, source_target_pairs={{0,8},{8,0},{16,24},{24,16},{1,9},{9,1},{17,25},{25,17},{2,10},{10... | collective-permute-start | bytes 49160 | tf_op jit(solution)/shard_map/ppermute | solution.py:255
  5.2 2.6 %collective-permute-start.1 = (bf16[16,512]{1,0:T(8,128)(2,1)S(1)}, bf16[16,512]{1,0:T(8,128)(2,1)S(1)}, u32[]{:S(2)}, u32[]{:S(2)}) collective-permute-start(bf16[16,512]{1,0:T(8,128)(2,1)S(1)} %get-tuple-element.17), channel_id=1, source_target_pairs={{0,16},{8,24},{16,0},{24,8},{1,17},{9,25},{17,1},{25,9},{2,18},{10... | collective-permute-start | bytes 49160 | tf_op jit(solution)/shard_map/ppermute | solution.py:255
  7.8 2.1 %collective-permute-done.1 = bf16[16,512]{1,0:T(8,128)(2,1)S(1)} collective-permute-done((bf16[16,512]{1,0:T(8,128)(2,1)S(1)}, bf16[16,512]{1,0:T(8,128)(2,1)S(1)}, u32[]{:S(2)}, u32[]{:S(2)}) %collective-permute-start.1) | collective-permute-done | bytes 16416 | tf_op jit(solution)/shard_map/ppermute | solution.py:255
  9.9 3.4 %collective-permute-done.2 = bf16[16,512]{1,0:T(8,128)(2,1)S(1)} collective-permute-done((bf16[16,512]{1,0:T(8,128)(2,1)S(1)}, bf16[16,512]{1,0:T(8,128)(2,1)S(1)}, u32[]{:S(2)}, u32[]{:S(2)}) %collective-permute-start.2) | collective-permute-done | bytes 16416 | tf_op jit(solution)/shard_map/ppermute | solution.py:255
  13.3 1.5 %collective-permute-start.3 = (bf16[64,512]{1,0:T(8,128)(2,1)S(1)}, bf16[64,512]{1,0:T(8,128)(2,1)S(1)}, u32[]{:S(2)}, u32[]{:S(2)}) collective-permute-start(bf16[64,512]{1,0:T(8,128)(2,1)S(1)} %get-tuple-element.39), channel_id=1, source_target_pairs={{0,2},{1,3},{2,0},{3,1},{4,6},{5,7},{6,4},{7,5},{8,10},{9,11},{10,... | collective-permute-start | bytes 196616 | tf_op jit(solution)/shard_map/ppermute | solution.py:255
  14.8 2.6 %collective-permute-start.8 = (bf16[64,512]{1,0:T(8,128)(2,1)S(1)}, bf16[64,512]{1,0:T(8,128)(2,1)S(1)}, u32[]{:S(2)}, u32[]{:S(2)}) collective-permute-start(bf16[64,512]{1,0:T(8,128)(2,1)S(1)} %get-tuple-element.19), channel_id=1, source_target_pairs={{0,7},{1,0},{2,1},{3,2},{4,3},{5,4},{6,5},{7,6},{8,15},{9,8},{10,9... | collective-permute-start | bytes 196616 | tf_op jit(solution)/shard_map/ppermute | solution.py:260
  17.4 1.5 %collective-permute-start.4 = (bf16[64,512]{1,0:T(8,128)(2,1)S(1)}, bf16[64,512]{1,0:T(8,128)(2,1)S(1)}, u32[]{:S(2)}, u32[]{:S(2)}) collective-permute-start(bf16[64,512]{1,0:T(8,128)(2,1)S(1)} %get-tuple-element.39), channel_id=1, source_target_pairs={{0,4},{1,5},{2,6},{3,7},{4,0},{5,1},{6,2},{7,3},{8,12},{9,13},{10,... | collective-permute-start | bytes 196616 | tf_op jit(solution)/shard_map/ppermute | solution.py:255
  19.0 2.7 %collective-permute-done.4 = bf16[64,512]{1,0:T(8,128)(2,1)S(1)} collective-permute-done((bf16[64,512]{1,0:T(8,128)(2,1)S(1)}, bf16[64,512]{1,0:T(8,128)(2,1)S(1)}, u32[]{:S(2)}, u32[]{:S(2)}) %collective-permute-start.4) | collective-permute-done | bytes 65568 | tf_op jit(solution)/shard_map/ppermute | solution.py:255
  21.7 2.4 %collective-permute-done.5 = bf16[64,512]{1,0:T(8,128)(2,1)S(1)} collective-permute-done((bf16[64,512]{1,0:T(8,128)(2,1)S(1)}, bf16[64,512]{1,0:T(8,128)(2,1)S(1)}, u32[]{:S(2)}, u32[]{:S(2)}) %collective-permute-start.5) | collective-permute-done | bytes 65568 | tf_op jit(solution)/shard_map/ppermute | solution.py:255
  24.2 0.0 copy-start.1
  24.2 0.0 copy-start.3
  24.2 0.0 copy-start.4
  24.3 0.0 copy-start.9
  24.3 0.0 copy-start.10
  24.3 0.0 copy-start.12
  24.3 0.0 copy-start.13
  24.3 9.0 %shard_map.175 = (bf16[2048,512]{1,0:T(8,128)(2,1)S(1)}, f32[320,512]{1,0:T(8,128)S(1)}) custom-call(bf16[2048,512]{1,0:T(8,128)(2,1)S(1)} %copy-done.14, s32[4,1,512]{2,1,0:T(1,128)S(1)} %bitcast.11, s32[4,1,512]{2,1,0:T(1,128)S(1)} %bitcast.13, bf16[320,512]{1,0:T(8,128)(2,1)S(1)} %copy-done.6, bf16[64,512]{1,0:T(8,128)(2,1)S(1)} %collective-permute-done.7.lo_ref, ...), custom_call_target="tpu_custom_call" | custom-call | flops 5368709120 | bytes 8388608 | tf_op jit(solution)/shard_map/pallas_call | solution.py:116
  33.4 3.2 %shard_map.176 = (bf16[512,512]{1,0:T(8,128)(2,1)S(1)}, bf16[320,512]{1,0:T(8,128)(2,1)S(1)}, bf16[16,512]{1,0:T(8,128)(2,1)S(1)}, bf16[64,512]{1,0:T(8,128)(2,1)S(1)}, bf16[64,512]{1,0:T(8,128)(2,1)S(1)}) custom-call(bf16[512,512]{1,0:T(8,128)(2,1)S(1)} %copy-done.4, s32[1,512]{1,0:T(1,128)S(1)} %bitcast.5, s32[1,512]{1,0:T(1,128)S(1)} %bitcast.7, ...), custom_call_target="tpu_custom_call" | custom-call | flops 1644167168 | bytes 8388608 | tf_op jit(solution)/shard_map/pallas_call | solution.py:204
  36.6 0.1 collective-permute-start.9
  36.7 0.8 %collective-permute-start.10 = (bf16[16,512]{1,0:T(8,128)(2,1)S(1)}, bf16[16,512]{1,0:T(8,128)(2,1)S(1)}, u32[]{:S(2)}, u32[]{:S(2)}) collective-permute-start(bf16[16,512]{1,0:T(8,128)(2,1)S(1)} %get-tuple-element.22), channel_id=1, source_target_pairs={{0,16},{8,24},{16,0},{24,8},{1,17},{9,25},{17,1},{25,9},{2,18},{10... | collective-permute-start | bytes 49160 | tf_op jit(solution)/shard_map/ppermute | solution.py:255
  37.4 3.6 %collective-permute-start.11 = (bf16[16,512]{1,0:T(8,128)(2,1)S(1)}, bf16[16,512]{1,0:T(8,128)(2,1)S(1)}, u32[]{:S(2)}, u32[]{:S(2)}) collective-permute-start(bf16[16,512]{1,0:T(8,128)(2,1)S(1)} %get-tuple-element.22), channel_id=1, source_target_pairs={{0,24},{8,16},{16,8},{24,0},{1,25},{9,17},{17,9},{25,1},{2,26},{10... | collective-permute-start | bytes 49160 | tf_op jit(solution)/shard_map/ppermute | solution.py:255
  41.0 0.3 collective-permute-done.10
  41.4 1.6 %collective-permute-done.11 = bf16[16,512]{1,0:T(8,128)(2,1)S(1)} collective-permute-done((bf16[16,512]{1,0:T(8,128)(2,1)S(1)}, bf16[16,512]{1,0:T(8,128)(2,1)S(1)}, u32[]{:S(2)}, u32[]{:S(2)}) %collective-permute-start.11) | collective-permute-done | bytes 16416 | tf_op jit(solution)/shard_map/ppermute | solution.py:255
  43.0 2.6 %collective-permute-start.17 = (bf16[64,512]{1,0:T(8,128)(2,1)S(1)}, bf16[64,512]{1,0:T(8,128)(2,1)S(1)}, u32[]{:S(2)}, u32[]{:S(2)}) collective-permute-start(bf16[64,512]{1,0:T(8,128)(2,1)S(1)} %get-tuple-element.26), channel_id=1, source_target_pairs={{0,7},{1,0},{2,1},{3,2},{4,3},{5,4},{6,5},{7,6},{8,15},{9,8},{10,9... | collective-permute-start | bytes 196616 | tf_op jit(solution)/shard_map/ppermute | solution.py:260
  45.6 0.9 %collective-permute-start.13 = (bf16[64,512]{1,0:T(8,128)(2,1)S(1)}, bf16[64,512]{1,0:T(8,128)(2,1)S(1)}, u32[]{:S(2)}, u32[]{:S(2)}) collective-permute-start(bf16[64,512]{1,0:T(8,128)(2,1)S(1)} %get-tuple-element.31), channel_id=1, source_target_pairs={{0,4},{1,5},{2,6},{3,7},{4,0},{5,1},{6,2},{7,3},{8,12},{9,13},{10,... | collective-permute-start | bytes 196616 | tf_op jit(solution)/shard_map/ppermute | solution.py:255
  46.5 1.7 %collective-permute-start.14 = (bf16[64,512]{1,0:T(8,128)(2,1)S(1)}, bf16[64,512]{1,0:T(8,128)(2,1)S(1)}, u32[]{:S(2)}, u32[]{:S(2)}) collective-permute-start(bf16[64,512]{1,0:T(8,128)(2,1)S(1)} %get-tuple-element.31), channel_id=1, source_target_pairs={{0,6},{1,7},{2,4},{3,5},{4,2},{5,3},{6,0},{7,1},{8,14},{9,15},{10,... | collective-permute-start | bytes 196616 | tf_op jit(solution)/shard_map/ppermute | solution.py:255
  48.2 2.1 %collective-permute-done.13 = bf16[64,512]{1,0:T(8,128)(2,1)S(1)} collective-permute-done((bf16[64,512]{1,0:T(8,128)(2,1)S(1)}, bf16[64,512]{1,0:T(8,128)(2,1)S(1)}, u32[]{:S(2)}, u32[]{:S(2)}) %collective-permute-start.13) | collective-permute-done | bytes 65568 | tf_op jit(solution)/shard_map/ppermute | solution.py:255
  50.3 1.4 %collective-permute-done.14 = bf16[64,512]{1,0:T(8,128)(2,1)S(1)} collective-permute-done((bf16[64,512]{1,0:T(8,128)(2,1)S(1)}, bf16[64,512]{1,0:T(8,128)(2,1)S(1)}, u32[]{:S(2)}, u32[]{:S(2)}) %collective-permute-start.14) | collective-permute-done | bytes 65568 | tf_op jit(solution)/shard_map/ppermute | solution.py:255
  51.7 10.1 %shard_map.177 = (bf16[2048,512]{1,0:T(8,128)(2,1)}, f32[320,512]{1,0:T(8,128)S(1)}) custom-call(bf16[2048,512]{1,0:T(8,128)(2,1)S(1)} %get-tuple-element.24.e_ref, s32[4,1,512]{2,1,0:T(1,128)S(1)} %bitcast.12, s32[4,1,512]{2,1,0:T(1,128)S(1)} %bitcast.14, bf16[320,512]{1,0:T(8,128)(2,1)S(1)} %get-tuple-element.23.h_ref, ...), custom_call_target="tpu_custom_call" | custom-call | flops 5368709120 | bytes 8388608 | tf_op jit(solution)/shard_map/pallas_call | solution.py:116
  61.9 3.9 %shard_map.178 = (bf16[512,512]{1,0:T(8,128)(2,1)}, bf16[320,512]{1,0:T(8,128)(2,1)}) custom-call(bf16[512,512]{1,0:T(8,128)(2,1)S(1)} %get-tuple-element.21.e_ref, s32[1,512]{1,0:T(1,128)S(1)} %bitcast.6, s32[1,512]{1,0:T(1,128)S(1)} %bitcast.8, s32[1,512]{1,0:T(1,128)S(1)} %bitcast.10, bf16[256,512]{1,0:T(8,128)(2,1)S(1)} %constant_dynamic-update-slice_fusion.15.near_ref, ...), custom_call_target="tpu_custom_call" | custom-call | flops 1644167168 | bytes 8388608 | tf_op jit(solution)/shard_map/pallas_call | solution.py:204
  (57 shorter events, 0.2 us)
Async XLA Ops:
  0.6 23.5 %copy-start = (bf16[2,1536,512]{2,1,0:T(8,128)(2,1)S(1)}, bf16[2,1536,512]{2,1,0:T(8,128)(2,1)}, u32[]{:S(2)}) copy-start(bf16[2,1536,512]{2,1,0:T(8,128)(2,1)} %first_ref.7) | copy-start | bytes 9437188
  0.6 23.5 %copy-start.2 = (bf16[2,512,512]{2,1,0:T(8,128)(2,1)S(1)}, bf16[2,512,512]{2,1,0:T(8,128)(2,1)}, u32[]{:S(2)}) copy-start(bf16[2,512,512]{2,1,0:T(8,128)(2,1)} %second_ref.7) | copy-start | bytes 3145732
  1.8 22.4 %copy-start.6 = (bf16[320,512]{1,0:T(8,128)(2,1)S(1)}, bf16[320,512]{1,0:T(8,128)(2,1)}, u32[]{:S(2)}) copy-start(bf16[320,512]{1,0:T(8,128)(2,1)} %h_ref.5) | copy-start | bytes 983044
  1.8 22.4 %copy-start.7 = (f32[2,512]{1,0:T(2,128)S(1)}, f32[2,512]{1,0:T(2,128)}, u32[]{:S(2)}) copy-start(f32[2,512]{1,0:T(2,128)} %bias_ref.7) | copy-start | bytes 12292
  1.8 22.4 %copy-start.8 = (f32[2,512]{1,0:T(2,128)S(1)}, f32[2,512]{1,0:T(2,128)}, u32[]{:S(2)}) copy-start(f32[2,512]{1,0:T(2,128)} %gain_ref.7) | copy-start | bytes 12292
  1.8 22.4 %copy-start.14 = (bf16[2048,512]{1,0:T(8,128)(2,1)S(1)}, bf16[2048,512]{1,0:T(8,128)(2,1)}, u32[]{:S(2)}) copy-start(bf16[2048,512]{1,0:T(8,128)(2,1)} %e_ref.2) | copy-start | bytes 6291460
  1.8 22.4 %copy-start.15 = (s32[2048]{0:T(1024)S(1)}, s32[2048]{0:T(1024)}, u32[]{:S(2)}) copy-start(s32[2048]{0:T(1024)} %param.19) | copy-start | bytes 24580
  1.8 22.4 %copy-start.16 = (s32[2048]{0:T(1024)S(1)}, s32[2048]{0:T(1024)}, u32[]{:S(2)}) copy-start(s32[2048]{0:T(1024)} %param.20) | copy-start | bytes 24580
  2.0 5.7 %collective-permute-start = (bf16[16,512]{1,0:T(8,128)(2,1)S(1)}, bf16[16,512]{1,0:T(8,128)(2,1)S(1)}, u32[]{:S(2)}, u32[]{:S(2)}) collective-permute-start(bf16[16,512]{1,0:T(8,128)(2,1)S(1)} %get-tuple-element.17), channel_id=1, source_target_pairs={{0,8},{8,0},{16,24},{24,16},{1,9},{9,1},{17,25},{25,17},{2,10},{10... | collective-permute-start | bytes 49160 | tf_op jit(solution)/shard_map/ppermute | solution.py:255
  5.2 4.7 %collective-permute-start.1 = (bf16[16,512]{1,0:T(8,128)(2,1)S(1)}, bf16[16,512]{1,0:T(8,128)(2,1)S(1)}, u32[]{:S(2)}, u32[]{:S(2)}) collective-permute-start(bf16[16,512]{1,0:T(8,128)(2,1)S(1)} %get-tuple-element.17), channel_id=1, source_target_pairs={{0,16},{8,24},{16,0},{24,8},{1,17},{9,25},{17,1},{25,9},{2,18},{10... | collective-permute-start | bytes 49160 | tf_op jit(solution)/shard_map/ppermute | solution.py:255
  7.7 5.5 %collective-permute-start.2 = (bf16[16,512]{1,0:T(8,128)(2,1)S(1)}, bf16[16,512]{1,0:T(8,128)(2,1)S(1)}, u32[]{:S(2)}, u32[]{:S(2)}) collective-permute-start(bf16[16,512]{1,0:T(8,128)(2,1)S(1)} %get-tuple-element.17), channel_id=1, source_target_pairs={{0,24},{8,16},{16,8},{24,0},{1,25},{9,17},{17,9},{25,1},{2,26},{10... | collective-permute-start | bytes 49160 | tf_op jit(solution)/shard_map/ppermute | solution.py:255
  13.3 5.7 %collective-permute-start.3 = (bf16[64,512]{1,0:T(8,128)(2,1)S(1)}, bf16[64,512]{1,0:T(8,128)(2,1)S(1)}, u32[]{:S(2)}, u32[]{:S(2)}) collective-permute-start(bf16[64,512]{1,0:T(8,128)(2,1)S(1)} %get-tuple-element.39), channel_id=1, source_target_pairs={{0,2},{1,3},{2,0},{3,1},{4,6},{5,7},{6,4},{7,5},{8,10},{9,11},{10,... | collective-permute-start | bytes 196616 | tf_op jit(solution)/shard_map/ppermute | solution.py:255
  14.8 9.3 %collective-permute-start.7 = (bf16[64,512]{1,0:T(8,128)(2,1)S(1)}, bf16[64,512]{1,0:T(8,128)(2,1)S(1)}, u32[]{:S(2)}, u32[]{:S(2)}) collective-permute-start(bf16[64,512]{1,0:T(8,128)(2,1)S(1)} %get-tuple-element.18), channel_id=1, source_target_pairs={{0,1},{1,2},{2,3},{3,4},{4,5},{5,6},{6,7},{7,0},{8,9},{9,10},{10,1... | collective-permute-start | bytes 196616 | tf_op jit(solution)/shard_map/ppermute | solution.py:260
  14.8 9.4 %collective-permute-start.8 = (bf16[64,512]{1,0:T(8,128)(2,1)S(1)}, bf16[64,512]{1,0:T(8,128)(2,1)S(1)}, u32[]{:S(2)}, u32[]{:S(2)}) collective-permute-start(bf16[64,512]{1,0:T(8,128)(2,1)S(1)} %get-tuple-element.19), channel_id=1, source_target_pairs={{0,7},{1,0},{2,1},{3,2},{4,3},{5,4},{6,5},{7,6},{8,15},{9,8},{10,9... | collective-permute-start | bytes 196616 | tf_op jit(solution)/shard_map/ppermute | solution.py:260
  17.4 4.3 %collective-permute-start.4 = (bf16[64,512]{1,0:T(8,128)(2,1)S(1)}, bf16[64,512]{1,0:T(8,128)(2,1)S(1)}, u32[]{:S(2)}, u32[]{:S(2)}) collective-permute-start(bf16[64,512]{1,0:T(8,128)(2,1)S(1)} %get-tuple-element.39), channel_id=1, source_target_pairs={{0,4},{1,5},{2,6},{3,7},{4,0},{5,1},{6,2},{7,3},{8,12},{9,13},{10,... | collective-permute-start | bytes 196616 | tf_op jit(solution)/shard_map/ppermute | solution.py:255
  18.9 5.2 %collective-permute-start.5 = (bf16[64,512]{1,0:T(8,128)(2,1)S(1)}, bf16[64,512]{1,0:T(8,128)(2,1)S(1)}, u32[]{:S(2)}, u32[]{:S(2)}) collective-permute-start(bf16[64,512]{1,0:T(8,128)(2,1)S(1)} %get-tuple-element.39), channel_id=1, source_target_pairs={{0,6},{1,7},{2,4},{3,5},{4,2},{5,3},{6,0},{7,1},{8,14},{9,15},{10,... | collective-permute-start | bytes 196616 | tf_op jit(solution)/shard_map/ppermute | solution.py:255
  24.1 9.2 %collective-permute-start.6 = (bf16[256,512]{1,0:T(8,128)(2,1)S(1)}, bf16[256,512]{1,0:T(8,128)(2,1)S(1)}, u32[]{:S(2)}, u32[]{:S(2)}) collective-permute-start(bf16[256,512]{1,0:T(8,128)(2,1)S(1)} %constant_dynamic-update-slice_fusion.4.near_ref), channel_id=1, source_target_pairs={{0,1},{1,0},{2,3},{3,2},{4,5},{5,4},{6,7},{7,6},{8,9},{9,8},{10,11... | collective-permute-start | bytes 786440 | tf_op jit(solution)/shard_map/ppermute | solution.py:255
  24.2 9.1 %copy-start.1 = (bf16[2,1024,512]{2,1,0:T(8,128)(2,1)S(1)}, bf16[2,1024,512]{2,1,0:T(8,128)(2,1)}, u32[]{:S(2)}) copy-start(bf16[2,1024,512]{2,1,0:T(8,128)(2,1)} %node_first_ref.3) | copy-start | bytes 6291460
  24.2 9.1 %copy-start.3 = (bf16[2,512,512]{2,1,0:T(8,128)(2,1)S(1)}, bf16[2,512,512]{2,1,0:T(8,128)(2,1)}, u32[]{:S(2)}) copy-start(bf16[2,512,512]{2,1,0:T(8,128)(2,1)} %node_second_ref.3) | copy-start | bytes 3145732
  24.2 9.1 %copy-start.4 = (bf16[512,512]{1,0:T(8,128)(2,1)S(1)}, bf16[512,512]{1,0:T(8,128)(2,1)}, u32[]{:S(2)}) copy-start(bf16[512,512]{1,0:T(8,128)(2,1)} %e_ref.3) | copy-start | bytes 1572868
  24.3 9.1 %copy-start.9 = (f32[2,512]{1,0:T(2,128)S(1)}, f32[2,512]{1,0:T(2,128)}, u32[]{:S(2)}) copy-start(f32[2,512]{1,0:T(2,128)} %node_bias_ref.3) | copy-start | bytes 12292
  24.3 9.1 %copy-start.10 = (f32[2,512]{1,0:T(2,128)S(1)}, f32[2,512]{1,0:T(2,128)}, u32[]{:S(2)}) copy-start(f32[2,512]{1,0:T(2,128)} %node_gain_ref.3) | copy-start | bytes 12292
  24.3 9.1 %copy-start.11 = (s32[512,1]{0,1:T(1,128)S(1)}, s32[512,1]{0,1:T(1,128)}, u32[]{:S(2)}) copy-start(s32[512,1]{0,1:T(1,128)} %param.21) | copy-start | bytes 6148
  36.6 4.5 %collective-permute-start.9 = (bf16[16,512]{1,0:T(8,128)(2,1)S(1)}, bf16[16,512]{1,0:T(8,128)(2,1)S(1)}, u32[]{:S(2)}, u32[]{:S(2)}) collective-permute-start(bf16[16,512]{1,0:T(8,128)(2,1)S(1)} %get-tuple-element.22), channel_id=1, source_target_pairs={{0,8},{8,0},{16,24},{24,16},{1,9},{9,1},{17,25},{25,17},{2,10},{10... | collective-permute-start | bytes 49160 | tf_op jit(solution)/shard_map/ppermute | solution.py:255
  36.7 4.7 %collective-permute-start.10 = (bf16[16,512]{1,0:T(8,128)(2,1)S(1)}, bf16[16,512]{1,0:T(8,128)(2,1)S(1)}, u32[]{:S(2)}, u32[]{:S(2)}) collective-permute-start(bf16[16,512]{1,0:T(8,128)(2,1)S(1)} %get-tuple-element.22), channel_id=1, source_target_pairs={{0,16},{8,24},{16,0},{24,8},{1,17},{9,25},{17,1},{25,9},{2,18},{10... | collective-permute-start | bytes 49160 | tf_op jit(solution)/shard_map/ppermute | solution.py:255
  37.4 5.5 %collective-permute-start.11 = (bf16[16,512]{1,0:T(8,128)(2,1)S(1)}, bf16[16,512]{1,0:T(8,128)(2,1)S(1)}, u32[]{:S(2)}, u32[]{:S(2)}) collective-permute-start(bf16[16,512]{1,0:T(8,128)(2,1)S(1)} %get-tuple-element.22), channel_id=1, source_target_pairs={{0,24},{8,16},{16,8},{24,0},{1,25},{9,17},{17,9},{25,1},{2,26},{10... | collective-permute-start | bytes 49160 | tf_op jit(solution)/shard_map/ppermute | solution.py:255
  43.0 5.2 %collective-permute-start.12 = (bf16[64,512]{1,0:T(8,128)(2,1)S(1)}, bf16[64,512]{1,0:T(8,128)(2,1)S(1)}, u32[]{:S(2)}, u32[]{:S(2)}) collective-permute-start(bf16[64,512]{1,0:T(8,128)(2,1)S(1)} %get-tuple-element.31), channel_id=1, source_target_pairs={{0,2},{1,3},{2,0},{3,1},{4,6},{5,7},{6,4},{7,5},{8,10},{9,11},{10,... | collective-permute-start | bytes 196616 | tf_op jit(solution)/shard_map/ppermute | solution.py:255
  43.0 8.8 %collective-permute-start.16 = (bf16[64,512]{1,0:T(8,128)(2,1)S(1)}, bf16[64,512]{1,0:T(8,128)(2,1)S(1)}, u32[]{:S(2)}, u32[]{:S(2)}) collective-permute-start(bf16[64,512]{1,0:T(8,128)(2,1)S(1)} %get-tuple-element.25), channel_id=1, source_target_pairs={{0,1},{1,2},{2,3},{3,4},{4,5},{5,6},{6,7},{7,0},{8,9},{9,10},{10,1... | collective-permute-start | bytes 196616 | tf_op jit(solution)/shard_map/ppermute | solution.py:260
  43.0 8.8 %collective-permute-start.17 = (bf16[64,512]{1,0:T(8,128)(2,1)S(1)}, bf16[64,512]{1,0:T(8,128)(2,1)S(1)}, u32[]{:S(2)}, u32[]{:S(2)}) collective-permute-start(bf16[64,512]{1,0:T(8,128)(2,1)S(1)} %get-tuple-element.26), channel_id=1, source_target_pairs={{0,7},{1,0},{2,1},{3,2},{4,3},{5,4},{6,5},{7,6},{8,15},{9,8},{10,9... | collective-permute-start | bytes 196616 | tf_op jit(solution)/shard_map/ppermute | solution.py:260
  45.6 4.7 %collective-permute-start.13 = (bf16[64,512]{1,0:T(8,128)(2,1)S(1)}, bf16[64,512]{1,0:T(8,128)(2,1)S(1)}, u32[]{:S(2)}, u32[]{:S(2)}) collective-permute-start(bf16[64,512]{1,0:T(8,128)(2,1)S(1)} %get-tuple-element.31), channel_id=1, source_target_pairs={{0,4},{1,5},{2,6},{3,7},{4,0},{5,1},{6,2},{7,3},{8,12},{9,13},{10,... | collective-permute-start | bytes 196616 | tf_op jit(solution)/shard_map/ppermute | solution.py:255
  46.5 5.2 %collective-permute-start.14 = (bf16[64,512]{1,0:T(8,128)(2,1)S(1)}, bf16[64,512]{1,0:T(8,128)(2,1)S(1)}, u32[]{:S(2)}, u32[]{:S(2)}) collective-permute-start(bf16[64,512]{1,0:T(8,128)(2,1)S(1)} %get-tuple-element.31), channel_id=1, source_target_pairs={{0,6},{1,7},{2,4},{3,5},{4,2},{5,3},{6,0},{7,1},{8,14},{9,15},{10,... | collective-permute-start | bytes 196616 | tf_op jit(solution)/shard_map/ppermute | solution.py:255
  51.7 10.1 %collective-permute-start.15 = (bf16[256,512]{1,0:T(8,128)(2,1)S(1)}, bf16[256,512]{1,0:T(8,128)(2,1)S(1)}, u32[]{:S(2)}, u32[]{:S(2)}) collective-permute-start(bf16[256,512]{1,0:T(8,128)(2,1)S(1)} %constant_dynamic-update-slice_fusion.15.near_ref), channel_id=1, source_target_pairs={{0,1},{1,0},{2,3},{3,2},{4,5},{5,4},{6,7},{7,6},{8,9},{9,8},{10,11... | collective-permute-start | bytes 786440 | tf_op jit(solution)/shard_map/ppermute | solution.py:255
  (3 other events, 19.3 us)
where the time goes:
time: 65.9 us; the launch traced here: 65.7 us
  Pallas kernels  26.3 us (40%)
  starting transfers between devices  21 us (32%)
  waiting for transfers between devices  16.1 us (24%)
  local copies, waits for them, and re-layouts  1.26 us (2%)
  between operations  1 us (2%)
    pallas_call x2, Pallas kernels, fine_call(): pl.pallas_call(functools.partial(fine_kernel, layer, sub), in_specs=[VMEM...  19.1 us
    ppermute x14, waiting for transfers between devices, swap(): return lax.ppermute(value, axis, [(i, i ^ bit) for i in range(count)])  16.1 us
    ppermute x14, starting transfers between devices, swap(): return lax.ppermute(value, axis, [(i, i ^ bit) for i in range(count)])  15.8 us
    pallas_call x2, Pallas kernels, coarse_call(): pl.pallas_call(functools.partial(coarse_kernel, layer, sub), in_specs=[VM...  7.03 us
    ppermute x4, starting transfers between devices, turn(): lax.ppermute(value, axis, [(i, (i + by) % count) for i in range(count)])  5.28 us
  transfers between devices with their start and end apart: 18, of which 8 were waited for; matrix products, arithmetic and copies ran while one was open for 0% of the time, Pallas kernels for 29%

commit v1 on v0

--- a/solution.py
+++ b/solution.py
@@ -78,10 +78,9 @@
     agg_ref[...] = jnp.zeros_like(agg_ref)
     gain_row = gain_ref[layer : layer + 1, :]
 
-    @pl.loop(0, steps)
-    def _(step):
+    def run(step):
         total = agg_ref[...]
-        base = pl.multiple_of(step * block, block)
+        base = step * block
         for start in range(0, block, sub):
             snd = snd_ref[step, :, start : start + sub]
             rcv = rcv_ref[step, :, start : start + sub]
@@ -103,6 +102,9 @@
             out_ref[rows, :] = updated
             total += dot(onehot_sublanes(rcv, nodes), message)
         agg_ref[...] = total
+
+    for step in range(steps):
+        run(step)
 
 
 VMEM = pl.BlockSpec(memory_space=pltpu.VMEM)
@@ -133,93 +135,133 @@
     )(e, snd.reshape(steps, 1, block), rcv.reshape(steps, 1, block), h, lo, hi, first, bias, second, gain)
 
 
-def coarse_kernel(
-    layer, sub, e_ref, own_ref, row_ref, rcv_ref, near_ref, far_ref, h_ref, agg_ref,
-    first_ref, bias_ref, second_ref, gain_ref,
-    node_first_ref, node_bias_ref, node_second_ref, node_gain_ref,
-    out_ref, node_ref, *rest,
-):
-    slices, (table, total) = rest[:-2], rest[-2:]
-    nodes, width = h_ref.shape
+def near_kernel(
+    layer, e_ref, own_ref, row_ref, rcv_ref, near_ref, h_ref, first_ref, bias_ref, second_ref,
+    node_first_ref, node_bias_ref, node_second_ref,
+    pre_ref, far_hot_ref, head_hot_ref, second_out, node_pre_ref, node_second_out, table,
+):
+    _, width = h_ref.shape
     near = near_ref.shape[0]
-    count = near + far_ref.shape[0]
-    w_s = first_ref[layer, width : 2 * width, :]
-    table[0:near, :] = (dot(near_ref[...], w_s) * 0.5).astype(jnp.bfloat16)
-    table[near:count, :] = (dot(far_ref[...], w_s) * 0.5).astype(jnp.bfloat16)
-    received = dot(h_ref[0:COARSE, :], first_ref[layer, 2 * width :, :]) + bias_ref[layer : layer + 1, :]
-    table[count : count + COARSE, :] = (received * 0.5).astype(jnp.bfloat16)
-    table[count + COARSE :, :] = jnp.zeros((128 - COARSE, width), jnp.bfloat16)
-    w_edge = (first_ref[layer, 0:width, :] * 0.5).astype(jnp.bfloat16)
-    w_second = centred_columns(second_ref[layer])
-    gain_row = gain_ref[layer : layer + 1, :]
     groups = lax.axis_size("group")
     patches = lax.axis_size("patch")
-    my_group = lax.axis_index("group")
-    my_patch = lax.axis_index("patch")
-    heads = agg_ref[0:COARSE, :]
-    for start in range(0, e_ref.shape[0], sub):
-        rows = slice(start, start + sub)
-        rcv = rcv_ref[:, rows]
-        owner = own_ref[:, rows]
-        patch_offset = (owner & (patches - 1)) ^ my_patch
-        group_offset = (owner >> (patches.bit_length() - 1)) ^ my_group
-        slot = ((patch_offset & 1) * (patches // 2) + (patch_offset >> 1)) * groups + group_offset
-        place = slot * COARSE + row_ref[:, rows]
-        ends = jnp.concatenate(
-            [onehot_lanes(column_of(place), count), onehot_lanes(column_of(rcv), 128)], axis=1
-        )
-        updated, message = edge_rows(e_ref[rows, :], ends, table[...], w_edge, w_second, gain_row)
-        out_ref[rows, :] = updated
-        heads += dot(onehot_sublanes(rcv, COARSE), message)
-    total[0:COARSE, :] = heads.astype(jnp.bfloat16)
-    total[COARSE:, :] = agg_ref[COARSE:, :].astype(jnp.bfloat16)
-    h = h_ref[...]
-    pre = (
-        dot(h, node_first_ref[layer, 0:width, :])
-        + dot(total[...], node_first_ref[layer, width:, :])
-        + node_bias_ref[layer : layer + 1, :]
-    )
-    hidden = half_silu(pre * 0.5).astype(jnp.bfloat16)
-    change = scale_rows(dot(hidden, centred_columns(node_second_ref[layer])), node_gain_ref[layer : layer + 1, :])
-    updated = (h.astype(jnp.float32) + change).astype(jnp.bfloat16)
-    node_ref[...] = updated
-    if slices:
-        head, low, high = slices
-        head[...] = updated[0:COARSE, :]
-        low[...] = updated[0:HALO, :]
-        high[...] = updated[nodes - HALO :, :]
-
-
-def coarse_call(
-    layer, e, owner, row, rcv, near, far, h, agg, first, bias, second, gain,
-    node_first, node_bias, node_second, node_gain, sub, more,
+    table[0:near, :] = (dot(near_ref[...], first_ref[layer, width : 2 * width, :]) * 0.5).astype(jnp.bfloat16)
+    received = dot(h_ref[0:COARSE, :], first_ref[layer, 2 * width :, :]) + bias_ref[layer : layer + 1, :]
+    table[near : near + COARSE, :] = (received * 0.5).astype(jnp.bfloat16)
+    table[near + COARSE :, :] = jnp.zeros((128 - COARSE, width), jnp.bfloat16)
+    w_edge = (first_ref[layer, 0:width, :] * 0.5).astype(jnp.bfloat16)
+    owner = own_ref[...]
+    rcv = rcv_ref[...]
+    patch_offset = (owner & (patches - 1)) ^ lax.axis_index("patch")
+    group_offset = (owner >> (patches.bit_length() - 1)) ^ lax.axis_index("group")
+    slot = ((patch_offset & 1) * (patches // 2) + (patch_offset >> 1)) * groups + group_offset
+    place = column_of(slot * COARSE + row_ref[...])
+    ends = jnp.concatenate([onehot_lanes(place, near), onehot_lanes(column_of(rcv), 128)], axis=1)
+    pre_ref[...] = dot(e_ref[...], w_edge) + dot(ends, table[...])
+    far_hot_ref[...] = onehot_lanes(place - near, near)
+    head_hot_ref[...] = onehot_sublanes(rcv, COARSE)
+    second_out[...] = centred_columns(second_ref[layer])
+    node_pre = dot(h_ref[...], node_first_ref[layer, 0:width, :]) + node_bias_ref[layer : layer + 1, :]
+    node_pre_ref[...] = node_pre
+    node_second_out[...] = centred_columns(node_second_ref[layer])
+
+
+def near_call(
+    layer, e, owner, row, rcv, near, h, first, bias, second, node_first, node_bias, node_second,
 ):
     edges, width = e.shape
     nodes = h.shape[0]
-    table_rows = near.shape[0] + far.shape[0] + 128
+    count = near.shape[0]
     flat = lambda a: a.reshape(1, edges)
-    outs = [(edges, width), (nodes, width)]
-    if more:
-        outs += [(COARSE, width), (HALO, width), (HALO, width)]
+    outs = [
+        ((edges, width), jnp.float32),
+        ((edges, count), jnp.bfloat16),
+        ((COARSE, edges), jnp.bfloat16),
+        ((width, width), jnp.bfloat16),
+        ((nodes, width), jnp.float32),
+        ((width, width), jnp.bfloat16),
+    ]
     return pl.pallas_call(
-        functools.partial(coarse_kernel, layer, sub),
-        in_specs=[VMEM] * 16,
+        functools.partial(near_kernel, layer),
+        in_specs=[VMEM] * 12,
         out_specs=[VMEM] * len(outs),
-        out_shape=[jax.ShapeDtypeStruct(s, jnp.bfloat16) for s in outs],
-        scratch_shapes=[
-            pltpu.VMEM((table_rows, width), jnp.bfloat16),
-            pltpu.VMEM((nodes, width), jnp.bfloat16),
-        ],
+        out_shape=[jax.ShapeDtypeStruct(*o) for o in outs],
+        scratch_shapes=[pltpu.VMEM((count + 128, width), jnp.bfloat16)],
         compiler_params=pltpu.CompilerParams(vmem_limit_bytes=LIMIT),
         cost_estimate=pl.CostEstimate(
-            flops=2 * edges * width * (3 * width + table_rows) + 6 * nodes * width * width,
-            bytes_accessed=8 << 20,
+            flops=2 * edges * width * (width + count + 128), bytes_accessed=4 << 20, transcendentals=0
+        ),
+    )(
+        e, flat(owner), flat(row), flat(rcv), near, h, first, bias, second, node_first, node_bias, node_second,
+    )
+
+
+def far_kernel(
+    layer, last, e_ref, pre_ref, far_hot_ref, head_hot_ref, w_second, node_pre_ref, node_second, far_ref, h_ref,
+    agg_ref, fine_ref, first_ref, gain_ref, node_first_ref, node_gain_ref, *rest,
+):
+    nodes, width = h_ref.shape
+    if last:
+        out_hbm, node_ref, fine_hbm, out_ref, sems = rest
+        fine_copy = pltpu.make_async_copy(fine_ref, fine_hbm, sems.at[0])
+        fine_copy.start()
+    else:
+        out_ref, node_ref, head_ref, low_ref, high_ref = rest
+    table = (dot(far_ref[...], first_ref[layer, width : 2 * width, :]) * 0.5).astype(jnp.bfloat16)
+    half = pre_ref[...] + dot(far_hot_ref[...], table)
+    hidden = half_silu(half).astype(jnp.bfloat16)
+    message = scale_rows(dot(hidden, w_second[...]), gain_ref[layer : layer + 1, :])
+    out_ref[...] = (e_ref[...].astype(jnp.float32) + message).astype(jnp.bfloat16)
+    if last:
+        out_copy = pltpu.make_async_copy(out_ref, out_hbm, sems.at[1])
+        out_copy.start()
+    heads = agg_ref[0:COARSE, :] + dot(head_hot_ref[...], message.astype(jnp.bfloat16))
+    w_total = node_first_ref[layer, width:, :]
+    node_gain = node_gain_ref[layer : layer + 1, :]
+    for start, stop, total in ((COARSE, nodes, agg_ref[COARSE:, :]), (0, COARSE, heads)):
+        pre = node_pre_ref[start:stop, :] + dot(total.astype(jnp.bfloat16), w_total)
+        node_hidden = half_silu(pre * 0.5).astype(jnp.bfloat16)
+        change = scale_rows(dot(node_hidden, node_second[...]), node_gain)
+        updated = (h_ref[start:stop, :].astype(jnp.float32) + change).astype(jnp.bfloat16)
+        node_ref[start:stop, :] = updated
+        if not last:
+            if start == 0:
+                head_ref[...] = updated
+                low_ref[0:COARSE, :] = updated
+            else:
+                low_ref[COARSE:, :] = updated[0 : HALO - COARSE, :]
+                high_ref[...] = updated[nodes - HALO - COARSE :, :]
+    if last:
+        fine_copy.wait()
+        out_copy.wait()
+
+
+def far_call(layer, last, e, partial, far, h, agg, fine, first, gain, node_first, node_gain):
+    edges, width = e.shape
+    nodes = h.shape[0]
+    outs = [(edges, width), (nodes, width)]
+    if last:
+        outs += [fine.shape]
+        hbm = pl.BlockSpec(memory_space=pl.ANY)
+        out_specs = [hbm, VMEM, hbm]
+        scratch = [pltpu.VMEM((edges, width), jnp.bfloat16), pltpu.SemaphoreType.DMA((2,))]
+    else:
+        outs += [(COARSE, width), (HALO, width), (HALO, width)]
+        out_specs = [VMEM] * len(outs)
+        scratch = []
+    args = (e, *partial, far, h, agg, fine, first, gain, node_first, node_gain)
+    return pl.pallas_call(
+        functools.partial(far_kernel, layer, last),
+        in_specs=[VMEM] * len(args),
+        out_specs=out_specs,
+        out_shape=[jax.ShapeDtypeStruct(s, jnp.bfloat16) for s in outs],
+        scratch_shapes=scratch,
+        compiler_params=pltpu.CompilerParams(vmem_limit_bytes=LIMIT),
+        cost_estimate=pl.CostEstimate(
+            flops=2 * edges * width * (2 * width + 2 * far.shape[0]) + 4 * nodes * width * width,
+            bytes_accessed=4 << 20,
             transcendentals=0,
         ),
-    )(
-        e, flat(owner), flat(row), flat(rcv), near, far, h, agg, first, bias, second, gain,
-        node_first, node_bias, node_second, node_gain,
-    )
+    )(*args)
 
 
 def open_kernel(h_ref, head_ref, low_ref, high_ref, sems):
@@ -281,19 +323,21 @@
     h, fine, coarse = node_latent, fine_latent, coarse_latent
     head, low, high = open_call(h)
     edge_weights = (edge_first, edge_bias, edge_second, edge_gain)
-    node_weights = (node_first, node_bias, node_second, node_gain)
     for layer in range(layers):
         below, above, near, far = exchange(head, low, high)
         fine, agg = fine_call(
-            layer, fine, fine_sender, fine_receiver, h, below, above, *edge_weights, block=512, sub=256
+            layer, fine, fine_sender, fine_receiver, h, below, above, *edge_weights, block=2048, sub=1024
         )
         last = layer == layers - 1
-        out = coarse_call(
-            layer, coarse, coarse_owner, coarse_row, coarse_receiver, near, far, h, agg,
-            *edge_weights, *node_weights, sub=256, more=not last,
+        partial = near_call(
+            layer, coarse, coarse_owner, coarse_row, coarse_receiver, near, h,
+            edge_first, edge_bias, edge_second, node_first, node_bias, node_second,
         )
+        out = far_call(layer, last, coarse, partial, far, h, agg, fine, edge_first, edge_gain, node_first, node_gain)
         coarse, h = out[:2]
-        if not last:
+        if last:
+            fine = out[2]
+        else:
             head, low, high = out[2:]
     return h, fine, coarse
 

time: 65.9 us -> 57.6 us (0.87)
  Pallas kernels: 26.3 us -> 19.4 us
  waiting for transfers between devices: 16.1 us -> 14.3 us
    pallas_call x2, Pallas kernels: 19.1 us -> 11.9 us  [fine_call(): pl.pallas_call(functools.partial(fine_kernel, layer, sub), in_specs=[VMEM...]
    ppermute x14, waiting for transfers between devices: 16.1 us -> 14.3 us  [swap(): return lax.ppermute(value, axis, [(i, i ^ bit) for i in range(count)])]
    pallas_call x2 -> x4, Pallas kernels: 7.03 us -> 7.25 us  [the longest x2 4.71 us: far_call(): pl.pallas_call(functools.partial(far_kernel, layer, last), in_specs=[VMEM...]
  transfers between devices with their start and end apart: 18 -> 18, of which waited for: 8 -> 6; matrix products, arithmetic and copies ran while one was open for 0% -> 0% of each run, Pallas kernels for 29% -> 25%
where the time goes in v1:
time: 57.6 us; the launch traced here: 57.4 us
  starting transfers between devices  21.3 us (37%)
  Pallas kernels  19.4 us (34%)
  waiting for transfers between devices  14.3 us (25%)
  local copies, waits for them, and re-layouts  1.26 us (2%)
  between operations  1.19 us (2%)
    ppermute x14, starting transfers between devices, swap(): return lax.ppermute(value, axis, [(i, i ^ bit) for i in range(count)])  16 us
    ppermute x14, waiting for transfers between devices, swap(): return lax.ppermute(value, axis, [(i, i ^ bit) for i in range(count)])  14.3 us
    pallas_call x2, Pallas kernels, fine_call(): pl.pallas_call(functools.partial(fine_kernel, layer, sub), in_specs=[VMEM...  11.9 us
    ppermute x4, starting transfers between devices, turn(): lax.ppermute(value, axis, [(i, (i + by) % count) for i in range(count)])  5.29 us
    pallas_call x2, Pallas kernels, far_call(): pl.pallas_call(functools.partial(far_kernel, layer, last), in_specs=[VMEM...  4.71 us
    pallas_call x2, Pallas kernels, near_call(): pl.pallas_call(functools.partial(near_kernel, layer), in_specs=[VMEM] * 1...  2.54 us
    unnamed x44, local copies, waits for them, and re-layouts  1.24 us
  transfers between devices with their start and end apart: 18, of which 6 were waited for; matrix products, arithmetic and copies ran while one was open for 0% of the time, Pallas kernels for 25%

profile of v1, /device:TPU:0, one launch (start us, length us, event | category | flops | bytes accessed | tf_op | source)
XLA Modules:
  0.0 57.4 jit_solution(1401868486681799351)
XLA Ops:
  0.7 1.1 %copy-done.5 = bf16[320,512]{1,0:T(8,128)(2,1)S(1)} copy-done((bf16[320,512]{1,0:T(8,128)(2,1)S(1)}, bf16[320,512]{1,0:T(8,128)(2,1)}, u32[]{:S(2)}) %copy-start.5) | copy-done | bytes 327704
  1.8 0.2 open.1
  2.0 5.1 %collective-permute-start.2 = (bf16[16,512]{1,0:T(8,128)(2,1)S(1)}, bf16[16,512]{1,0:T(8,128)(2,1)S(1)}, u32[]{:S(2)}, u32[]{:S(2)}) collective-permute-start(bf16[16,512]{1,0:T(8,128)(2,1)S(1)} %get-tuple-element.30), channel_id=1, source_target_pairs={{0,24},{8,16},{16,8},{24,0},{1,25},{9,17},{17,9},{25,1},{2,26},{10... | collective-permute-start | bytes 49160 | tf_op jit(solution)/shard_map/ppermute | solution.py:297
  7.2 0.6 %collective-permute-start = (bf16[16,512]{1,0:T(8,128)(2,1)S(1)}, bf16[16,512]{1,0:T(8,128)(2,1)S(1)}, u32[]{:S(2)}, u32[]{:S(2)}) collective-permute-start(bf16[16,512]{1,0:T(8,128)(2,1)S(1)} %get-tuple-element.30), channel_id=1, source_target_pairs={{0,8},{8,0},{16,24},{24,16},{1,9},{9,1},{17,25},{25,17},{2,10},{10... | collective-permute-start | bytes 49160 | tf_op jit(solution)/shard_map/ppermute | solution.py:297
  7.8 3.1 %collective-permute-done = bf16[16,512]{1,0:T(8,128)(2,1)S(1)} collective-permute-done((bf16[16,512]{1,0:T(8,128)(2,1)S(1)}, bf16[16,512]{1,0:T(8,128)(2,1)S(1)}, u32[]{:S(2)}, u32[]{:S(2)}) %collective-permute-start) | collective-permute-done | bytes 16416 | tf_op jit(solution)/shard_map/ppermute | solution.py:297
  10.9 0.9 %collective-permute-done.1 = bf16[16,512]{1,0:T(8,128)(2,1)S(1)} collective-permute-done((bf16[16,512]{1,0:T(8,128)(2,1)S(1)}, bf16[16,512]{1,0:T(8,128)(2,1)S(1)}, u32[]{:S(2)}, u32[]{:S(2)}) %collective-permute-start.1) | collective-permute-done | bytes 16416 | tf_op jit(solution)/shard_map/ppermute | solution.py:297
  11.8 1.6 %collective-permute-start.3 = (bf16[64,512]{1,0:T(8,128)(2,1)S(1)}, bf16[64,512]{1,0:T(8,128)(2,1)S(1)}, u32[]{:S(2)}, u32[]{:S(2)}) collective-permute-start(bf16[64,512]{1,0:T(8,128)(2,1)S(1)} %get-tuple-element.65), channel_id=1, source_target_pairs={{0,2},{1,3},{2,0},{3,1},{4,6},{5,7},{6,4},{7,5},{8,10},{9,11},{10,... | collective-permute-start | bytes 196616 | tf_op jit(solution)/shard_map/ppermute | solution.py:297
  13.4 2.6 %collective-permute-start.8 = (bf16[64,512]{1,0:T(8,128)(2,1)S(1)}, bf16[64,512]{1,0:T(8,128)(2,1)S(1)}, u32[]{:S(2)}, u32[]{:S(2)}) collective-permute-start(bf16[64,512]{1,0:T(8,128)(2,1)S(1)} %get-tuple-element.38), channel_id=1, source_target_pairs={{0,7},{1,0},{2,1},{3,2},{4,3},{5,4},{6,5},{7,6},{8,15},{9,8},{10,9... | collective-permute-start | bytes 196616 | tf_op jit(solution)/shard_map/ppermute | solution.py:302
  16.0 0.6 %collective-permute-start.5 = (bf16[64,512]{1,0:T(8,128)(2,1)S(1)}, bf16[64,512]{1,0:T(8,128)(2,1)S(1)}, u32[]{:S(2)}, u32[]{:S(2)}) collective-permute-start(bf16[64,512]{1,0:T(8,128)(2,1)S(1)} %get-tuple-element.65), channel_id=1, source_target_pairs={{0,6},{1,7},{2,4},{3,5},{4,2},{5,3},{6,0},{7,1},{8,14},{9,15},{10,... | collective-permute-start | bytes 196616 | tf_op jit(solution)/shard_map/ppermute | solution.py:297
  16.6 0.9 %collective-permute-start.4 = (bf16[64,512]{1,0:T(8,128)(2,1)S(1)}, bf16[64,512]{1,0:T(8,128)(2,1)S(1)}, u32[]{:S(2)}, u32[]{:S(2)}) collective-permute-start(bf16[64,512]{1,0:T(8,128)(2,1)S(1)} %get-tuple-element.65), channel_id=1, source_target_pairs={{0,4},{1,5},{2,6},{3,7},{4,0},{5,1},{6,2},{7,3},{8,12},{9,13},{10,... | collective-permute-start | bytes 196616 | tf_op jit(solution)/shard_map/ppermute | solution.py:297
  17.6 4.0 %collective-permute-done.4 = bf16[64,512]{1,0:T(8,128)(2,1)S(1)} collective-permute-done((bf16[64,512]{1,0:T(8,128)(2,1)S(1)}, bf16[64,512]{1,0:T(8,128)(2,1)S(1)}, u32[]{:S(2)}, u32[]{:S(2)}) %collective-permute-start.4) | collective-permute-done | bytes 65568 | tf_op jit(solution)/shard_map/ppermute | solution.py:297
  21.6 0.1 collective-permute-start.6
  21.8 0.0 copy-start.1
  21.8 0.0 copy-start.8
  21.9 0.0 copy-start.11
  21.9 6.0 %shard_map.176 = (bf16[2048,512]{1,0:T(8,128)(2,1)S(1)}, f32[320,512]{1,0:T(8,128)S(1)}) custom-call(bf16[2048,512]{1,0:T(8,128)(2,1)S(1)} %copy-done.14, s32[1,1,2048]{2,1,0:T(1,128)S(1)} %bitcast.11, s32[1,1,2048]{2,1,0:T(1,128)S(1)} %bitcast.13, bf16[320,512]{1,0:T(8,128)(2,1)S(1)} %copy-done.6, bf16[64,512]{1,0:T(8,128)(2,1)S(1)} %collective-permute-done.7.lo_ref, ...), custom_call_target="tpu_custom_call" | custom-call | flops 5368709120 | bytes 8388608 | tf_op jit(solution)/shard_map/pallas_call | solution.py:118
  27.9 0.0 copy-start.10
  28.0 1.3 %shard_map.175 = (f32[512,512]{1,0:T(8,128)S(1)}, bf16[512,256]{1,0:T(8,128)(2,1)S(1)}, bf16[16,512]{1,0:T(8,128)(2,1)S(1)}, bf16[512,512]{1,0:T(8,128)(2,1)S(1)...) custom-call(bf16[512,512]{1,0:T(8,128)(2,1)S(1)} %copy-done.4, s32[1,512]{1,0:T(1,128)S(1)} %bitcast.5, ...), custom_call_target="tpu_custom_call" | custom-call | flops 469762048 | bytes 4194304 | tf_op jit(solution)/shard_map/pallas_call | solution.py:183
  29.2 2.0 %shard_map.177 = (bf16[512,512]{1,0:T(8,128)(2,1)S(1)}, bf16[320,512]{1,0:T(8,128)(2,1)S(1)}, bf16[16,512]{1,0:T(8,128)(2,1)S(1)}, bf16[64,512]{1,0:T(8,128)(2,1)S(1)}, bf16[64,512]{1,0:T(8,128)(2,1)S(1)}) custom-call(bf16[512,512]{1,0:T(8,128)(2,1)S(1)} %copy-done.4, f32[512,512]{1,0:T(8,128)S(1)} %get-tuple-element.31.pre_ref, ...), custom_call_target="tpu_custom_call" | custom-call | flops 1140850688 | bytes 4194304 | tf_op jit(solution)/shard_map/pallas_call | solution.py:252
  31.2 1.6 %collective-permute-start.11 = (bf16[16,512]{1,0:T(8,128)(2,1)S(1)}, bf16[16,512]{1,0:T(8,128)(2,1)S(1)}, u32[]{:S(2)}, u32[]{:S(2)}) collective-permute-start(bf16[16,512]{1,0:T(8,128)(2,1)S(1)} %get-tuple-element.42), channel_id=1, source_target_pairs={{0,24},{8,16},{16,8},{24,0},{1,25},{9,17},{17,9},{25,1},{2,26},{10... | collective-permute-start | bytes 49160 | tf_op jit(solution)/shard_map/ppermute | solution.py:297
  32.8 0.6 %collective-permute-start.10 = (bf16[16,512]{1,0:T(8,128)(2,1)S(1)}, bf16[16,512]{1,0:T(8,128)(2,1)S(1)}, u32[]{:S(2)}, u32[]{:S(2)}) collective-permute-start(bf16[16,512]{1,0:T(8,128)(2,1)S(1)} %get-tuple-element.42), channel_id=1, source_target_pairs={{0,16},{8,24},{16,0},{24,8},{1,17},{9,25},{17,1},{25,9},{2,18},{10... | collective-permute-start | bytes 49160 | tf_op jit(solution)/shard_map/ppermute | solution.py:297
  33.4 2.3 %collective-permute-start.9 = (bf16[16,512]{1,0:T(8,128)(2,1)S(1)}, bf16[16,512]{1,0:T(8,128)(2,1)S(1)}, u32[]{:S(2)}, u32[]{:S(2)}) collective-permute-start(bf16[16,512]{1,0:T(8,128)(2,1)S(1)} %get-tuple-element.42), channel_id=1, source_target_pairs={{0,8},{8,0},{16,24},{24,16},{1,9},{9,1},{17,25},{25,17},{2,10},{10... | collective-permute-start | bytes 49160 | tf_op jit(solution)/shard_map/ppermute | solution.py:297
  35.7 1.9 %collective-permute-done.9 = bf16[16,512]{1,0:T(8,128)(2,1)S(1)} collective-permute-done((bf16[16,512]{1,0:T(8,128)(2,1)S(1)}, bf16[16,512]{1,0:T(8,128)(2,1)S(1)}, u32[]{:S(2)}, u32[]{:S(2)}) %collective-permute-start.9) | collective-permute-done | bytes 16416 | tf_op jit(solution)/shard_map/ppermute | solution.py:297
  37.6 1.8 %collective-permute-start.12 = (bf16[64,512]{1,0:T(8,128)(2,1)S(1)}, bf16[64,512]{1,0:T(8,128)(2,1)S(1)}, u32[]{:S(2)}, u32[]{:S(2)}) collective-permute-start(bf16[64,512]{1,0:T(8,128)(2,1)S(1)} %get-tuple-element.57), channel_id=1, source_target_pairs={{0,2},{1,3},{2,0},{3,1},{4,6},{5,7},{6,4},{7,5},{8,10},{9,11},{10,... | collective-permute-start | bytes 196616 | tf_op jit(solution)/shard_map/ppermute | solution.py:297
  39.3 2.6 %collective-permute-start.17 = (bf16[64,512]{1,0:T(8,128)(2,1)S(1)}, bf16[64,512]{1,0:T(8,128)(2,1)S(1)}, u32[]{:S(2)}, u32[]{:S(2)}) collective-permute-start(bf16[64,512]{1,0:T(8,128)(2,1)S(1)} %get-tuple-element.51), channel_id=1, source_target_pairs={{0,7},{1,0},{2,1},{3,2},{4,3},{5,4},{6,5},{7,6},{8,15},{9,8},{10,9... | collective-permute-start | bytes 196616 | tf_op jit(solution)/shard_map/ppermute | solution.py:302
  42.0 0.2 collective-permute-start.14
  42.2 0.7 %collective-permute-start.13 = (bf16[64,512]{1,0:T(8,128)(2,1)S(1)}, bf16[64,512]{1,0:T(8,128)(2,1)S(1)}, u32[]{:S(2)}, u32[]{:S(2)}) collective-permute-start(bf16[64,512]{1,0:T(8,128)(2,1)S(1)} %get-tuple-element.57), channel_id=1, source_target_pairs={{0,4},{1,5},{2,6},{3,7},{4,0},{5,1},{6,2},{7,3},{8,12},{9,13},{10,... | collective-permute-start | bytes 196616 | tf_op jit(solution)/shard_map/ppermute | solution.py:297
  42.9 3.6 %collective-permute-done.13 = bf16[64,512]{1,0:T(8,128)(2,1)S(1)} collective-permute-done((bf16[64,512]{1,0:T(8,128)(2,1)S(1)}, bf16[64,512]{1,0:T(8,128)(2,1)S(1)}, u32[]{:S(2)}, u32[]{:S(2)}) %collective-permute-start.13) | collective-permute-done | bytes 65568 | tf_op jit(solution)/shard_map/ppermute | solution.py:297
  46.6 0.7 %collective-permute-done.14 = bf16[64,512]{1,0:T(8,128)(2,1)S(1)} collective-permute-done((bf16[64,512]{1,0:T(8,128)(2,1)S(1)}, bf16[64,512]{1,0:T(8,128)(2,1)S(1)}, u32[]{:S(2)}, u32[]{:S(2)}) %collective-permute-start.14) | collective-permute-done | bytes 65568 | tf_op jit(solution)/shard_map/ppermute | solution.py:297
  47.3 5.9 %shard_map.179 = (bf16[2048,512]{1,0:T(8,128)(2,1)S(1)}, f32[320,512]{1,0:T(8,128)S(1)}) custom-call(bf16[2048,512]{1,0:T(8,128)(2,1)S(1)} %get-tuple-element.40.fine_ref.e_ref, s32[1,1,2048]{2,1,0:T(1,128)S(1)} %bitcast.12, s32[1,1,2048]{2,1,0:T(1,128)S(1)} %bitcast.14, bf16[320,512]{1,0:T(8,128)(2,1)S(1)} %get-tuple-element.43.h_ref, ...), custom_call_target="tpu_custom_call" | custom-call | flops 5368709120 | bytes 8388608 | tf_op jit(solution)/shard_map/pallas_call | solution.py:118
  53.2 1.3 %shard_map.178 = (f32[512,512]{1,0:T(8,128)S(1)}, bf16[512,256]{1,0:T(8,128)(2,1)S(1)}, bf16[16,512]{1,0:T(8,128)(2,1)S(1)}, bf16[512,512]{1,0:T(8,128)(2,1)S(1)...) custom-call(bf16[512,512]{1,0:T(8,128)(2,1)S(1)} %get-tuple-element.41.e_ref, s32[1,512]{1,0:T(1,128)S(1)} %bitcast.6, ...), custom_call_target="tpu_custom_call" | custom-call | flops 469762048 | bytes 4194304 | tf_op jit(solution)/shard_map/pallas_call | solution.py:183
  54.5 2.8 %shard_map.180 = (bf16[512,512]{1,0:T(8,128)(2,1)}, bf16[320,512]{1,0:T(8,128)(2,1)}, bf16[2048,512]{1,0:T(8,128)(2,1)}) custom-call(bf16[512,512]{1,0:T(8,128)(2,1)S(1)} %get-tuple-element.41.e_ref, f32[512,512]{1,0:T(8,128)S(1)} %get-tuple-element.44.pre_ref, bf16[512,256]{1,0:T(8,128)(2,1)S(1)} %get-tuple-element.45.far_hot_ref, ...), custom_call_target="tpu_custom_call" | custom-call | flops 1140850688 | bytes 4194304 | tf_op jit(solution)/shard_map/pallas_call | solution.py:252
  (59 shorter events, 0.2 us)
Async XLA Ops:
  0.6 21.1 %copy-start = (bf16[2,1536,512]{2,1,0:T(8,128)(2,1)S(1)}, bf16[2,1536,512]{2,1,0:T(8,128)(2,1)}, u32[]{:S(2)}) copy-start(bf16[2,1536,512]{2,1,0:T(8,128)(2,1)} %first_ref.11) | copy-start | bytes 9437188
  0.6 21.1 %copy-start.2 = (bf16[2,512,512]{2,1,0:T(8,128)(2,1)S(1)}, bf16[2,512,512]{2,1,0:T(8,128)(2,1)}, u32[]{:S(2)}) copy-start(bf16[2,512,512]{2,1,0:T(8,128)(2,1)} %second_ref.7) | copy-start | bytes 3145732
  1.8 20.0 %copy-start.6 = (bf16[320,512]{1,0:T(8,128)(2,1)S(1)}, bf16[320,512]{1,0:T(8,128)(2,1)}, u32[]{:S(2)}) copy-start(bf16[320,512]{1,0:T(8,128)(2,1)} %h_ref.7) | copy-start | bytes 983044
  1.8 20.0 %copy-start.7 = (f32[2,512]{1,0:T(2,128)S(1)}, f32[2,512]{1,0:T(2,128)}, u32[]{:S(2)}) copy-start(f32[2,512]{1,0:T(2,128)} %bias_ref.7) | copy-start | bytes 12292
  1.8 20.0 %copy-start.9 = (f32[2,512]{1,0:T(2,128)S(1)}, f32[2,512]{1,0:T(2,128)}, u32[]{:S(2)}) copy-start(f32[2,512]{1,0:T(2,128)} %gain_ref.7) | copy-start | bytes 12292
  1.8 20.0 %copy-start.14 = (bf16[2048,512]{1,0:T(8,128)(2,1)S(1)}, bf16[2048,512]{1,0:T(8,128)(2,1)}, u32[]{:S(2)}) copy-start(bf16[2048,512]{1,0:T(8,128)(2,1)} %e_ref.4) | copy-start | bytes 6291460
  1.8 20.0 %copy-start.15 = (s32[2048]{0:T(1024)S(1)}, s32[2048]{0:T(1024)}, u32[]{:S(2)}) copy-start(s32[2048]{0:T(1024)} %param.19) | copy-start | bytes 24580
  1.8 20.0 %copy-start.16 = (s32[2048]{0:T(1024)S(1)}, s32[2048]{0:T(1024)}, u32[]{:S(2)}) copy-start(s32[2048]{0:T(1024)} %param.20) | copy-start | bytes 24580
  2.0 9.8 %collective-permute-start.2 = (bf16[16,512]{1,0:T(8,128)(2,1)S(1)}, bf16[16,512]{1,0:T(8,128)(2,1)S(1)}, u32[]{:S(2)}, u32[]{:S(2)}) collective-permute-start(bf16[16,512]{1,0:T(8,128)(2,1)S(1)} %get-tuple-element.30), channel_id=1, source_target_pairs={{0,24},{8,16},{16,8},{24,0},{1,25},{9,17},{17,9},{25,1},{2,26},{10... | collective-permute-start | bytes 49160 | tf_op jit(solution)/shard_map/ppermute | solution.py:297
  7.2 4.6 %collective-permute-start.1 = (bf16[16,512]{1,0:T(8,128)(2,1)S(1)}, bf16[16,512]{1,0:T(8,128)(2,1)S(1)}, u32[]{:S(2)}, u32[]{:S(2)}) collective-permute-start(bf16[16,512]{1,0:T(8,128)(2,1)S(1)} %get-tuple-element.30), channel_id=1, source_target_pairs={{0,16},{8,24},{16,0},{24,8},{1,17},{9,25},{17,1},{25,9},{2,18},{10... | collective-permute-start | bytes 49160 | tf_op jit(solution)/shard_map/ppermute | solution.py:297
  7.2 3.7 %collective-permute-start = (bf16[16,512]{1,0:T(8,128)(2,1)S(1)}, bf16[16,512]{1,0:T(8,128)(2,1)S(1)}, u32[]{:S(2)}, u32[]{:S(2)}) collective-permute-start(bf16[16,512]{1,0:T(8,128)(2,1)S(1)} %get-tuple-element.30), channel_id=1, source_target_pairs={{0,8},{8,0},{16,24},{24,16},{1,9},{9,1},{17,25},{25,17},{2,10},{10... | collective-permute-start | bytes 49160 | tf_op jit(solution)/shard_map/ppermute | solution.py:297
  11.8 5.7 %collective-permute-start.3 = (bf16[64,512]{1,0:T(8,128)(2,1)S(1)}, bf16[64,512]{1,0:T(8,128)(2,1)S(1)}, u32[]{:S(2)}, u32[]{:S(2)}) collective-permute-start(bf16[64,512]{1,0:T(8,128)(2,1)S(1)} %get-tuple-element.65), channel_id=1, source_target_pairs={{0,2},{1,3},{2,0},{3,1},{4,6},{5,7},{6,4},{7,5},{8,10},{9,11},{10,... | collective-permute-start | bytes 196616 | tf_op jit(solution)/shard_map/ppermute | solution.py:297
  13.4 8.3 %collective-permute-start.7 = (bf16[64,512]{1,0:T(8,128)(2,1)S(1)}, bf16[64,512]{1,0:T(8,128)(2,1)S(1)}, u32[]{:S(2)}, u32[]{:S(2)}) collective-permute-start(bf16[64,512]{1,0:T(8,128)(2,1)S(1)} %get-tuple-element.37), channel_id=1, source_target_pairs={{0,1},{1,2},{2,3},{3,4},{4,5},{5,6},{6,7},{7,0},{8,9},{9,10},{10,1... | collective-permute-start | bytes 196616 | tf_op jit(solution)/shard_map/ppermute | solution.py:302
  13.4 8.3 %collective-permute-start.8 = (bf16[64,512]{1,0:T(8,128)(2,1)S(1)}, bf16[64,512]{1,0:T(8,128)(2,1)S(1)}, u32[]{:S(2)}, u32[]{:S(2)}) collective-permute-start(bf16[64,512]{1,0:T(8,128)(2,1)S(1)} %get-tuple-element.38), channel_id=1, source_target_pairs={{0,7},{1,0},{2,1},{3,2},{4,3},{5,4},{6,5},{7,6},{8,15},{9,8},{10,9... | collective-permute-start | bytes 196616 | tf_op jit(solution)/shard_map/ppermute | solution.py:302
  16.0 5.6 %collective-permute-start.5 = (bf16[64,512]{1,0:T(8,128)(2,1)S(1)}, bf16[64,512]{1,0:T(8,128)(2,1)S(1)}, u32[]{:S(2)}, u32[]{:S(2)}) collective-permute-start(bf16[64,512]{1,0:T(8,128)(2,1)S(1)} %get-tuple-element.65), channel_id=1, source_target_pairs={{0,6},{1,7},{2,4},{3,5},{4,2},{5,3},{6,0},{7,1},{8,14},{9,15},{10,... | collective-permute-start | bytes 196616 | tf_op jit(solution)/shard_map/ppermute | solution.py:297
  16.6 5.0 %collective-permute-start.4 = (bf16[64,512]{1,0:T(8,128)(2,1)S(1)}, bf16[64,512]{1,0:T(8,128)(2,1)S(1)}, u32[]{:S(2)}, u32[]{:S(2)}) collective-permute-start(bf16[64,512]{1,0:T(8,128)(2,1)S(1)} %get-tuple-element.65), channel_id=1, source_target_pairs={{0,4},{1,5},{2,6},{3,7},{4,0},{5,1},{6,2},{7,3},{8,12},{9,13},{10,... | collective-permute-start | bytes 196616 | tf_op jit(solution)/shard_map/ppermute | solution.py:297
  21.6 7.6 %collective-permute-start.6 = (bf16[256,512]{1,0:T(8,128)(2,1)S(1)}, bf16[256,512]{1,0:T(8,128)(2,1)S(1)}, u32[]{:S(2)}, u32[]{:S(2)}) collective-permute-start(bf16[256,512]{1,0:T(8,128)(2,1)S(1)} %constant_dynamic-update-slice_fusion.4.near_ref), channel_id=1, source_target_pairs={{0,1},{1,0},{2,3},{3,2},{4,5},{5,4},{6,7},{7,6},{8,9},{9,8},{10,11... | collective-permute-start | bytes 786440 | tf_op jit(solution)/shard_map/ppermute | solution.py:297
  21.8 6.1 %copy-start.1 = (bf16[2,1024,512]{2,1,0:T(8,128)(2,1)S(1)}, bf16[2,1024,512]{2,1,0:T(8,128)(2,1)}, u32[]{:S(2)}) copy-start(bf16[2,1024,512]{2,1,0:T(8,128)(2,1)} %node_first_ref.7) | copy-start | bytes 6291460
  21.8 6.1 %copy-start.3 = (bf16[2,512,512]{2,1,0:T(8,128)(2,1)S(1)}, bf16[2,512,512]{2,1,0:T(8,128)(2,1)}, u32[]{:S(2)}) copy-start(bf16[2,512,512]{2,1,0:T(8,128)(2,1)} %node_second_ref.3) | copy-start | bytes 3145732
  21.8 6.1 %copy-start.4 = (bf16[512,512]{1,0:T(8,128)(2,1)S(1)}, bf16[512,512]{1,0:T(8,128)(2,1)}, u32[]{:S(2)}) copy-start(bf16[512,512]{1,0:T(8,128)(2,1)} %e_ref.5) | copy-start | bytes 1572868
  21.8 6.1 %copy-start.8 = (f32[2,512]{1,0:T(2,128)S(1)}, f32[2,512]{1,0:T(2,128)}, u32[]{:S(2)}) copy-start(f32[2,512]{1,0:T(2,128)} %node_bias_ref.3) | copy-start | bytes 12292
  21.9 6.1 %copy-start.11 = (s32[512,1]{0,1:T(1,128)S(1)}, s32[512,1]{0,1:T(1,128)}, u32[]{:S(2)}) copy-start(s32[512,1]{0,1:T(1,128)} %param.21) | copy-start | bytes 6148
  21.9 6.1 %copy-start.12 = (s32[512]{0:T(512)S(1)}, s32[512]{0:T(512)}, u32[]{:S(2)}) copy-start(s32[512]{0:T(512)} %param.22) | copy-start | bytes 6148
  31.2 6.4 %collective-permute-start.11 = (bf16[16,512]{1,0:T(8,128)(2,1)S(1)}, bf16[16,512]{1,0:T(8,128)(2,1)S(1)}, u32[]{:S(2)}, u32[]{:S(2)}) collective-permute-start(bf16[16,512]{1,0:T(8,128)(2,1)S(1)} %get-tuple-element.42), channel_id=1, source_target_pairs={{0,24},{8,16},{16,8},{24,0},{1,25},{9,17},{17,9},{25,1},{2,26},{10... | collective-permute-start | bytes 49160 | tf_op jit(solution)/shard_map/ppermute | solution.py:297
  32.8 4.8 %collective-permute-start.10 = (bf16[16,512]{1,0:T(8,128)(2,1)S(1)}, bf16[16,512]{1,0:T(8,128)(2,1)S(1)}, u32[]{:S(2)}, u32[]{:S(2)}) collective-permute-start(bf16[16,512]{1,0:T(8,128)(2,1)S(1)} %get-tuple-element.42), channel_id=1, source_target_pairs={{0,16},{8,24},{16,0},{24,8},{1,17},{9,25},{17,1},{25,9},{2,18},{10... | collective-permute-start | bytes 49160 | tf_op jit(solution)/shard_map/ppermute | solution.py:297
  33.4 4.1 %collective-permute-start.9 = (bf16[16,512]{1,0:T(8,128)(2,1)S(1)}, bf16[16,512]{1,0:T(8,128)(2,1)S(1)}, u32[]{:S(2)}, u32[]{:S(2)}) collective-permute-start(bf16[16,512]{1,0:T(8,128)(2,1)S(1)} %get-tuple-element.42), channel_id=1, source_target_pairs={{0,8},{8,0},{16,24},{24,16},{1,9},{9,1},{17,25},{25,17},{2,10},{10... | collective-permute-start | bytes 49160 | tf_op jit(solution)/shard_map/ppermute | solution.py:297
  37.6 5.3 %collective-permute-start.12 = (bf16[64,512]{1,0:T(8,128)(2,1)S(1)}, bf16[64,512]{1,0:T(8,128)(2,1)S(1)}, u32[]{:S(2)}, u32[]{:S(2)}) collective-permute-start(bf16[64,512]{1,0:T(8,128)(2,1)S(1)} %get-tuple-element.57), channel_id=1, source_target_pairs={{0,2},{1,3},{2,0},{3,1},{4,6},{5,7},{6,4},{7,5},{8,10},{9,11},{10,... | collective-permute-start | bytes 196616 | tf_op jit(solution)/shard_map/ppermute | solution.py:297
  39.3 7.9 %collective-permute-start.16 = (bf16[64,512]{1,0:T(8,128)(2,1)S(1)}, bf16[64,512]{1,0:T(8,128)(2,1)S(1)}, u32[]{:S(2)}, u32[]{:S(2)}) collective-permute-start(bf16[64,512]{1,0:T(8,128)(2,1)S(1)} %get-tuple-element.50), channel_id=1, source_target_pairs={{0,1},{1,2},{2,3},{3,4},{4,5},{5,6},{6,7},{7,0},{8,9},{9,10},{10,1... | collective-permute-start | bytes 196616 | tf_op jit(solution)/shard_map/ppermute | solution.py:302
  39.3 7.9 %collective-permute-start.17 = (bf16[64,512]{1,0:T(8,128)(2,1)S(1)}, bf16[64,512]{1,0:T(8,128)(2,1)S(1)}, u32[]{:S(2)}, u32[]{:S(2)}) collective-permute-start(bf16[64,512]{1,0:T(8,128)(2,1)S(1)} %get-tuple-element.51), channel_id=1, source_target_pairs={{0,7},{1,0},{2,1},{3,2},{4,3},{5,4},{6,5},{7,6},{8,15},{9,8},{10,9... | collective-permute-start | bytes 196616 | tf_op jit(solution)/shard_map/ppermute | solution.py:302
  42.0 5.3 %collective-permute-start.14 = (bf16[64,512]{1,0:T(8,128)(2,1)S(1)}, bf16[64,512]{1,0:T(8,128)(2,1)S(1)}, u32[]{:S(2)}, u32[]{:S(2)}) collective-permute-start(bf16[64,512]{1,0:T(8,128)(2,1)S(1)} %get-tuple-element.57), channel_id=1, source_target_pairs={{0,6},{1,7},{2,4},{3,5},{4,2},{5,3},{6,0},{7,1},{8,14},{9,15},{10,... | collective-permute-start | bytes 196616 | tf_op jit(solution)/shard_map/ppermute | solution.py:297
  42.2 4.4 %collective-permute-start.13 = (bf16[64,512]{1,0:T(8,128)(2,1)S(1)}, bf16[64,512]{1,0:T(8,128)(2,1)S(1)}, u32[]{:S(2)}, u32[]{:S(2)}) collective-permute-start(bf16[64,512]{1,0:T(8,128)(2,1)S(1)} %get-tuple-element.57), channel_id=1, source_target_pairs={{0,4},{1,5},{2,6},{3,7},{4,0},{5,1},{6,2},{7,3},{8,12},{9,13},{10,... | collective-permute-start | bytes 196616 | tf_op jit(solution)/shard_map/ppermute | solution.py:297
  47.3 7.3 %collective-permute-start.15 = (bf16[256,512]{1,0:T(8,128)(2,1)S(1)}, bf16[256,512]{1,0:T(8,128)(2,1)S(1)}, u32[]{:S(2)}, u32[]{:S(2)}) collective-permute-start(bf16[256,512]{1,0:T(8,128)(2,1)S(1)} %constant_dynamic-update-slice_fusion.15.near_ref), channel_id=1, source_target_pairs={{0,1},{1,0},{2,3},{3,2},{4,5},{5,4},{6,7},{7,6},{8,9},{9,8},{10,11... | collective-permute-start | bytes 786440 | tf_op jit(solution)/shard_map/ppermute | solution.py:297
  (3 other events, 8.5 us)

commit v2 on v1

v2 whole, which is shorter than its diff:
```python
import functools

import jax
import jax.numpy as jnp
from jax import lax
from jax.experimental import pallas as pl
from jax.experimental.pallas import tpu as pltpu
from jax.sharding import PartitionSpec as P


HALO = 64
COARSE = 16
EPSILON = 1e-05
GP = ("group", "patch")
LIMIT = 20 << 20


def dot(a, b):
    return jnp.dot(a, b, preferred_element_type=jnp.float32)


def half_silu(half):
    return half * jnp.tanh(half) + half


def centred_columns(weight):
    wide = weight.astype(jnp.float32)
    return (wide - jnp.mean(wide, axis=-1, keepdims=True)).astype(jnp.bfloat16)


def scale_rows(centred, gain_row):
    variance = jnp.mean(centred * centred, axis=-1, keepdims=True)
    return centred * lax.rsqrt(variance + EPSILON) * gain_row


def column_of(row):
    return jnp.transpose(jnp.broadcast_to(row, (128, row.shape[1])))


def onehot_lanes(columns, start, count):
    lanes = lax.broadcasted_iota(jnp.int32, columns[0][2].shape, 1)
    parts = []
    for place in range(start, start + count, 128):
        hit = None
        for low, high, column in columns:
            if low < place + 128 and high > place:
                one = column == lanes + place
                hit = one if hit is None else hit | one
        parts.append(jnp.where(hit, 1.0, 0.0).astype(jnp.bfloat16))
    return jnp.concatenate(parts, axis=1)


def onehot_sublanes(row, count):
    places = lax.broadcasted_iota(jnp.int32, (count, row.shape[1]), 0)
    return jnp.where(places == row, 1.0, 0.0).astype(jnp.bfloat16)


def finish_rows(latent, half, weight_second, gain_row):
    hidden = half_silu(half).astype(jnp.bfloat16)
    message = scale_rows(dot(hidden, weight_second), gain_row)
    updated = (latent.astype(jnp.float32) + message).astype(jnp.bfloat16)
    return updated, message.astype(jnp.bfloat16)


def end_columns(snd, rcv, nodes):
    inner = HALO + nodes
    odd = lax.axis_index("patch") & 1
    before = 2 * nodes + odd * HALO
    after = 2 * nodes + (1 - odd) * HALO
    sender = jnp.where(snd < HALO, snd + before, jnp.where(snd < inner, snd - HALO, snd - inner + after))
    return column_of(sender), column_of(rcv + nodes)


def halves(value):
    return (value * 0.5).astype(jnp.bfloat16)


def prep_kernel(layer, h_ref, first_ref, bias_ref, second_ref, table_ref, tail_ref, w_edge, w_second):
    nodes, width = h_ref.shape
    split = table_ref.shape[0]
    h = h_ref[...]
    table_ref[0:nodes, :] = halves(dot(h, first_ref[layer, width : 2 * width, :]))
    received = halves(dot(h, first_ref[layer, 2 * width :, :]) + bias_ref[layer : layer + 1, :])
    table_ref[nodes:, :] = received[0 : split - nodes, :]
    tail_ref[...] = received[split - nodes :, :]
    w_edge[...] = halves(first_ref[layer, 0:width, :])
    w_second[...] = centred_columns(second_ref[layer])


VMEM = pl.BlockSpec(memory_space=pltpu.VMEM)


def call(kernel, args, outs, flops, scratch=(), out_specs=None, in_specs=None, limit=LIMIT):
    return pl.pallas_call(
        kernel,
        in_specs=in_specs or [VMEM] * len(args),
        out_specs=out_specs or [VMEM] * len(outs),
        out_shape=[jax.ShapeDtypeStruct(*o) for o in outs],
        scratch_shapes=list(scratch),
        compiler_params=pltpu.CompilerParams(vmem_limit_bytes=limit),
        cost_estimate=pl.CostEstimate(flops=flops, bytes_accessed=4 << 20, transcendentals=0),
    )(*args)


def prep_call(layer, h, first, bias, second):
    nodes, width = h.shape
    split = 2 * nodes // 256 * 256
    outs = [((rows, width), jnp.bfloat16) for rows in (split, 2 * nodes - split, width, width)]
    return call(functools.partial(prep_kernel, layer), (h, first, bias, second), outs, 4 * nodes * width * width)


def fine_kernel(
    layer, pieces, e_ref, snd_ref, rcv_ref, gain_ref, first_ref, w_edge, w_second, table_ref, tail_ref, sibling_ref,
    cross_ref, out_ref, agg_ref, last_table,
):
    width = e_ref.shape[1]
    nodes = agg_ref.shape[0]
    split = table_ref.shape[0]
    tail = tail_ref.shape[0]
    places = 2 * nodes + 2 * HALO
    w_s = first_ref[layer, width : 2 * width, :]
    last_table[0:tail, :] = tail_ref[...]
    last_table[tail : tail + HALO, :] = halves(dot(cross_ref[...], w_s))
    last_table[tail + HALO :, :] = halves(dot(sibling_ref[...], w_s))
    gain_row = gain_ref[layer : layer + 1, :]
    total = None
    for rows in pieces:
        rcv = rcv_ref[:, rows]
        sender, receiver = end_columns(snd_ref[:, rows], rcv, nodes)
        columns = [(0, nodes, sender), (nodes, 2 * nodes, receiver), (2 * nodes, places, sender)]
        half = (
            dot(e_ref[rows, :], w_edge[...])
            + dot(onehot_lanes(columns, 0, split), table_ref[...])
            + dot(onehot_lanes(columns, split, places - split), last_table[...])
        )
        updated, message = finish_rows(e_ref[rows, :], half, w_second[...], gain_row)
        out_ref[rows, :] = updated
        part = dot(onehot_sublanes(rcv, nodes), message)
        total = part if total is None else total + part
    agg_ref[...] = total


def fine_call(layer, pieces, e, snd, rcv, gain, first, prep, beside, across, nodes):
    edges, width = e.shape
    table, tail, w_edge, w_second = prep
    rows = tail.shape[0] + 2 * HALO
    return call(
        functools.partial(fine_kernel, layer, pieces),
        (e, snd, rcv, gain, first, w_edge, w_second, table, tail, beside, across),
        [((edges, width), jnp.bfloat16), ((nodes, width), jnp.float32)],
        2 * width * edges * (2 * width + table.shape[0] + rows + nodes),
        [pltpu.VMEM((rows, width), jnp.bfloat16)],
    )


def near_kernel(
    layer, e_ref, own_ref, row_ref, rcv_ref, near_ref, h_ref, agg_ref, w_edge, first_ref, bias_ref, node_first_ref,
    node_bias_ref, node_second_ref, node_gain_ref,
    pre_ref, far_hot_ref, head_hot_ref, head_pre_ref, node_second_out, others_ref, table,
):
    width = h_ref.shape[1]
    near = near_ref.shape[0]
    groups = lax.axis_size("group")
    patches = lax.axis_size("patch")
    table[0:near, :] = halves(dot(near_ref[...], first_ref[layer, width : 2 * width, :]))
    received = dot(h_ref[0:COARSE, :], first_ref[layer, 2 * width :, :]) + bias_ref[layer : layer + 1, :]
    table[near : near + COARSE, :] = halves(received)
    table[near + COARSE :, :] = jnp.zeros((128 - COARSE, width), jnp.bfloat16)
    owner = own_ref[...]
    rcv = rcv_ref[...]
    offset = (owner & (patches - 1)) ^ lax.axis_index("patch")
    group_offset = (owner >> (patches.bit_length() - 1)) ^ lax.axis_index("group")
    slot = ((offset & 1) * (patches // 2) + (offset >> 1)) * groups + group_offset
    place = column_of(slot * COARSE + row_ref[...])
    ends = onehot_lanes([(0, near, place), (near, near + 128, column_of(rcv + near))], 0, near + 128)
    pre_ref[...] = dot(e_ref[...], w_edge[...]) + dot(ends, table[...])
    far_hot_ref[...] = onehot_lanes([(near, 2 * near, place)], near, near)
    head_hot_ref[...] = onehot_sublanes(rcv, COARSE)
    node_pre = dot(h_ref[...], node_first_ref[layer, 0:width, :]) + node_bias_ref[layer : layer + 1, :]
    head_pre_ref[...] = node_pre[0:COARSE, :]
    node_second_out[...] = centred_columns(node_second_ref[layer])
    others_ref[...] = update_nodes(
        h_ref[COARSE:, :], node_pre[COARSE:, :], agg_ref[COARSE:, :], node_first_ref[layer, width:, :],
        node_second_out[...], node_gain_ref[layer : layer + 1, :],
    )


def update_nodes(h, node_pre, total, w_total, w_second, gain_row):
    pre = node_pre + dot(total.astype(jnp.bfloat16), w_total)
    hidden = half_silu(pre * 0.5).astype(jnp.bfloat16)
    change = scale_rows(dot(hidden, w_second), gain_row)
    return (h.astype(jnp.float32) + change).astype(jnp.bfloat16)


def near_call(
    layer, e, owner, row, rcv, near, h, agg, w_edge, first, bias, node_first, node_bias, node_second, node_gain
):
    edges, width = e.shape
    nodes = h.shape[0]
    count = near.shape[0]
    flat = lambda a: a.reshape(1, edges)
    outs = [
        ((edges, width), jnp.float32),
        ((edges, count), jnp.bfloat16),
        ((COARSE, edges), jnp.bfloat16),
        ((COARSE, width), jnp.float32),
        ((width, width), jnp.bfloat16),
        ((nodes - COARSE, width), jnp.bfloat16),
    ]
    args = (
        e, flat(owner), flat(row), flat(rcv), near, h, agg, w_edge, first, bias,
        node_first, node_bias, node_second, node_gain,
    )
    return call(
        functools.partial(near_kernel, layer), args, outs,
        2 * width * (edges * (width + count + 128) + 3 * nodes * width),
        [pltpu.VMEM((count + 128, width), jnp.bfloat16)],
    )


def far_kernel(
    layer, last, e_ref, pre_ref, far_hot_ref, head_hot_ref, head_pre_ref, node_second, others_ref, w_second, far_ref,
    h_ref, agg_ref, fine_ref, first_ref, gain_ref, node_first_ref, node_gain_ref, *rest,
):
    nodes, width = h_ref.shape
    copies = []

    def send(source, target):
        copies.append(pltpu.make_async_copy(source, target, sems.at[len(copies)]))
        copies[-1].start()

    if last:
        out_hbm, node_hbm, fine_hbm, out_ref, head_ref, sems = rest
        send(fine_ref, fine_hbm)
        send(others_ref, node_hbm.at[COARSE:nodes, :])
    else:
        out_ref, node_ref, head_ref, cross_ref, sibling_ref = rest
    table = halves(dot(far_ref[...], first_ref[layer, width : 2 * width, :]))
    half = pre_ref[...] + dot(far_hot_ref[...], table)
    updated, message = finish_rows(e_ref[...], half, w_second[...], gain_ref[layer : layer + 1, :])
    out_ref[...] = updated
    if last:
        send(out_ref, out_hbm)
    heads = agg_ref[0:COARSE, :] + dot(head_hot_ref[...], message)
    head = update_nodes(
        h_ref[0:COARSE, :], head_pre_ref[...], heads, node_first_ref[layer, width:, :], node_second[...],
        node_gain_ref[layer : layer + 1, :],
    )
    head_ref[...] = head
    if last:
        send(head_ref, node_hbm.at[0:COARSE, :])
        for copy in copies:
            copy.wait()
    else:
        others = others_ref[...]
        node_ref[0:COARSE, :] = head
        node_ref[COARSE:, :] = others
        low = jnp.concatenate([head, others[0 : HALO - COARSE, :]], axis=0)
        high = others[nodes - HALO - COARSE :, :]
        odd = (lax.axis_index("patch") & 1) == 1
        cross_ref[...] = jnp.where(odd, high, low)
        sibling_ref[...] = jnp.where(odd, low, high)


def far_call(layer, last, e, partial, w_second, far, h, agg, fine, first, gain, node_first, node_gain):
    edges, width = e.shape
    nodes = h.shape[0]
    outs = [(edges, width), (nodes, width)]
    if last:
        outs += [fine.shape]
        out_specs = [pl.BlockSpec(memory_space=pl.ANY)] * 3
        scratch = [pltpu.VMEM((n, width), jnp.bfloat16) for n in (edges, COARSE)] + [pltpu.SemaphoreType.DMA((4,))]
    else:
        outs += [(COARSE, width), (HALO, width), (HALO, width)]
        out_specs = None
        scratch = []
    args = (e, *partial, w_second, far, h, agg, fine, first, gain, node_first, node_gain)
    return call(
        functools.partial(far_kernel, layer, last), args, [(o, jnp.bfloat16) for o in outs],
        2 * width * (edges * (width + far.shape[0]) + far.shape[0] * width + 2 * nodes * width),
        scratch, out_specs,
    )


def open_kernel(h_ref, head_ref, cross_ref, sibling_ref, sems):
    nodes = h_ref.shape[0]
    odd = lax.axis_index("patch") & 1
    upper = pl.multiple_of(odd * (nodes - HALO), HALO)
    lower = pl.multiple_of((1 - odd) * (nodes - HALO), HALO)
    copies = [
        pltpu.make_async_copy(h_ref.at[0:COARSE, :], head_ref, sems.at[0]),
        pltpu.make_async_copy(h_ref.at[pl.ds(upper, HALO), :], cross_ref, sems.at[1]),
        pltpu.make_async_copy(h_ref.at[pl.ds(lower, HALO), :], sibling_ref, sems.at[2]),
    ]
    for copy in copies:
        copy.start()
    for copy in copies:
        copy.wait()


def open_call(h):
    width = h.shape[1]
    outs = [((n, width), jnp.bfloat16) for n in (COARSE, HALO, HALO)]
    return call(
        open_kernel, (h,), outs, 10**10, [pltpu.SemaphoreType.DMA((3,))],
        in_specs=[pl.BlockSpec(memory_space=pl.ANY)], limit=1 << 20,
    )


def swap(value, axis, bit):
    count = lax.axis_size(axis)
    return lax.ppermute(value, axis, [(i, i ^ bit) for i in range(count)])


def exchange(head, cross, sibling):
    groups = lax.axis_size("group")
    patches = lax.axis_size("patch")
    parts = [head] + [swap(head, "group", k) for k in range(1, groups)]
    beside = swap(sibling, "patch", 1)
    pairs = [(p, (p + (1 if p % 2 else -1)) % patches) for p in range(patches)]
    across = lax.ppermute(cross, "patch", pairs)
    line = jnp.concatenate(parts, axis=0)
    parts = [line] + [swap(line, "patch", k) for k in range(2, patches, 2)]
    near = jnp.concatenate(parts, axis=0)
    far = swap(near, "patch", 1)
    return beside, across, near, far


def body(
    node_latent, fine_latent, coarse_latent, fine_sender, fine_receiver, coarse_owner, coarse_row, coarse_receiver,
    edge_first, edge_bias, edge_second, edge_gain, node_first, node_bias, node_second, node_gain,
):
    layers = edge_first.shape[0]
    h, fine, coarse = node_latent, fine_latent, coarse_latent
    edges = fine.shape[0]
    nodes = h.shape[0]
    snd = fine_sender.reshape(1, edges)
    rcv = fine_receiver.reshape(1, edges)
    pieces = [slice(0, edges // 2), slice(edges // 2, edges)]
    head, cross, sibling = open_call(h)
    for layer in range(layers):
        last = layer == layers - 1
        beside, across, near, far = exchange(head, cross, sibling)
        prep = prep_call(layer, h, edge_first, edge_bias, edge_second)
        fine, agg = fine_call(
            layer, pieces, fine, snd, rcv, edge_gain, edge_first, prep, beside, across, nodes
        )
        partial = near_call(
            layer, coarse, coarse_owner, coarse_row, coarse_receiver, near, h, agg, prep[2],
            edge_first, edge_bias, node_first, node_bias, node_second, node_gain,
        )
        out = far_call(
            layer, last, coarse, partial, prep[3], far, h, agg, fine,
            edge_first, edge_gain, node_first, node_gain,
        )
        coarse, h = out[:2]
        if last:
            fine = out[2]
        else:
            head, cross, sibling = out[2:]
    return h, fine, coarse


def solution(mesh):
    assert all(size & (size - 1) == 0 for size in mesh.shape.values())
    rows = P(GP, None)
    flat = P(GP)
    in_specs = (rows, rows, rows, flat, flat, rows, flat, flat) + (P(),) * 8
    return jax.shard_map(body, mesh=mesh, in_specs=in_specs, out_specs=(rows, rows, rows), check_vma=False)
```

time: 57.6 us -> 56.7 us (0.984)
  waiting for transfers between devices: 14.3 us -> 13.6 us
  starting transfers between devices: 21.3 us -> 20.7 us
    ppermute x4 -> x2, starting transfers between devices: 5.29 us -> 3.22 us  [exchange(): across = lax.ppermute(cross, 'patch', pairs)]
    ppermute x14 -> x16, starting transfers between devices: 16 us -> 17.4 us  [swap(): return lax.ppermute(value, axis, [(i, i ^ bit) for i in range(count)])]
    ppermute x14 -> x16, waiting for transfers between devices: 14.3 us -> 13.6 us  [swap(): return lax.ppermute(value, axis, [(i, i ^ bit) for i in range(count)])]
    pallas_call x7 -> x9, Pallas kernels: 19.4 us -> 19.8 us  [call(): pl.pallas_call(kernel, in_specs=in_specs or [VMEM] * len(args), out_specs...]
  transfers between devices with their start and end apart: 18 -> 18, of which waited for: 6 -> 5; matrix products, arithmetic and copies ran while one was open for 0% -> 0% of each run, Pallas kernels for 25% -> 28%
where the time goes in v2:
time: 56.7 us; the launch traced here: 56.5 us
  starting transfers between devices  20.7 us (37%)
  Pallas kernels  19.8 us (35%)
  waiting for transfers between devices  13.6 us (24%)
  local copies, waits for them, and re-layouts  1.2 us (2%)
  between operations  1.18 us (2%)
    pallas_call x9, Pallas kernels, call(): pl.pallas_call(kernel, in_specs=in_specs or [VMEM] * len(args), out_specs...  19.8 us
    ppermute x16, starting transfers between devices, swap(): return lax.ppermute(value, axis, [(i, i ^ bit) for i in range(count)])  17.4 us
    ppermute x16, waiting for transfers between devices, swap(): return lax.ppermute(value, axis, [(i, i ^ bit) for i in range(count)])  13.6 us
    ppermute x2, starting transfers between devices, exchange(): across = lax.ppermute(cross, 'patch', pairs)  3.22 us
    unnamed x44, local copies, waits for them, and re-layouts  1.18 us
  transfers between devices with their start and end apart: 18, of which 5 were waited for; matrix products, arithmetic and copies ran while one was open for 0% of the time, Pallas kernels for 28%

profile of v2, /device:TPU:0, one launch (start us, length us, event | category | flops | bytes accessed | tf_op | source)
XLA Modules:
  0.0 56.5 jit_solution(3245498323146489516)
XLA Ops:
  0.7 1.1 %copy-done.4 = bf16[320,512]{1,0:T(8,128)(2,1)S(1)} copy-done((bf16[320,512]{1,0:T(8,128)(2,1)S(1)}, bf16[320,512]{1,0:T(8,128)(2,1)}, u32[]{:S(2)}) %copy-start.4) | copy-done | bytes 327704
  1.7 0.2 shard_map.175
  1.9 5.1 %collective-permute-start.2 = (bf16[16,512]{1,0:T(8,128)(2,1)S(1)}, bf16[16,512]{1,0:T(8,128)(2,1)S(1)}, u32[]{:S(2)}, u32[]{:S(2)}) collective-permute-start(bf16[16,512]{1,0:T(8,128)(2,1)S(1)} %get-tuple-element.38), channel_id=1, source_target_pairs={{0,24},{8,16},{16,8},{24,0},{1,25},{9,17},{17,9},{25,1},{2,26},{10... | collective-permute-start | bytes 49160 | tf_op jit(solution)/shard_map/ppermute | solution.py:312
  7.1 0.6 %collective-permute-start = (bf16[16,512]{1,0:T(8,128)(2,1)S(1)}, bf16[16,512]{1,0:T(8,128)(2,1)S(1)}, u32[]{:S(2)}, u32[]{:S(2)}) collective-permute-start(bf16[16,512]{1,0:T(8,128)(2,1)S(1)} %get-tuple-element.38), channel_id=1, source_target_pairs={{0,8},{8,0},{16,24},{24,16},{1,9},{9,1},{17,25},{25,17},{2,10},{10... | collective-permute-start | bytes 49160 | tf_op jit(solution)/shard_map/ppermute | solution.py:312
  7.7 3.1 %collective-permute-done = bf16[16,512]{1,0:T(8,128)(2,1)S(1)} collective-permute-done((bf16[16,512]{1,0:T(8,128)(2,1)S(1)}, bf16[16,512]{1,0:T(8,128)(2,1)S(1)}, u32[]{:S(2)}, u32[]{:S(2)}) %collective-permute-start) | collective-permute-done | bytes 16416 | tf_op jit(solution)/shard_map/ppermute | solution.py:312
  10.8 0.9 %collective-permute-done.1 = bf16[16,512]{1,0:T(8,128)(2,1)S(1)} collective-permute-done((bf16[16,512]{1,0:T(8,128)(2,1)S(1)}, bf16[16,512]{1,0:T(8,128)(2,1)S(1)}, u32[]{:S(2)}, u32[]{:S(2)}) %collective-permute-start.1) | collective-permute-done | bytes 16416 | tf_op jit(solution)/shard_map/ppermute | solution.py:312
  11.7 1.6 %collective-permute-start.3 = (bf16[64,512]{1,0:T(8,128)(2,1)S(1)}, bf16[64,512]{1,0:T(8,128)(2,1)S(1)}, u32[]{:S(2)}, u32[]{:S(2)}) collective-permute-start(bf16[64,512]{1,0:T(8,128)(2,1)S(1)} %get-tuple-element.81), channel_id=1, source_target_pairs={{0,2},{1,3},{2,0},{3,1},{4,6},{5,7},{6,4},{7,5},{8,10},{9,11},{10,... | collective-permute-start | bytes 196616 | tf_op jit(solution)/shard_map/ppermute | solution.py:312
  13.3 1.7 %collective-permute-start.7 = (bf16[64,512]{1,0:T(8,128)(2,1)S(1)}, bf16[64,512]{1,0:T(8,128)(2,1)S(1)}, u32[]{:S(2)}, u32[]{:S(2)}) collective-permute-start(bf16[64,512]{1,0:T(8,128)(2,1)S(1)} %get-tuple-element.44), channel_id=1, source_target_pairs={{0,7},{1,2},{2,1},{3,4},{4,3},{5,6},{6,5},{7,0},{8,15},{9,10},{10,... | collective-permute-start | bytes 196616 | tf_op jit(solution)/shard_map/ppermute | solution.py:321
  15.0 0.6 shard_map.176
  15.5 1.6 %collective-permute-start.5 = (bf16[64,512]{1,0:T(8,128)(2,1)S(1)}, bf16[64,512]{1,0:T(8,128)(2,1)S(1)}, u32[]{:S(2)}, u32[]{:S(2)}) collective-permute-start(bf16[64,512]{1,0:T(8,128)(2,1)S(1)} %get-tuple-element.81), channel_id=1, source_target_pairs={{0,6},{1,7},{2,4},{3,5},{4,2},{5,3},{6,0},{7,1},{8,14},{9,15},{10,... | collective-permute-start | bytes 196616 | tf_op jit(solution)/shard_map/ppermute | solution.py:312
  17.1 0.5 collective-permute-start.4
  17.6 3.9 %collective-permute-done.4 = bf16[64,512]{1,0:T(8,128)(2,1)S(1)} collective-permute-done((bf16[64,512]{1,0:T(8,128)(2,1)S(1)}, bf16[64,512]{1,0:T(8,128)(2,1)S(1)}, u32[]{:S(2)}, u32[]{:S(2)}) %collective-permute-start.4) | collective-permute-done | bytes 65568 | tf_op jit(solution)/shard_map/ppermute | solution.py:312
  21.5 0.1 collective-permute-start.8
  21.7 0.0 copy-start.1
  21.7 0.0 copy-start.7
  21.8 5.5 %shard_map.177 = (bf16[2048,512]{1,0:T(8,128)(2,1)S(1)}, f32[320,512]{1,0:T(8,128)S(1)}) custom-call(bf16[2048,512]{1,0:T(8,128)(2,1)S(1)} %copy-done.14, s32[1,2048]{1,0:T(1,128)S(1)} %bitcast.11, s32[1,2048]{1,0:T(1,128)S(1)} %bitcast.13, f32[2,512]{1,0:T(2,128)S(1)} %copy-done.9, bf16[2,1536,512]{2,1,0:T(8,128)(2,1)S(1)} %copy-done, ...), custom_call_target="tpu_custom_call" | custom-call | flops 4429185024 | bytes 4194304 | tf_op jit(solution)/shard_map/pallas_call | solution.py:94
  27.3 1.8 %shard_map.178 = (f32[512,512]{1,0:T(8,128)S(1)}, bf16[512,256]{1,0:T(8,128)(2,1)S(1)}, bf16[16,512]{1,0:T(8,128)(2,1)S(1)}, f32[16,512]{1,0:T(8,128)S(1)}, bf16...) custom-call(bf16[512,512]{1,0:T(8,128)(2,1)S(1)} %copy-done.6, s32[1,512]{1,0:T(1,128)S(1)} %bitcast.5, ...), custom_call_target="tpu_custom_call" | custom-call | flops 973078528 | bytes 4194304 | tf_op jit(solution)/shard_map/pallas_call | solution.py:94
  29.2 1.6 %shard_map.179 = (bf16[512,512]{1,0:T(8,128)(2,1)S(1)}, bf16[320,512]{1,0:T(8,128)(2,1)S(1)}, bf16[16,512]{1,0:T(8,128)(2,1)S(1)}, bf16[64,512]{1,0:T(8,128)(2,1)S(1)}, bf16[64,512]{1,0:T(8,128)(2,1)S(1)}) custom-call(bf16[512,512]{1,0:T(8,128)(2,1)S(1)} %copy-done.6, f32[512,512]{1,0:T(8,128)S(1)} %get-tuple-element.46.pre_ref, ...), custom_call_target="tpu_custom_call" | custom-call | flops 872415232 | bytes 4194304 | tf_op jit(solution)/shard_map/pallas_call | solution.py:94
  30.7 1.6 %collective-permute-start.11 = (bf16[16,512]{1,0:T(8,128)(2,1)S(1)}, bf16[16,512]{1,0:T(8,128)(2,1)S(1)}, u32[]{:S(2)}, u32[]{:S(2)}) collective-permute-start(bf16[16,512]{1,0:T(8,128)(2,1)S(1)} %get-tuple-element.54), channel_id=1, source_target_pairs={{0,24},{8,16},{16,8},{24,0},{1,25},{9,17},{17,9},{25,1},{2,26},{10... | collective-permute-start | bytes 49160 | tf_op jit(solution)/shard_map/ppermute | solution.py:312
  32.3 0.6 %collective-permute-start.10 = (bf16[16,512]{1,0:T(8,128)(2,1)S(1)}, bf16[16,512]{1,0:T(8,128)(2,1)S(1)}, u32[]{:S(2)}, u32[]{:S(2)}) collective-permute-start(bf16[16,512]{1,0:T(8,128)(2,1)S(1)} %get-tuple-element.54), channel_id=1, source_target_pairs={{0,16},{8,24},{16,0},{24,8},{1,17},{9,25},{17,1},{25,9},{2,18},{10... | collective-permute-start | bytes 49160 | tf_op jit(solution)/shard_map/ppermute | solution.py:312
  32.9 2.3 %collective-permute-start.9 = (bf16[16,512]{1,0:T(8,128)(2,1)S(1)}, bf16[16,512]{1,0:T(8,128)(2,1)S(1)}, u32[]{:S(2)}, u32[]{:S(2)}) collective-permute-start(bf16[16,512]{1,0:T(8,128)(2,1)S(1)} %get-tuple-element.54), channel_id=1, source_target_pairs={{0,8},{8,0},{16,24},{24,16},{1,9},{9,1},{17,25},{25,17},{2,10},{10... | collective-permute-start | bytes 49160 | tf_op jit(solution)/shard_map/ppermute | solution.py:312
  35.2 1.9 %collective-permute-done.9 = bf16[16,512]{1,0:T(8,128)(2,1)S(1)} collective-permute-done((bf16[16,512]{1,0:T(8,128)(2,1)S(1)}, bf16[16,512]{1,0:T(8,128)(2,1)S(1)}, u32[]{:S(2)}, u32[]{:S(2)}) %collective-permute-start.9) | collective-permute-done | bytes 16416 | tf_op jit(solution)/shard_map/ppermute | solution.py:312
  37.1 1.3 %collective-permute-start.12 = (bf16[64,512]{1,0:T(8,128)(2,1)S(1)}, bf16[64,512]{1,0:T(8,128)(2,1)S(1)}, u32[]{:S(2)}, u32[]{:S(2)}) collective-permute-start(bf16[64,512]{1,0:T(8,128)(2,1)S(1)} %get-tuple-element.73), channel_id=1, source_target_pairs={{0,2},{1,3},{2,0},{3,1},{4,6},{5,7},{6,4},{7,5},{8,10},{9,11},{10,... | collective-permute-start | bytes 196616 | tf_op jit(solution)/shard_map/ppermute | solution.py:312
  38.5 1.6 %collective-permute-start.16 = (bf16[64,512]{1,0:T(8,128)(2,1)S(1)}, bf16[64,512]{1,0:T(8,128)(2,1)S(1)}, u32[]{:S(2)}, u32[]{:S(2)}) collective-permute-start(bf16[64,512]{1,0:T(8,128)(2,1)S(1)} %get-tuple-element.61), channel_id=1, source_target_pairs={{0,7},{1,2},{2,1},{3,4},{4,3},{5,6},{6,5},{7,0},{8,15},{9,10},{10,... | collective-permute-start | bytes 196616 | tf_op jit(solution)/shard_map/ppermute | solution.py:321
  40.0 0.6 shard_map.180
  40.6 0.8 %collective-permute-start.14 = (bf16[64,512]{1,0:T(8,128)(2,1)S(1)}, bf16[64,512]{1,0:T(8,128)(2,1)S(1)}, u32[]{:S(2)}, u32[]{:S(2)}) collective-permute-start(bf16[64,512]{1,0:T(8,128)(2,1)S(1)} %get-tuple-element.73), channel_id=1, source_target_pairs={{0,6},{1,7},{2,4},{3,5},{4,2},{5,3},{6,0},{7,1},{8,14},{9,15},{10,... | collective-permute-start | bytes 196616 | tf_op jit(solution)/shard_map/ppermute | solution.py:312
  41.4 1.3 %collective-permute-start.13 = (bf16[64,512]{1,0:T(8,128)(2,1)S(1)}, bf16[64,512]{1,0:T(8,128)(2,1)S(1)}, u32[]{:S(2)}, u32[]{:S(2)}) collective-permute-start(bf16[64,512]{1,0:T(8,128)(2,1)S(1)} %get-tuple-element.73), channel_id=1, source_target_pairs={{0,4},{1,5},{2,6},{3,7},{4,0},{5,1},{6,2},{7,3},{8,12},{9,13},{10,... | collective-permute-start | bytes 196616 | tf_op jit(solution)/shard_map/ppermute | solution.py:312
  42.7 3.8 %collective-permute-done.13 = bf16[64,512]{1,0:T(8,128)(2,1)S(1)} collective-permute-done((bf16[64,512]{1,0:T(8,128)(2,1)S(1)}, bf16[64,512]{1,0:T(8,128)(2,1)S(1)}, u32[]{:S(2)}, u32[]{:S(2)}) %collective-permute-start.13) | collective-permute-done | bytes 65568 | tf_op jit(solution)/shard_map/ppermute | solution.py:312
  46.6 0.1 collective-permute-start.17
  46.7 5.7 %shard_map.181 = (bf16[2048,512]{1,0:T(8,128)(2,1)S(1)}, f32[320,512]{1,0:T(8,128)S(1)}) custom-call(bf16[2048,512]{1,0:T(8,128)(2,1)S(1)} %get-tuple-element.52.fine_ref.e_ref, s32[1,2048]{1,0:T(1,128)S(1)} %bitcast.12, s32[1,2048]{1,0:T(1,128)S(1)} %bitcast.14, f32[2,512]{1,0:T(2,128)S(1)} %copy-done.9, bf16[2,1536,512]{2,1,0:T(8,128)(2,1)S(1)} %copy-done, ...), custom_call_target="tpu_custom_call" | custom-call | flops 4429185024 | bytes 4194304 | tf_op jit(solution)/shard_map/pallas_call | solution.py:94
  52.3 1.8 %shard_map.182 = (f32[512,512]{1,0:T(8,128)S(1)}, bf16[512,256]{1,0:T(8,128)(2,1)S(1)}, bf16[16,512]{1,0:T(8,128)(2,1)S(1)}, f32[16,512]{1,0:T(8,128)S(1)}, bf16...) custom-call(bf16[512,512]{1,0:T(8,128)(2,1)S(1)} %get-tuple-element.53.e_ref, s32[1,512]{1,0:T(1,128)S(1)} %bitcast.6, ...), custom_call_target="tpu_custom_call" | custom-call | flops 973078528 | bytes 4194304 | tf_op jit(solution)/shard_map/pallas_call | solution.py:94
  54.2 2.2 %shard_map.183 = (bf16[512,512]{1,0:T(8,128)(2,1)}, bf16[320,512]{1,0:T(8,128)(2,1)}, bf16[2048,512]{1,0:T(8,128)(2,1)}) custom-call(bf16[512,512]{1,0:T(8,128)(2,1)S(1)} %get-tuple-element.53.e_ref, f32[512,512]{1,0:T(8,128)S(1)} %get-tuple-element.63.pre_ref, bf16[512,256]{1,0:T(8,128)(2,1)S(1)} %get-tuple-element.64.far_hot_ref, ...), custom_call_target="tpu_custom_call" | custom-call | flops 872415232 | bytes 4194304 | tf_op jit(solution)/shard_map/pallas_call | solution.py:94
  (61 shorter events, 0.2 us)
Async XLA Ops:
  0.6 14.3 %copy-start.2 = (bf16[2,512,512]{2,1,0:T(8,128)(2,1)S(1)}, bf16[2,512,512]{2,1,0:T(8,128)(2,1)}, u32[]{:S(2)}) copy-start(bf16[2,512,512]{2,1,0:T(8,128)(2,1)} %second_ref.3) | copy-start | bytes 3145732
  1.7 13.3 %copy-start = (bf16[2,1536,512]{2,1,0:T(8,128)(2,1)S(1)}, bf16[2,1536,512]{2,1,0:T(8,128)(2,1)}, u32[]{:S(2)}) copy-start(bf16[2,1536,512]{2,1,0:T(8,128)(2,1)} %first_ref.15) | copy-start | bytes 9437188
  1.7 13.3 %copy-start.5 = (bf16[320,512]{1,0:T(8,128)(2,1)S(1)}, bf16[320,512]{1,0:T(8,128)(2,1)}, u32[]{:S(2)}) copy-start(bf16[320,512]{1,0:T(8,128)(2,1)} %h_ref.7) | copy-start | bytes 983044
  1.7 13.3 %copy-start.8 = (f32[2,512]{1,0:T(2,128)S(1)}, f32[2,512]{1,0:T(2,128)}, u32[]{:S(2)}) copy-start(f32[2,512]{1,0:T(2,128)} %bias_ref.7) | copy-start | bytes 12292
  1.9 9.8 %collective-permute-start.2 = (bf16[16,512]{1,0:T(8,128)(2,1)S(1)}, bf16[16,512]{1,0:T(8,128)(2,1)S(1)}, u32[]{:S(2)}, u32[]{:S(2)}) collective-permute-start(bf16[16,512]{1,0:T(8,128)(2,1)S(1)} %get-tuple-element.38), channel_id=1, source_target_pairs={{0,24},{8,16},{16,8},{24,0},{1,25},{9,17},{17,9},{25,1},{2,26},{10... | collective-permute-start | bytes 49160 | tf_op jit(solution)/shard_map/ppermute | solution.py:312
  7.1 4.6 %collective-permute-start.1 = (bf16[16,512]{1,0:T(8,128)(2,1)S(1)}, bf16[16,512]{1,0:T(8,128)(2,1)S(1)}, u32[]{:S(2)}, u32[]{:S(2)}) collective-permute-start(bf16[16,512]{1,0:T(8,128)(2,1)S(1)} %get-tuple-element.38), channel_id=1, source_target_pairs={{0,16},{8,24},{16,0},{24,8},{1,17},{9,25},{17,1},{25,9},{2,18},{10... | collective-permute-start | bytes 49160 | tf_op jit(solution)/shard_map/ppermute | solution.py:312
  7.1 3.7 %collective-permute-start = (bf16[16,512]{1,0:T(8,128)(2,1)S(1)}, bf16[16,512]{1,0:T(8,128)(2,1)S(1)}, u32[]{:S(2)}, u32[]{:S(2)}) collective-permute-start(bf16[16,512]{1,0:T(8,128)(2,1)S(1)} %get-tuple-element.38), channel_id=1, source_target_pairs={{0,8},{8,0},{16,24},{24,16},{1,9},{9,1},{17,25},{25,17},{2,10},{10... | collective-permute-start | bytes 49160 | tf_op jit(solution)/shard_map/ppermute | solution.py:312
  11.7 5.9 %collective-permute-start.3 = (bf16[64,512]{1,0:T(8,128)(2,1)S(1)}, bf16[64,512]{1,0:T(8,128)(2,1)S(1)}, u32[]{:S(2)}, u32[]{:S(2)}) collective-permute-start(bf16[64,512]{1,0:T(8,128)(2,1)S(1)} %get-tuple-element.81), channel_id=1, source_target_pairs={{0,2},{1,3},{2,0},{3,1},{4,6},{5,7},{6,4},{7,5},{8,10},{9,11},{10,... | collective-permute-start | bytes 196616 | tf_op jit(solution)/shard_map/ppermute | solution.py:312
  13.3 8.3 %collective-permute-start.6 = (bf16[64,512]{1,0:T(8,128)(2,1)S(1)}, bf16[64,512]{1,0:T(8,128)(2,1)S(1)}, u32[]{:S(2)}, u32[]{:S(2)}) collective-permute-start(bf16[64,512]{1,0:T(8,128)(2,1)S(1)} %get-tuple-element.43), channel_id=1, source_target_pairs={{0,1},{1,0},{2,3},{3,2},{4,5},{5,4},{6,7},{7,6},{8,9},{9,8},{10,11... | collective-permute-start | bytes 196616 | tf_op jit(solution)/shard_map/ppermute | solution.py:312
  13.3 8.3 %copy-start.9 = (f32[2,512]{1,0:T(2,128)S(1)}, f32[2,512]{1,0:T(2,128)}, u32[]{:S(2)}) copy-start(f32[2,512]{1,0:T(2,128)} %gain_ref.7) | copy-start | bytes 12292
  13.3 8.4 %copy-start.14 = (bf16[2048,512]{1,0:T(8,128)(2,1)S(1)}, bf16[2048,512]{1,0:T(8,128)(2,1)}, u32[]{:S(2)}) copy-start(bf16[2048,512]{1,0:T(8,128)(2,1)} %e_ref.3) | copy-start | bytes 6291460
  13.3 8.4 %copy-start.15 = (s32[2048]{0:T(1024)S(1)}, s32[2048]{0:T(1024)}, u32[]{:S(2)}) copy-start(s32[2048]{0:T(1024)} %param.19) | copy-start | bytes 24580
  13.3 8.4 %copy-start.16 = (s32[2048]{0:T(1024)S(1)}, s32[2048]{0:T(1024)}, u32[]{:S(2)}) copy-start(s32[2048]{0:T(1024)} %param.20) | copy-start | bytes 24580
  13.3 8.3 %collective-permute-start.7 = (bf16[64,512]{1,0:T(8,128)(2,1)S(1)}, bf16[64,512]{1,0:T(8,128)(2,1)S(1)}, u32[]{:S(2)}, u32[]{:S(2)}) collective-permute-start(bf16[64,512]{1,0:T(8,128)(2,1)S(1)} %get-tuple-element.44), channel_id=1, source_target_pairs={{0,7},{1,2},{2,1},{3,4},{4,3},{5,6},{6,5},{7,0},{8,15},{9,10},{10,... | collective-permute-start | bytes 196616 | tf_op jit(solution)/shard_map/ppermute | solution.py:321
  15.5 6.0 %collective-permute-start.5 = (bf16[64,512]{1,0:T(8,128)(2,1)S(1)}, bf16[64,512]{1,0:T(8,128)(2,1)S(1)}, u32[]{:S(2)}, u32[]{:S(2)}) collective-permute-start(bf16[64,512]{1,0:T(8,128)(2,1)S(1)} %get-tuple-element.81), channel_id=1, source_target_pairs={{0,6},{1,7},{2,4},{3,5},{4,2},{5,3},{6,0},{7,1},{8,14},{9,15},{10,... | collective-permute-start | bytes 196616 | tf_op jit(solution)/shard_map/ppermute | solution.py:312
  17.1 4.4 %collective-permute-start.4 = (bf16[64,512]{1,0:T(8,128)(2,1)S(1)}, bf16[64,512]{1,0:T(8,128)(2,1)S(1)}, u32[]{:S(2)}, u32[]{:S(2)}) collective-permute-start(bf16[64,512]{1,0:T(8,128)(2,1)S(1)} %get-tuple-element.81), channel_id=1, source_target_pairs={{0,4},{1,5},{2,6},{3,7},{4,0},{5,1},{6,2},{7,3},{8,12},{9,13},{10,... | collective-permute-start | bytes 196616 | tf_op jit(solution)/shard_map/ppermute | solution.py:312
  21.5 7.6 %collective-permute-start.8 = (bf16[256,512]{1,0:T(8,128)(2,1)S(1)}, bf16[256,512]{1,0:T(8,128)(2,1)S(1)}, u32[]{:S(2)}, u32[]{:S(2)}) collective-permute-start(bf16[256,512]{1,0:T(8,128)(2,1)S(1)} %constant_dynamic-update-slice_fusion.4.near_ref), channel_id=1, source_target_pairs={{0,1},{1,0},{2,3},{3,2},{4,5},{5,4},{6,7},{7,6},{8,9},{9,8},{10,11... | collective-permute-start | bytes 786440 | tf_op jit(solution)/shard_map/ppermute | solution.py:312
  21.7 5.6 %copy-start.1 = (bf16[2,1024,512]{2,1,0:T(8,128)(2,1)S(1)}, bf16[2,1024,512]{2,1,0:T(8,128)(2,1)}, u32[]{:S(2)}) copy-start(bf16[2,1024,512]{2,1,0:T(8,128)(2,1)} %node_first_ref.7) | copy-start | bytes 6291460
  21.7 5.6 %copy-start.3 = (bf16[2,512,512]{2,1,0:T(8,128)(2,1)S(1)}, bf16[2,512,512]{2,1,0:T(8,128)(2,1)}, u32[]{:S(2)}) copy-start(bf16[2,512,512]{2,1,0:T(8,128)(2,1)} %node_second_ref.3) | copy-start | bytes 3145732
  21.7 5.6 %copy-start.6 = (bf16[512,512]{1,0:T(8,128)(2,1)S(1)}, bf16[512,512]{1,0:T(8,128)(2,1)}, u32[]{:S(2)}) copy-start(bf16[512,512]{1,0:T(8,128)(2,1)} %e_ref.5) | copy-start | bytes 1572868
  21.7 5.6 %copy-start.7 = (f32[2,512]{1,0:T(2,128)S(1)}, f32[2,512]{1,0:T(2,128)}, u32[]{:S(2)}) copy-start(f32[2,512]{1,0:T(2,128)} %node_gain_ref.7) | copy-start | bytes 12292
  21.7 5.6 %copy-start.10 = (f32[2,512]{1,0:T(2,128)S(1)}, f32[2,512]{1,0:T(2,128)}, u32[]{:S(2)}) copy-start(f32[2,512]{1,0:T(2,128)} %node_bias_ref.3) | copy-start | bytes 12292
  21.7 5.6 %copy-start.11 = (s32[512,1]{0,1:T(1,128)S(1)}, s32[512,1]{0,1:T(1,128)}, u32[]{:S(2)}) copy-start(s32[512,1]{0,1:T(1,128)} %param.21) | copy-start | bytes 6148
  30.7 6.4 %collective-permute-start.11 = (bf16[16,512]{1,0:T(8,128)(2,1)S(1)}, bf16[16,512]{1,0:T(8,128)(2,1)S(1)}, u32[]{:S(2)}, u32[]{:S(2)}) collective-permute-start(bf16[16,512]{1,0:T(8,128)(2,1)S(1)} %get-tuple-element.54), channel_id=1, source_target_pairs={{0,24},{8,16},{16,8},{24,0},{1,25},{9,17},{17,9},{25,1},{2,26},{10... | collective-permute-start | bytes 49160 | tf_op jit(solution)/shard_map/ppermute | solution.py:312
  32.3 4.8 %collective-permute-start.10 = (bf16[16,512]{1,0:T(8,128)(2,1)S(1)}, bf16[16,512]{1,0:T(8,128)(2,1)S(1)}, u32[]{:S(2)}, u32[]{:S(2)}) collective-permute-start(bf16[16,512]{1,0:T(8,128)(2,1)S(1)} %get-tuple-element.54), channel_id=1, source_target_pairs={{0,16},{8,24},{16,0},{24,8},{1,17},{9,25},{17,1},{25,9},{2,18},{10... | collective-permute-start | bytes 49160 | tf_op jit(solution)/shard_map/ppermute | solution.py:312
  32.9 4.2 %collective-permute-start.9 = (bf16[16,512]{1,0:T(8,128)(2,1)S(1)}, bf16[16,512]{1,0:T(8,128)(2,1)S(1)}, u32[]{:S(2)}, u32[]{:S(2)}) collective-permute-start(bf16[16,512]{1,0:T(8,128)(2,1)S(1)} %get-tuple-element.54), channel_id=1, source_target_pairs={{0,8},{8,0},{16,24},{24,16},{1,9},{9,1},{17,25},{25,17},{2,10},{10... | collective-permute-start | bytes 49160 | tf_op jit(solution)/shard_map/ppermute | solution.py:312
  37.1 5.6 %collective-permute-start.12 = (bf16[64,512]{1,0:T(8,128)(2,1)S(1)}, bf16[64,512]{1,0:T(8,128)(2,1)S(1)}, u32[]{:S(2)}, u32[]{:S(2)}) collective-permute-start(bf16[64,512]{1,0:T(8,128)(2,1)S(1)} %get-tuple-element.73), channel_id=1, source_target_pairs={{0,2},{1,3},{2,0},{3,1},{4,6},{5,7},{6,4},{7,5},{8,10},{9,11},{10,... | collective-permute-start | bytes 196616 | tf_op jit(solution)/shard_map/ppermute | solution.py:312
  38.4 8.2 %collective-permute-start.15 = (bf16[64,512]{1,0:T(8,128)(2,1)S(1)}, bf16[64,512]{1,0:T(8,128)(2,1)S(1)}, u32[]{:S(2)}, u32[]{:S(2)}) collective-permute-start(bf16[64,512]{1,0:T(8,128)(2,1)S(1)} %get-tuple-element.60), channel_id=1, source_target_pairs={{0,1},{1,0},{2,3},{3,2},{4,5},{5,4},{6,7},{7,6},{8,9},{9,8},{10,11... | collective-permute-start | bytes 196616 | tf_op jit(solution)/shard_map/ppermute | solution.py:312
  38.5 8.2 %collective-permute-start.16 = (bf16[64,512]{1,0:T(8,128)(2,1)S(1)}, bf16[64,512]{1,0:T(8,128)(2,1)S(1)}, u32[]{:S(2)}, u32[]{:S(2)}) collective-permute-start(bf16[64,512]{1,0:T(8,128)(2,1)S(1)} %get-tuple-element.61), channel_id=1, source_target_pairs={{0,7},{1,2},{2,1},{3,4},{4,3},{5,6},{6,5},{7,0},{8,15},{9,10},{10,... | collective-permute-start | bytes 196616 | tf_op jit(solution)/shard_map/ppermute | solution.py:321
  40.6 6.0 %collective-permute-start.14 = (bf16[64,512]{1,0:T(8,128)(2,1)S(1)}, bf16[64,512]{1,0:T(8,128)(2,1)S(1)}, u32[]{:S(2)}, u32[]{:S(2)}) collective-permute-start(bf16[64,512]{1,0:T(8,128)(2,1)S(1)} %get-tuple-element.73), channel_id=1, source_target_pairs={{0,6},{1,7},{2,4},{3,5},{4,2},{5,3},{6,0},{7,1},{8,14},{9,15},{10,... | collective-permute-start | bytes 196616 | tf_op jit(solution)/shard_map/ppermute | solution.py:312
  41.4 5.1 %collective-permute-start.13 = (bf16[64,512]{1,0:T(8,128)(2,1)S(1)}, bf16[64,512]{1,0:T(8,128)(2,1)S(1)}, u32[]{:S(2)}, u32[]{:S(2)}) collective-permute-start(bf16[64,512]{1,0:T(8,128)(2,1)S(1)} %get-tuple-element.73), channel_id=1, source_target_pairs={{0,4},{1,5},{2,6},{3,7},{4,0},{5,1},{6,2},{7,3},{8,12},{9,13},{10,... | collective-permute-start | bytes 196616 | tf_op jit(solution)/shard_map/ppermute | solution.py:312
  46.6 7.6 %collective-permute-start.17 = (bf16[256,512]{1,0:T(8,128)(2,1)S(1)}, bf16[256,512]{1,0:T(8,128)(2,1)S(1)}, u32[]{:S(2)}, u32[]{:S(2)}) collective-permute-start(bf16[256,512]{1,0:T(8,128)(2,1)S(1)} %constant_dynamic-update-slice_fusion.15.near_ref), channel_id=1, source_target_pairs={{0,1},{1,0},{2,3},{3,2},{4,5},{5,4},{6,7},{7,6},{8,9},{9,8},{10,11... | collective-permute-start | bytes 786440 | tf_op jit(solution)/shard_map/ppermute | solution.py:312
  (3 other events, 12.2 us)

commit v3 on v2

--- a/solution.py
+++ b/solution.py
@@ -315,12 +315,16 @@
 def exchange(head, cross, sibling):
     groups = lax.axis_size("group")
     patches = lax.axis_size("patch")
-    parts = [head] + [swap(head, "group", k) for k in range(1, groups)]
+    parts = [head]
+    for k in range(1, groups):
+        parts.append(swap(head, "group", k))
     beside = swap(sibling, "patch", 1)
     pairs = [(p, (p + (1 if p % 2 else -1)) % patches) for p in range(patches)]
     across = lax.ppermute(cross, "patch", pairs)
     line = jnp.concatenate(parts, axis=0)
-    parts = [line] + [swap(line, "patch", k) for k in range(2, patches, 2)]
+    parts = [line]
+    for k in range(2, patches, 2):
+        parts.append(swap(line, "patch", k))
     near = jnp.concatenate(parts, axis=0)
     far = swap(near, "patch", 1)
     return beside, across, near, far

time: 56.7 us -> 56.7 us (level)
  no operation moved by 1% of the time
where the time goes in v3:
time: 56.7 us; the launch traced here: 56.5 us
  starting transfers between devices  20.7 us (37%)
  Pallas kernels  19.8 us (35%)
  waiting for transfers between devices  13.6 us (24%)
  local copies, waits for them, and re-layouts  1.2 us (2%)
  between operations  1.18 us (2%)
    pallas_call x9, Pallas kernels, call(): pl.pallas_call(kernel, in_specs=in_specs or [VMEM] * len(args), out_specs...  19.8 us
    ppermute x16, starting transfers between devices, swap(): return lax.ppermute(value, axis, [(i, i ^ bit) for i in range(count)])  17.4 us
    ppermute x16, waiting for transfers between devices, swap(): return lax.ppermute(value, axis, [(i, i ^ bit) for i in range(count)])  13.6 us
    ppermute x2, starting transfers between devices, exchange(): across = lax.ppermute(cross, 'patch', pairs)  3.22 us
    unnamed x44, local copies, waits for them, and re-layouts  1.18 us
  transfers between devices with their start and end apart: 18, of which 5 were waited for; matrix products, arithmetic and copies ran while one was open for 0% of the time, Pallas kernels for 28%

profile of v3, /device:TPU:0, one launch (start us, length us, event | category | flops | bytes accessed | tf_op | source)
XLA Modules:
  0.0 56.5 jit_solution(3245498323146489516)
XLA Ops:
  0.7 1.1 %copy-done.4 = bf16[320,512]{1,0:T(8,128)(2,1)S(1)} copy-done((bf16[320,512]{1,0:T(8,128)(2,1)S(1)}, bf16[320,512]{1,0:T(8,128)(2,1)}, u32[]{:S(2)}) %copy-start.4) | copy-done | bytes 327704
  1.7 0.2 shard_map.175
  1.9 5.1 %collective-permute-start.2 = (bf16[16,512]{1,0:T(8,128)(2,1)S(1)}, bf16[16,512]{1,0:T(8,128)(2,1)S(1)}, u32[]{:S(2)}, u32[]{:S(2)}) collective-permute-start(bf16[16,512]{1,0:T(8,128)(2,1)S(1)} %get-tuple-element.38), channel_id=1, source_target_pairs={{0,24},{8,16},{16,8},{24,0},{1,25},{9,17},{17,9},{25,1},{2,26},{10... | collective-permute-start | bytes 49160 | tf_op jit(solution)/shard_map/ppermute | solution.py:312
  7.1 0.6 %collective-permute-start = (bf16[16,512]{1,0:T(8,128)(2,1)S(1)}, bf16[16,512]{1,0:T(8,128)(2,1)S(1)}, u32[]{:S(2)}, u32[]{:S(2)}) collective-permute-start(bf16[16,512]{1,0:T(8,128)(2,1)S(1)} %get-tuple-element.38), channel_id=1, source_target_pairs={{0,8},{8,0},{16,24},{24,16},{1,9},{9,1},{17,25},{25,17},{2,10},{10... | collective-permute-start | bytes 49160 | tf_op jit(solution)/shard_map/ppermute | solution.py:312
  7.7 3.1 %collective-permute-done = bf16[16,512]{1,0:T(8,128)(2,1)S(1)} collective-permute-done((bf16[16,512]{1,0:T(8,128)(2,1)S(1)}, bf16[16,512]{1,0:T(8,128)(2,1)S(1)}, u32[]{:S(2)}, u32[]{:S(2)}) %collective-permute-start) | collective-permute-done | bytes 16416 | tf_op jit(solution)/shard_map/ppermute | solution.py:312
  10.8 0.9 %collective-permute-done.1 = bf16[16,512]{1,0:T(8,128)(2,1)S(1)} collective-permute-done((bf16[16,512]{1,0:T(8,128)(2,1)S(1)}, bf16[16,512]{1,0:T(8,128)(2,1)S(1)}, u32[]{:S(2)}, u32[]{:S(2)}) %collective-permute-start.1) | collective-permute-done | bytes 16416 | tf_op jit(solution)/shard_map/ppermute | solution.py:312
  11.7 1.6 %collective-permute-start.3 = (bf16[64,512]{1,0:T(8,128)(2,1)S(1)}, bf16[64,512]{1,0:T(8,128)(2,1)S(1)}, u32[]{:S(2)}, u32[]{:S(2)}) collective-permute-start(bf16[64,512]{1,0:T(8,128)(2,1)S(1)} %get-tuple-element.81), channel_id=1, source_target_pairs={{0,2},{1,3},{2,0},{3,1},{4,6},{5,7},{6,4},{7,5},{8,10},{9,11},{10,... | collective-permute-start | bytes 196616 | tf_op jit(solution)/shard_map/ppermute | solution.py:312
  13.3 1.7 %collective-permute-start.7 = (bf16[64,512]{1,0:T(8,128)(2,1)S(1)}, bf16[64,512]{1,0:T(8,128)(2,1)S(1)}, u32[]{:S(2)}, u32[]{:S(2)}) collective-permute-start(bf16[64,512]{1,0:T(8,128)(2,1)S(1)} %get-tuple-element.44), channel_id=1, source_target_pairs={{0,7},{1,2},{2,1},{3,4},{4,3},{5,6},{6,5},{7,0},{8,15},{9,10},{10,... | collective-permute-start | bytes 196616 | tf_op jit(solution)/shard_map/ppermute | solution.py:323
  15.0 0.6 shard_map.176
  15.5 1.6 %collective-permute-start.5 = (bf16[64,512]{1,0:T(8,128)(2,1)S(1)}, bf16[64,512]{1,0:T(8,128)(2,1)S(1)}, u32[]{:S(2)}, u32[]{:S(2)}) collective-permute-start(bf16[64,512]{1,0:T(8,128)(2,1)S(1)} %get-tuple-element.81), channel_id=1, source_target_pairs={{0,6},{1,7},{2,4},{3,5},{4,2},{5,3},{6,0},{7,1},{8,14},{9,15},{10,... | collective-permute-start | bytes 196616 | tf_op jit(solution)/shard_map/ppermute | solution.py:312
  17.1 0.5 collective-permute-start.4
  17.6 3.9 %collective-permute-done.4 = bf16[64,512]{1,0:T(8,128)(2,1)S(1)} collective-permute-done((bf16[64,512]{1,0:T(8,128)(2,1)S(1)}, bf16[64,512]{1,0:T(8,128)(2,1)S(1)}, u32[]{:S(2)}, u32[]{:S(2)}) %collective-permute-start.4) | collective-permute-done | bytes 65568 | tf_op jit(solution)/shard_map/ppermute | solution.py:312
  21.5 0.1 collective-permute-start.8
  21.7 0.0 copy-start.1
  21.7 0.0 copy-start.7
  21.8 5.5 %shard_map.177 = (bf16[2048,512]{1,0:T(8,128)(2,1)S(1)}, f32[320,512]{1,0:T(8,128)S(1)}) custom-call(bf16[2048,512]{1,0:T(8,128)(2,1)S(1)} %copy-done.14, s32[1,2048]{1,0:T(1,128)S(1)} %bitcast.11, s32[1,2048]{1,0:T(1,128)S(1)} %bitcast.13, f32[2,512]{1,0:T(2,128)S(1)} %copy-done.9, bf16[2,1536,512]{2,1,0:T(8,128)(2,1)S(1)} %copy-done, ...), custom_call_target="tpu_custom_call" | custom-call | flops 4429185024 | bytes 4194304 | tf_op jit(solution)/shard_map/pallas_call | solution.py:94
  27.3 1.8 %shard_map.178 = (f32[512,512]{1,0:T(8,128)S(1)}, bf16[512,256]{1,0:T(8,128)(2,1)S(1)}, bf16[16,512]{1,0:T(8,128)(2,1)S(1)}, f32[16,512]{1,0:T(8,128)S(1)}, bf16...) custom-call(bf16[512,512]{1,0:T(8,128)(2,1)S(1)} %copy-done.6, s32[1,512]{1,0:T(1,128)S(1)} %bitcast.5, ...), custom_call_target="tpu_custom_call" | custom-call | flops 973078528 | bytes 4194304 | tf_op jit(solution)/shard_map/pallas_call | solution.py:94
  29.2 1.6 %shard_map.179 = (bf16[512,512]{1,0:T(8,128)(2,1)S(1)}, bf16[320,512]{1,0:T(8,128)(2,1)S(1)}, bf16[16,512]{1,0:T(8,128)(2,1)S(1)}, bf16[64,512]{1,0:T(8,128)(2,1)S(1)}, bf16[64,512]{1,0:T(8,128)(2,1)S(1)}) custom-call(bf16[512,512]{1,0:T(8,128)(2,1)S(1)} %copy-done.6, f32[512,512]{1,0:T(8,128)S(1)} %get-tuple-element.46.pre_ref, ...), custom_call_target="tpu_custom_call" | custom-call | flops 872415232 | bytes 4194304 | tf_op jit(solution)/shard_map/pallas_call | solution.py:94
  30.7 1.6 %collective-permute-start.11 = (bf16[16,512]{1,0:T(8,128)(2,1)S(1)}, bf16[16,512]{1,0:T(8,128)(2,1)S(1)}, u32[]{:S(2)}, u32[]{:S(2)}) collective-permute-start(bf16[16,512]{1,0:T(8,128)(2,1)S(1)} %get-tuple-element.54), channel_id=1, source_target_pairs={{0,24},{8,16},{16,8},{24,0},{1,25},{9,17},{17,9},{25,1},{2,26},{10... | collective-permute-start | bytes 49160 | tf_op jit(solution)/shard_map/ppermute | solution.py:312
  32.3 0.6 %collective-permute-start.10 = (bf16[16,512]{1,0:T(8,128)(2,1)S(1)}, bf16[16,512]{1,0:T(8,128)(2,1)S(1)}, u32[]{:S(2)}, u32[]{:S(2)}) collective-permute-start(bf16[16,512]{1,0:T(8,128)(2,1)S(1)} %get-tuple-element.54), channel_id=1, source_target_pairs={{0,16},{8,24},{16,0},{24,8},{1,17},{9,25},{17,1},{25,9},{2,18},{10... | collective-permute-start | bytes 49160 | tf_op jit(solution)/shard_map/ppermute | solution.py:312
  32.9 2.3 %collective-permute-start.9 = (bf16[16,512]{1,0:T(8,128)(2,1)S(1)}, bf16[16,512]{1,0:T(8,128)(2,1)S(1)}, u32[]{:S(2)}, u32[]{:S(2)}) collective-permute-start(bf16[16,512]{1,0:T(8,128)(2,1)S(1)} %get-tuple-element.54), channel_id=1, source_target_pairs={{0,8},{8,0},{16,24},{24,16},{1,9},{9,1},{17,25},{25,17},{2,10},{10... | collective-permute-start | bytes 49160 | tf_op jit(solution)/shard_map/ppermute | solution.py:312
  35.2 1.9 %collective-permute-done.9 = bf16[16,512]{1,0:T(8,128)(2,1)S(1)} collective-permute-done((bf16[16,512]{1,0:T(8,128)(2,1)S(1)}, bf16[16,512]{1,0:T(8,128)(2,1)S(1)}, u32[]{:S(2)}, u32[]{:S(2)}) %collective-permute-start.9) | collective-permute-done | bytes 16416 | tf_op jit(solution)/shard_map/ppermute | solution.py:312
  37.1 1.3 %collective-permute-start.12 = (bf16[64,512]{1,0:T(8,128)(2,1)S(1)}, bf16[64,512]{1,0:T(8,128)(2,1)S(1)}, u32[]{:S(2)}, u32[]{:S(2)}) collective-permute-start(bf16[64,512]{1,0:T(8,128)(2,1)S(1)} %get-tuple-element.73), channel_id=1, source_target_pairs={{0,2},{1,3},{2,0},{3,1},{4,6},{5,7},{6,4},{7,5},{8,10},{9,11},{10,... | collective-permute-start | bytes 196616 | tf_op jit(solution)/shard_map/ppermute | solution.py:312
  38.5 1.6 %collective-permute-start.16 = (bf16[64,512]{1,0:T(8,128)(2,1)S(1)}, bf16[64,512]{1,0:T(8,128)(2,1)S(1)}, u32[]{:S(2)}, u32[]{:S(2)}) collective-permute-start(bf16[64,512]{1,0:T(8,128)(2,1)S(1)} %get-tuple-element.61), channel_id=1, source_target_pairs={{0,7},{1,2},{2,1},{3,4},{4,3},{5,6},{6,5},{7,0},{8,15},{9,10},{10,... | collective-permute-start | bytes 196616 | tf_op jit(solution)/shard_map/ppermute | solution.py:323
  40.0 0.6 shard_map.180
  40.6 0.8 %collective-permute-start.14 = (bf16[64,512]{1,0:T(8,128)(2,1)S(1)}, bf16[64,512]{1,0:T(8,128)(2,1)S(1)}, u32[]{:S(2)}, u32[]{:S(2)}) collective-permute-start(bf16[64,512]{1,0:T(8,128)(2,1)S(1)} %get-tuple-element.73), channel_id=1, source_target_pairs={{0,6},{1,7},{2,4},{3,5},{4,2},{5,3},{6,0},{7,1},{8,14},{9,15},{10,... | collective-permute-start | bytes 196616 | tf_op jit(solution)/shard_map/ppermute | solution.py:312
  41.4 1.3 %collective-permute-start.13 = (bf16[64,512]{1,0:T(8,128)(2,1)S(1)}, bf16[64,512]{1,0:T(8,128)(2,1)S(1)}, u32[]{:S(2)}, u32[]{:S(2)}) collective-permute-start(bf16[64,512]{1,0:T(8,128)(2,1)S(1)} %get-tuple-element.73), channel_id=1, source_target_pairs={{0,4},{1,5},{2,6},{3,7},{4,0},{5,1},{6,2},{7,3},{8,12},{9,13},{10,... | collective-permute-start | bytes 196616 | tf_op jit(solution)/shard_map/ppermute | solution.py:312
  42.7 3.8 %collective-permute-done.13 = bf16[64,512]{1,0:T(8,128)(2,1)S(1)} collective-permute-done((bf16[64,512]{1,0:T(8,128)(2,1)S(1)}, bf16[64,512]{1,0:T(8,128)(2,1)S(1)}, u32[]{:S(2)}, u32[]{:S(2)}) %collective-permute-start.13) | collective-permute-done | bytes 65568 | tf_op jit(solution)/shard_map/ppermute | solution.py:312
  46.6 0.1 collective-permute-start.17
  46.7 5.7 %shard_map.181 = (bf16[2048,512]{1,0:T(8,128)(2,1)S(1)}, f32[320,512]{1,0:T(8,128)S(1)}) custom-call(bf16[2048,512]{1,0:T(8,128)(2,1)S(1)} %get-tuple-element.52.fine_ref.e_ref, s32[1,2048]{1,0:T(1,128)S(1)} %bitcast.12, s32[1,2048]{1,0:T(1,128)S(1)} %bitcast.14, f32[2,512]{1,0:T(2,128)S(1)} %copy-done.9, bf16[2,1536,512]{2,1,0:T(8,128)(2,1)S(1)} %copy-done, ...), custom_call_target="tpu_custom_call" | custom-call | flops 4429185024 | bytes 4194304 | tf_op jit(solution)/shard_map/pallas_call | solution.py:94
  52.3 1.8 %shard_map.182 = (f32[512,512]{1,0:T(8,128)S(1)}, bf16[512,256]{1,0:T(8,128)(2,1)S(1)}, bf16[16,512]{1,0:T(8,128)(2,1)S(1)}, f32[16,512]{1,0:T(8,128)S(1)}, bf16...) custom-call(bf16[512,512]{1,0:T(8,128)(2,1)S(1)} %get-tuple-element.53.e_ref, s32[1,512]{1,0:T(1,128)S(1)} %bitcast.6, ...), custom_call_target="tpu_custom_call" | custom-call | flops 973078528 | bytes 4194304 | tf_op jit(solution)/shard_map/pallas_call | solution.py:94
  54.2 2.2 %shard_map.183 = (bf16[512,512]{1,0:T(8,128)(2,1)}, bf16[320,512]{1,0:T(8,128)(2,1)}, bf16[2048,512]{1,0:T(8,128)(2,1)}) custom-call(bf16[512,512]{1,0:T(8,128)(2,1)S(1)} %get-tuple-element.53.e_ref, f32[512,512]{1,0:T(8,128)S(1)} %get-tuple-element.63.pre_ref, bf16[512,256]{1,0:T(8,128)(2,1)S(1)} %get-tuple-element.64.far_hot_ref, ...), custom_call_target="tpu_custom_call" | custom-call | flops 872415232 | bytes 4194304 | tf_op jit(solution)/shard_map/pallas_call | solution.py:94
  (61 shorter events, 0.2 us)
Async XLA Ops:
  0.6 14.3 %copy-start.2 = (bf16[2,512,512]{2,1,0:T(8,128)(2,1)S(1)}, bf16[2,512,512]{2,1,0:T(8,128)(2,1)}, u32[]{:S(2)}) copy-start(bf16[2,512,512]{2,1,0:T(8,128)(2,1)} %second_ref.3) | copy-start | bytes 3145732
  1.7 13.3 %copy-start = (bf16[2,1536,512]{2,1,0:T(8,128)(2,1)S(1)}, bf16[2,1536,512]{2,1,0:T(8,128)(2,1)}, u32[]{:S(2)}) copy-start(bf16[2,1536,512]{2,1,0:T(8,128)(2,1)} %first_ref.15) | copy-start | bytes 9437188
  1.7 13.3 %copy-start.5 = (bf16[320,512]{1,0:T(8,128)(2,1)S(1)}, bf16[320,512]{1,0:T(8,128)(2,1)}, u32[]{:S(2)}) copy-start(bf16[320,512]{1,0:T(8,128)(2,1)} %h_ref.7) | copy-start | bytes 983044
  1.7 13.3 %copy-start.8 = (f32[2,512]{1,0:T(2,128)S(1)}, f32[2,512]{1,0:T(2,128)}, u32[]{:S(2)}) copy-start(f32[2,512]{1,0:T(2,128)} %bias_ref.7) | copy-start | bytes 12292
  1.9 9.8 %collective-permute-start.2 = (bf16[16,512]{1,0:T(8,128)(2,1)S(1)}, bf16[16,512]{1,0:T(8,128)(2,1)S(1)}, u32[]{:S(2)}, u32[]{:S(2)}) collective-permute-start(bf16[16,512]{1,0:T(8,128)(2,1)S(1)} %get-tuple-element.38), channel_id=1, source_target_pairs={{0,24},{8,16},{16,8},{24,0},{1,25},{9,17},{17,9},{25,1},{2,26},{10... | collective-permute-start | bytes 49160 | tf_op jit(solution)/shard_map/ppermute | solution.py:312
  7.1 4.6 %collective-permute-start.1 = (bf16[16,512]{1,0:T(8,128)(2,1)S(1)}, bf16[16,512]{1,0:T(8,128)(2,1)S(1)}, u32[]{:S(2)}, u32[]{:S(2)}) collective-permute-start(bf16[16,512]{1,0:T(8,128)(2,1)S(1)} %get-tuple-element.38), channel_id=1, source_target_pairs={{0,16},{8,24},{16,0},{24,8},{1,17},{9,25},{17,1},{25,9},{2,18},{10... | collective-permute-start | bytes 49160 | tf_op jit(solution)/shard_map/ppermute | solution.py:312
  7.1 3.7 %collective-permute-start = (bf16[16,512]{1,0:T(8,128)(2,1)S(1)}, bf16[16,512]{1,0:T(8,128)(2,1)S(1)}, u32[]{:S(2)}, u32[]{:S(2)}) collective-permute-start(bf16[16,512]{1,0:T(8,128)(2,1)S(1)} %get-tuple-element.38), channel_id=1, source_target_pairs={{0,8},{8,0},{16,24},{24,16},{1,9},{9,1},{17,25},{25,17},{2,10},{10... | collective-permute-start | bytes 49160 | tf_op jit(solution)/shard_map/ppermute | solution.py:312
  11.7 5.9 %collective-permute-start.3 = (bf16[64,512]{1,0:T(8,128)(2,1)S(1)}, bf16[64,512]{1,0:T(8,128)(2,1)S(1)}, u32[]{:S(2)}, u32[]{:S(2)}) collective-permute-start(bf16[64,512]{1,0:T(8,128)(2,1)S(1)} %get-tuple-element.81), channel_id=1, source_target_pairs={{0,2},{1,3},{2,0},{3,1},{4,6},{5,7},{6,4},{7,5},{8,10},{9,11},{10,... | collective-permute-start | bytes 196616 | tf_op jit(solution)/shard_map/ppermute | solution.py:312
  13.3 8.3 %collective-permute-start.6 = (bf16[64,512]{1,0:T(8,128)(2,1)S(1)}, bf16[64,512]{1,0:T(8,128)(2,1)S(1)}, u32[]{:S(2)}, u32[]{:S(2)}) collective-permute-start(bf16[64,512]{1,0:T(8,128)(2,1)S(1)} %get-tuple-element.43), channel_id=1, source_target_pairs={{0,1},{1,0},{2,3},{3,2},{4,5},{5,4},{6,7},{7,6},{8,9},{9,8},{10,11... | collective-permute-start | bytes 196616 | tf_op jit(solution)/shard_map/ppermute | solution.py:312
  13.3 8.3 %copy-start.9 = (f32[2,512]{1,0:T(2,128)S(1)}, f32[2,512]{1,0:T(2,128)}, u32[]{:S(2)}) copy-start(f32[2,512]{1,0:T(2,128)} %gain_ref.7) | copy-start | bytes 12292
  13.3 8.4 %copy-start.14 = (bf16[2048,512]{1,0:T(8,128)(2,1)S(1)}, bf16[2048,512]{1,0:T(8,128)(2,1)}, u32[]{:S(2)}) copy-start(bf16[2048,512]{1,0:T(8,128)(2,1)} %e_ref.3) | copy-start | bytes 6291460
  13.3 8.4 %copy-start.15 = (s32[2048]{0:T(1024)S(1)}, s32[2048]{0:T(1024)}, u32[]{:S(2)}) copy-start(s32[2048]{0:T(1024)} %param.19) | copy-start | bytes 24580
  13.3 8.4 %copy-start.16 = (s32[2048]{0:T(1024)S(1)}, s32[2048]{0:T(1024)}, u32[]{:S(2)}) copy-start(s32[2048]{0:T(1024)} %param.20) | copy-start | bytes 24580
  13.3 8.3 %collective-permute-start.7 = (bf16[64,512]{1,0:T(8,128)(2,1)S(1)}, bf16[64,512]{1,0:T(8,128)(2,1)S(1)}, u32[]{:S(2)}, u32[]{:S(2)}) collective-permute-start(bf16[64,512]{1,0:T(8,128)(2,1)S(1)} %get-tuple-element.44), channel_id=1, source_target_pairs={{0,7},{1,2},{2,1},{3,4},{4,3},{5,6},{6,5},{7,0},{8,15},{9,10},{10,... | collective-permute-start | bytes 196616 | tf_op jit(solution)/shard_map/ppermute | solution.py:323
  15.5 6.0 %collective-permute-start.5 = (bf16[64,512]{1,0:T(8,128)(2,1)S(1)}, bf16[64,512]{1,0:T(8,128)(2,1)S(1)}, u32[]{:S(2)}, u32[]{:S(2)}) collective-permute-start(bf16[64,512]{1,0:T(8,128)(2,1)S(1)} %get-tuple-element.81), channel_id=1, source_target_pairs={{0,6},{1,7},{2,4},{3,5},{4,2},{5,3},{6,0},{7,1},{8,14},{9,15},{10,... | collective-permute-start | bytes 196616 | tf_op jit(solution)/shard_map/ppermute | solution.py:312
  17.1 4.4 %collective-permute-start.4 = (bf16[64,512]{1,0:T(8,128)(2,1)S(1)}, bf16[64,512]{1,0:T(8,128)(2,1)S(1)}, u32[]{:S(2)}, u32[]{:S(2)}) collective-permute-start(bf16[64,512]{1,0:T(8,128)(2,1)S(1)} %get-tuple-element.81), channel_id=1, source_target_pairs={{0,4},{1,5},{2,6},{3,7},{4,0},{5,1},{6,2},{7,3},{8,12},{9,13},{10,... | collective-permute-start | bytes 196616 | tf_op jit(solution)/shard_map/ppermute | solution.py:312
  21.5 7.6 %collective-permute-start.8 = (bf16[256,512]{1,0:T(8,128)(2,1)S(1)}, bf16[256,512]{1,0:T(8,128)(2,1)S(1)}, u32[]{:S(2)}, u32[]{:S(2)}) collective-permute-start(bf16[256,512]{1,0:T(8,128)(2,1)S(1)} %constant_dynamic-update-slice_fusion.4.near_ref), channel_id=1, source_target_pairs={{0,1},{1,0},{2,3},{3,2},{4,5},{5,4},{6,7},{7,6},{8,9},{9,8},{10,11... | collective-permute-start | bytes 786440 | tf_op jit(solution)/shard_map/ppermute | solution.py:312
  21.7 5.6 %copy-start.1 = (bf16[2,1024,512]{2,1,0:T(8,128)(2,1)S(1)}, bf16[2,1024,512]{2,1,0:T(8,128)(2,1)}, u32[]{:S(2)}) copy-start(bf16[2,1024,512]{2,1,0:T(8,128)(2,1)} %node_first_ref.7) | copy-start | bytes 6291460
  21.7 5.6 %copy-start.3 = (bf16[2,512,512]{2,1,0:T(8,128)(2,1)S(1)}, bf16[2,512,512]{2,1,0:T(8,128)(2,1)}, u32[]{:S(2)}) copy-start(bf16[2,512,512]{2,1,0:T(8,128)(2,1)} %node_second_ref.3) | copy-start | bytes 3145732
  21.7 5.6 %copy-start.6 = (bf16[512,512]{1,0:T(8,128)(2,1)S(1)}, bf16[512,512]{1,0:T(8,128)(2,1)}, u32[]{:S(2)}) copy-start(bf16[512,512]{1,0:T(8,128)(2,1)} %e_ref.5) | copy-start | bytes 1572868
  21.7 5.6 %copy-start.7 = (f32[2,512]{1,0:T(2,128)S(1)}, f32[2,512]{1,0:T(2,128)}, u32[]{:S(2)}) copy-start(f32[2,512]{1,0:T(2,128)} %node_gain_ref.7) | copy-start | bytes 12292
  21.7 5.6 %copy-start.10 = (f32[2,512]{1,0:T(2,128)S(1)}, f32[2,512]{1,0:T(2,128)}, u32[]{:S(2)}) copy-start(f32[2,512]{1,0:T(2,128)} %node_bias_ref.3) | copy-start | bytes 12292
  21.7 5.6 %copy-start.11 = (s32[512,1]{0,1:T(1,128)S(1)}, s32[512,1]{0,1:T(1,128)}, u32[]{:S(2)}) copy-start(s32[512,1]{0,1:T(1,128)} %param.21) | copy-start | bytes 6148
  30.7 6.4 %collective-permute-start.11 = (bf16[16,512]{1,0:T(8,128)(2,1)S(1)}, bf16[16,512]{1,0:T(8,128)(2,1)S(1)}, u32[]{:S(2)}, u32[]{:S(2)}) collective-permute-start(bf16[16,512]{1,0:T(8,128)(2,1)S(1)} %get-tuple-element.54), channel_id=1, source_target_pairs={{0,24},{8,16},{16,8},{24,0},{1,25},{9,17},{17,9},{25,1},{2,26},{10... | collective-permute-start | bytes 49160 | tf_op jit(solution)/shard_map/ppermute | solution.py:312
  32.3 4.8 %collective-permute-start.10 = (bf16[16,512]{1,0:T(8,128)(2,1)S(1)}, bf16[16,512]{1,0:T(8,128)(2,1)S(1)}, u32[]{:S(2)}, u32[]{:S(2)}) collective-permute-start(bf16[16,512]{1,0:T(8,128)(2,1)S(1)} %get-tuple-element.54), channel_id=1, source_target_pairs={{0,16},{8,24},{16,0},{24,8},{1,17},{9,25},{17,1},{25,9},{2,18},{10... | collective-permute-start | bytes 49160 | tf_op jit(solution)/shard_map/ppermute | solution.py:312
  32.9 4.2 %collective-permute-start.9 = (bf16[16,512]{1,0:T(8,128)(2,1)S(1)}, bf16[16,512]{1,0:T(8,128)(2,1)S(1)}, u32[]{:S(2)}, u32[]{:S(2)}) collective-permute-start(bf16[16,512]{1,0:T(8,128)(2,1)S(1)} %get-tuple-element.54), channel_id=1, source_target_pairs={{0,8},{8,0},{16,24},{24,16},{1,9},{9,1},{17,25},{25,17},{2,10},{10... | collective-permute-start | bytes 49160 | tf_op jit(solution)/shard_map/ppermute | solution.py:312
  37.1 5.6 %collective-permute-start.12 = (bf16[64,512]{1,0:T(8,128)(2,1)S(1)}, bf16[64,512]{1,0:T(8,128)(2,1)S(1)}, u32[]{:S(2)}, u32[]{:S(2)}) collective-permute-start(bf16[64,512]{1,0:T(8,128)(2,1)S(1)} %get-tuple-element.73), channel_id=1, source_target_pairs={{0,2},{1,3},{2,0},{3,1},{4,6},{5,7},{6,4},{7,5},{8,10},{9,11},{10,... | collective-permute-start | bytes 196616 | tf_op jit(solution)/shard_map/ppermute | solution.py:312
  38.4 8.2 %collective-permute-start.15 = (bf16[64,512]{1,0:T(8,128)(2,1)S(1)}, bf16[64,512]{1,0:T(8,128)(2,1)S(1)}, u32[]{:S(2)}, u32[]{:S(2)}) collective-permute-start(bf16[64,512]{1,0:T(8,128)(2,1)S(1)} %get-tuple-element.60), channel_id=1, source_target_pairs={{0,1},{1,0},{2,3},{3,2},{4,5},{5,4},{6,7},{7,6},{8,9},{9,8},{10,11... | collective-permute-start | bytes 196616 | tf_op jit(solution)/shard_map/ppermute | solution.py:312
  38.5 8.2 %collective-permute-start.16 = (bf16[64,512]{1,0:T(8,128)(2,1)S(1)}, bf16[64,512]{1,0:T(8,128)(2,1)S(1)}, u32[]{:S(2)}, u32[]{:S(2)}) collective-permute-start(bf16[64,512]{1,0:T(8,128)(2,1)S(1)} %get-tuple-element.61), channel_id=1, source_target_pairs={{0,7},{1,2},{2,1},{3,4},{4,3},{5,6},{6,5},{7,0},{8,15},{9,10},{10,... | collective-permute-start | bytes 196616 | tf_op jit(solution)/shard_map/ppermute | solution.py:323
  40.6 6.0 %collective-permute-start.14 = (bf16[64,512]{1,0:T(8,128)(2,1)S(1)}, bf16[64,512]{1,0:T(8,128)(2,1)S(1)}, u32[]{:S(2)}, u32[]{:S(2)}) collective-permute-start(bf16[64,512]{1,0:T(8,128)(2,1)S(1)} %get-tuple-element.73), channel_id=1, source_target_pairs={{0,6},{1,7},{2,4},{3,5},{4,2},{5,3},{6,0},{7,1},{8,14},{9,15},{10,... | collective-permute-start | bytes 196616 | tf_op jit(solution)/shard_map/ppermute | solution.py:312
  41.4 5.1 %collective-permute-start.13 = (bf16[64,512]{1,0:T(8,128)(2,1)S(1)}, bf16[64,512]{1,0:T(8,128)(2,1)S(1)}, u32[]{:S(2)}, u32[]{:S(2)}) collective-permute-start(bf16[64,512]{1,0:T(8,128)(2,1)S(1)} %get-tuple-element.73), channel_id=1, source_target_pairs={{0,4},{1,5},{2,6},{3,7},{4,0},{5,1},{6,2},{7,3},{8,12},{9,13},{10,... | collective-permute-start | bytes 196616 | tf_op jit(solution)/shard_map/ppermute | solution.py:312
  46.6 7.6 %collective-permute-start.17 = (bf16[256,512]{1,0:T(8,128)(2,1)S(1)}, bf16[256,512]{1,0:T(8,128)(2,1)S(1)}, u32[]{:S(2)}, u32[]{:S(2)}) collective-permute-start(bf16[256,512]{1,0:T(8,128)(2,1)S(1)} %constant_dynamic-update-slice_fusion.15.near_ref), channel_id=1, source_target_pairs={{0,1},{1,0},{2,3},{3,2},{4,5},{5,4},{6,7},{7,6},{8,9},{9,8},{10,11... | collective-permute-start | bytes 786440 | tf_op jit(solution)/shard_map/ppermute | solution.py:312
  (3 other events, 12.2 us)

commit v4 on v3

--- a/solution.py
+++ b/solution.py
@@ -170,7 +170,9 @@
     rcv = rcv_ref[...]
     offset = (owner & (patches - 1)) ^ lax.axis_index("patch")
     group_offset = (owner >> (patches.bit_length() - 1)) ^ lax.axis_index("group")
-    slot = ((offset & 1) * (patches // 2) + (offset >> 1)) * groups + group_offset
+    offset = offset ^ jnp.where(group_offset != 0, 1, 0)
+    far = (offset & 1) ^ jnp.where(offset >= 2, 1, 0)
+    slot = (far * (patches // 2) + (offset >> 1)) * groups + group_offset
     place = column_of(slot * COARSE + row_ref[...])
     ends = onehot_lanes([(0, near, place), (near, near + 128, column_of(rcv + near))], 0, near + 128)
     pre_ref[...] = dot(e_ref[...], w_edge[...]) + dot(ends, table[...])
@@ -317,13 +319,13 @@
     patches = lax.axis_size("patch")
     parts = [head]
     for k in range(1, groups):
-        parts.append(swap(head, "group", k))
+        parts.append(swap(head, GP, k * patches + 1))
     beside = swap(sibling, "patch", 1)
     pairs = [(p, (p + (1 if p % 2 else -1)) % patches) for p in range(patches)]
     across = lax.ppermute(cross, "patch", pairs)
     line = jnp.concatenate(parts, axis=0)
     parts = [line]
-    for k in range(2, patches, 2):
+    for k in range(3, patches, 2):
         parts.append(swap(line, "patch", k))
     near = jnp.concatenate(parts, axis=0)
     far = swap(near, "patch", 1)

time: 56.7 us -> 56 us (0.988)
  starting transfers between devices: 20.7 us -> 19.6 us
    ppermute x16, starting transfers between devices: 17.4 us -> 16.8 us  [swap(): return lax.ppermute(value, axis, [(i, i ^ bit) for i in range(count)])]
where the time goes in v4:
time: 56 us; the launch traced here: 55.9 us
  Pallas kernels  19.8 us (35%)
  starting transfers between devices  19.6 us (35%)
  waiting for transfers between devices  14.1 us (25%)
  local copies, waits for them, and re-layouts  1.2 us (2%)
  between operations  1.16 us (2%)
    pallas_call x9, Pallas kernels, call(): pl.pallas_call(kernel, in_specs=in_specs or [VMEM] * len(args), out_specs...  19.8 us
    ppermute x16, starting transfers between devices, swap(): return lax.ppermute(value, axis, [(i, i ^ bit) for i in range(count)])  16.8 us
    ppermute x16, waiting for transfers between devices, swap(): return lax.ppermute(value, axis, [(i, i ^ bit) for i in range(count)])  14.1 us
    ppermute x2, starting transfers between devices, exchange(): across = lax.ppermute(cross, 'patch', pairs)  2.82 us
    unnamed x44, local copies, waits for them, and re-layouts  1.18 us
  transfers between devices with their start and end apart: 18, of which 5 were waited for; matrix products, arithmetic and copies ran while one was open for 0% of the time, Pallas kernels for 28%

profile of v4, /device:TPU:0, one launch (start us, length us, event | category | flops | bytes accessed | tf_op | source)
XLA Modules:
  0.0 55.9 jit_solution(6401842603373474924)
XLA Ops:
  0.7 1.1 %copy-done.4 = bf16[320,512]{1,0:T(8,128)(2,1)S(1)} copy-done((bf16[320,512]{1,0:T(8,128)(2,1)S(1)}, bf16[320,512]{1,0:T(8,128)(2,1)}, u32[]{:S(2)}) %copy-start.4) | copy-done | bytes 327704
  1.7 0.2 shard_map.175
  1.9 4.6 %collective-permute-start.2 = (bf16[16,512]{1,0:T(8,128)(2,1)S(1)}, bf16[16,512]{1,0:T(8,128)(2,1)S(1)}, u32[]{:S(2)}, u32[]{:S(2)}) collective-permute-start(bf16[16,512]{1,0:T(8,128)(2,1)S(1)} %get-tuple-element.38), channel_id=1, source_target_pairs={{0,25},{1,24},{2,27},{3,26},{4,29},{5,28},{6,31},{7,30},{8,17},{9,... | collective-permute-start | bytes 49160 | tf_op jit(solution)/shard_map/ppermute | solution.py:314
  6.5 0.9 %collective-permute-start = (bf16[16,512]{1,0:T(8,128)(2,1)S(1)}, bf16[16,512]{1,0:T(8,128)(2,1)S(1)}, u32[]{:S(2)}, u32[]{:S(2)}) collective-permute-start(bf16[16,512]{1,0:T(8,128)(2,1)S(1)} %get-tuple-element.38), channel_id=1, source_target_pairs={{0,9},{1,8},{2,11},{3,10},{4,13},{5,12},{6,15},{7,14},{8,1},{9,0},... | collective-permute-start | bytes 49160 | tf_op jit(solution)/shard_map/ppermute | solution.py:314
  7.4 2.2 %collective-permute-done = bf16[16,512]{1,0:T(8,128)(2,1)S(1)} collective-permute-done((bf16[16,512]{1,0:T(8,128)(2,1)S(1)}, bf16[16,512]{1,0:T(8,128)(2,1)S(1)}, u32[]{:S(2)}, u32[]{:S(2)}) %collective-permute-start) | collective-permute-done | bytes 16416 | tf_op jit(solution)/shard_map/ppermute | solution.py:314
  9.7 1.0 %collective-permute-done.1 = bf16[16,512]{1,0:T(8,128)(2,1)S(1)} collective-permute-done((bf16[16,512]{1,0:T(8,128)(2,1)S(1)}, bf16[16,512]{1,0:T(8,128)(2,1)S(1)}, u32[]{:S(2)}, u32[]{:S(2)}) %collective-permute-start.1) | collective-permute-done | bytes 16416 | tf_op jit(solution)/shard_map/ppermute | solution.py:314
  10.7 1.7 %collective-permute-start.3 = (bf16[64,512]{1,0:T(8,128)(2,1)S(1)}, bf16[64,512]{1,0:T(8,128)(2,1)S(1)}, u32[]{:S(2)}, u32[]{:S(2)}) collective-permute-start(bf16[64,512]{1,0:T(8,128)(2,1)S(1)} %get-tuple-element.81), channel_id=1, source_target_pairs={{0,3},{1,2},{2,1},{3,0},{4,7},{5,6},{6,5},{7,4},{8,11},{9,10},{10,... | collective-permute-start | bytes 196616 | tf_op jit(solution)/shard_map/ppermute | solution.py:314
  12.5 1.7 %collective-permute-start.7 = (bf16[64,512]{1,0:T(8,128)(2,1)S(1)}, bf16[64,512]{1,0:T(8,128)(2,1)S(1)}, u32[]{:S(2)}, u32[]{:S(2)}) collective-permute-start(bf16[64,512]{1,0:T(8,128)(2,1)S(1)} %get-tuple-element.44), channel_id=1, source_target_pairs={{0,7},{1,2},{2,1},{3,4},{4,3},{5,6},{6,5},{7,0},{8,15},{9,10},{10,... | collective-permute-start | bytes 196616 | tf_op jit(solution)/shard_map/ppermute | solution.py:325
  14.1 0.6 %shard_map.176 = (bf16[512,512]{1,0:T(8,128)(2,1)S(1)}, bf16[128,512]{1,0:T(8,128)(2,1)S(1)}, bf16[512,512]{1,0:T(8,128)(2,1)S(1)}, bf16[512,512]{1,0:T(8,128)(2,1)S(1)}) custom-call(bf16[320,512]{1,0:T(8,128)(2,1)S(1)} %copy-done.5, bf16[2,1536,512]{2,1,0:T(8,128)(2,1)S(1)} %copy-done, f32[2,512]{1,0:T(2,128)S(1)} %copy-done.8, ...), custom_call_target="tpu_custom_call" | custom-call | flops 335544320 | bytes 4194304 | tf_op jit(solution)/shard_map/pallas_call | solution.py:94
  14.7 1.1 %collective-permute-start.5 = (bf16[64,512]{1,0:T(8,128)(2,1)S(1)}, bf16[64,512]{1,0:T(8,128)(2,1)S(1)}, u32[]{:S(2)}, u32[]{:S(2)}) collective-permute-start(bf16[64,512]{1,0:T(8,128)(2,1)S(1)} %get-tuple-element.81), channel_id=1, source_target_pairs={{0,7},{1,6},{2,5},{3,4},{4,3},{5,2},{6,1},{7,0},{8,15},{9,14},{10,... | collective-permute-start | bytes 196616 | tf_op jit(solution)/shard_map/ppermute | solution.py:314
  15.8 0.7 %collective-permute-start.4 = (bf16[64,512]{1,0:T(8,128)(2,1)S(1)}, bf16[64,512]{1,0:T(8,128)(2,1)S(1)}, u32[]{:S(2)}, u32[]{:S(2)}) collective-permute-start(bf16[64,512]{1,0:T(8,128)(2,1)S(1)} %get-tuple-element.81), channel_id=1, source_target_pairs={{0,5},{1,4},{2,7},{3,6},{4,1},{5,0},{6,3},{7,2},{8,13},{9,12},{10,... | collective-permute-start | bytes 196616 | tf_op jit(solution)/shard_map/ppermute | solution.py:314
  16.5 4.1 %collective-permute-done.4 = bf16[64,512]{1,0:T(8,128)(2,1)S(1)} collective-permute-done((bf16[64,512]{1,0:T(8,128)(2,1)S(1)}, bf16[64,512]{1,0:T(8,128)(2,1)S(1)}, u32[]{:S(2)}, u32[]{:S(2)}) %collective-permute-start.4) | collective-permute-done | bytes 65568 | tf_op jit(solution)/shard_map/ppermute | solution.py:314
  20.6 0.2 collective-permute-start.8
  20.8 0.0 copy-start.1
  20.9 5.5 %shard_map.177 = (bf16[2048,512]{1,0:T(8,128)(2,1)S(1)}, f32[320,512]{1,0:T(8,128)S(1)}) custom-call(bf16[2048,512]{1,0:T(8,128)(2,1)S(1)} %copy-done.14, s32[1,2048]{1,0:T(1,128)S(1)} %bitcast.11, s32[1,2048]{1,0:T(1,128)S(1)} %bitcast.13, f32[2,512]{1,0:T(2,128)S(1)} %copy-done.9, bf16[2,1536,512]{2,1,0:T(8,128)(2,1)S(1)} %copy-done, ...), custom_call_target="tpu_custom_call" | custom-call | flops 4429185024 | bytes 4194304 | tf_op jit(solution)/shard_map/pallas_call | solution.py:94
  26.5 1.8 %shard_map.178 = (f32[512,512]{1,0:T(8,128)S(1)}, bf16[512,256]{1,0:T(8,128)(2,1)S(1)}, bf16[16,512]{1,0:T(8,128)(2,1)S(1)}, f32[16,512]{1,0:T(8,128)S(1)}, bf16...) custom-call(bf16[512,512]{1,0:T(8,128)(2,1)S(1)} %copy-done.6, s32[1,512]{1,0:T(1,128)S(1)} %bitcast.5, ...), custom_call_target="tpu_custom_call" | custom-call | flops 973078528 | bytes 4194304 | tf_op jit(solution)/shard_map/pallas_call | solution.py:94
  28.3 1.6 %shard_map.179 = (bf16[512,512]{1,0:T(8,128)(2,1)S(1)}, bf16[320,512]{1,0:T(8,128)(2,1)S(1)}, bf16[16,512]{1,0:T(8,128)(2,1)S(1)}, bf16[64,512]{1,0:T(8,128)(2,1)S(1)}, bf16[64,512]{1,0:T(8,128)(2,1)S(1)}) custom-call(bf16[512,512]{1,0:T(8,128)(2,1)S(1)} %copy-done.6, f32[512,512]{1,0:T(8,128)S(1)} %get-tuple-element.46.pre_ref, ...), custom_call_target="tpu_custom_call" | custom-call | flops 872415232 | bytes 4194304 | tf_op jit(solution)/shard_map/pallas_call | solution.py:94
  29.9 1.8 %collective-permute-start.11 = (bf16[16,512]{1,0:T(8,128)(2,1)S(1)}, bf16[16,512]{1,0:T(8,128)(2,1)S(1)}, u32[]{:S(2)}, u32[]{:S(2)}) collective-permute-start(bf16[16,512]{1,0:T(8,128)(2,1)S(1)} %get-tuple-element.54), channel_id=1, source_target_pairs={{0,25},{1,24},{2,27},{3,26},{4,29},{5,28},{6,31},{7,30},{8,17},{9,... | collective-permute-start | bytes 49160 | tf_op jit(solution)/shard_map/ppermute | solution.py:314
  31.6 0.8 %collective-permute-start.10 = (bf16[16,512]{1,0:T(8,128)(2,1)S(1)}, bf16[16,512]{1,0:T(8,128)(2,1)S(1)}, u32[]{:S(2)}, u32[]{:S(2)}) collective-permute-start(bf16[16,512]{1,0:T(8,128)(2,1)S(1)} %get-tuple-element.54), channel_id=1, source_target_pairs={{0,17},{1,16},{2,19},{3,18},{4,21},{5,20},{6,23},{7,22},{8,25},{9,... | collective-permute-start | bytes 49160 | tf_op jit(solution)/shard_map/ppermute | solution.py:314
  32.4 1.6 %collective-permute-start.9 = (bf16[16,512]{1,0:T(8,128)(2,1)S(1)}, bf16[16,512]{1,0:T(8,128)(2,1)S(1)}, u32[]{:S(2)}, u32[]{:S(2)}) collective-permute-start(bf16[16,512]{1,0:T(8,128)(2,1)S(1)} %get-tuple-element.54), channel_id=1, source_target_pairs={{0,9},{1,8},{2,11},{3,10},{4,13},{5,12},{6,15},{7,14},{8,1},{9,0},... | collective-permute-start | bytes 49160 | tf_op jit(solution)/shard_map/ppermute | solution.py:314
  34.0 2.1 %collective-permute-done.9 = bf16[16,512]{1,0:T(8,128)(2,1)S(1)} collective-permute-done((bf16[16,512]{1,0:T(8,128)(2,1)S(1)}, bf16[16,512]{1,0:T(8,128)(2,1)S(1)}, u32[]{:S(2)}, u32[]{:S(2)}) %collective-permute-start.9) | collective-permute-done | bytes 16416 | tf_op jit(solution)/shard_map/ppermute | solution.py:314
  36.1 1.1 %collective-permute-start.12 = (bf16[64,512]{1,0:T(8,128)(2,1)S(1)}, bf16[64,512]{1,0:T(8,128)(2,1)S(1)}, u32[]{:S(2)}, u32[]{:S(2)}) collective-permute-start(bf16[64,512]{1,0:T(8,128)(2,1)S(1)} %get-tuple-element.73), channel_id=1, source_target_pairs={{0,3},{1,2},{2,1},{3,0},{4,7},{5,6},{6,5},{7,4},{8,11},{9,10},{10,... | collective-permute-start | bytes 196616 | tf_op jit(solution)/shard_map/ppermute | solution.py:314
  37.3 0.4 collective-permute-start.15
  37.7 1.2 %collective-permute-start.16 = (bf16[64,512]{1,0:T(8,128)(2,1)S(1)}, bf16[64,512]{1,0:T(8,128)(2,1)S(1)}, u32[]{:S(2)}, u32[]{:S(2)}) collective-permute-start(bf16[64,512]{1,0:T(8,128)(2,1)S(1)} %get-tuple-element.61), channel_id=1, source_target_pairs={{0,7},{1,2},{2,1},{3,4},{4,3},{5,6},{6,5},{7,0},{8,15},{9,10},{10,... | collective-permute-start | bytes 196616 | tf_op jit(solution)/shard_map/ppermute | solution.py:325
  38.8 0.6 %shard_map.180 = (bf16[512,512]{1,0:T(8,128)(2,1)S(1)}, bf16[128,512]{1,0:T(8,128)(2,1)S(1)}, bf16[512,512]{1,0:T(8,128)(2,1)S(1)}, bf16[512,512]{1,0:T(8,128)(2,1)S(1)}) custom-call(bf16[320,512]{1,0:T(8,128)(2,1)S(1)} %get-tuple-element.55.h_ref, bf16[2,1536,512]{2,1,0:T(8,128)(2,1)S(1)} %copy-done, f32[2,512]{1,0:T(2,128)S(1)} %copy-done.8, ...), custom_call_target="tpu_custom_call" | custom-call | flops 335544320 | bytes 4194304 | tf_op jit(solution)/shard_map/pallas_call | solution.py:94
  39.4 1.5 %collective-permute-start.14 = (bf16[64,512]{1,0:T(8,128)(2,1)S(1)}, bf16[64,512]{1,0:T(8,128)(2,1)S(1)}, u32[]{:S(2)}, u32[]{:S(2)}) collective-permute-start(bf16[64,512]{1,0:T(8,128)(2,1)S(1)} %get-tuple-element.73), channel_id=1, source_target_pairs={{0,7},{1,6},{2,5},{3,4},{4,3},{5,2},{6,1},{7,0},{8,15},{9,14},{10,... | collective-permute-start | bytes 196616 | tf_op jit(solution)/shard_map/ppermute | solution.py:314
  40.9 0.3 collective-permute-start.13
  41.2 4.7 %collective-permute-done.13 = bf16[64,512]{1,0:T(8,128)(2,1)S(1)} collective-permute-done((bf16[64,512]{1,0:T(8,128)(2,1)S(1)}, bf16[64,512]{1,0:T(8,128)(2,1)S(1)}, u32[]{:S(2)}, u32[]{:S(2)}) %collective-permute-start.13) | collective-permute-done | bytes 65568 | tf_op jit(solution)/shard_map/ppermute | solution.py:314
  45.9 0.1 collective-permute-start.17
  46.0 5.7 %shard_map.181 = (bf16[2048,512]{1,0:T(8,128)(2,1)S(1)}, f32[320,512]{1,0:T(8,128)S(1)}) custom-call(bf16[2048,512]{1,0:T(8,128)(2,1)S(1)} %get-tuple-element.52.fine_ref.e_ref, s32[1,2048]{1,0:T(1,128)S(1)} %bitcast.12, s32[1,2048]{1,0:T(1,128)S(1)} %bitcast.14, f32[2,512]{1,0:T(2,128)S(1)} %copy-done.9, bf16[2,1536,512]{2,1,0:T(8,128)(2,1)S(1)} %copy-done, ...), custom_call_target="tpu_custom_call" | custom-call | flops 4429185024 | bytes 4194304 | tf_op jit(solution)/shard_map/pallas_call | solution.py:94
  51.7 1.8 %shard_map.182 = (f32[512,512]{1,0:T(8,128)S(1)}, bf16[512,256]{1,0:T(8,128)(2,1)S(1)}, bf16[16,512]{1,0:T(8,128)(2,1)S(1)}, f32[16,512]{1,0:T(8,128)S(1)}, bf16...) custom-call(bf16[512,512]{1,0:T(8,128)(2,1)S(1)} %get-tuple-element.53.e_ref, s32[1,512]{1,0:T(1,128)S(1)} %bitcast.6, ...), custom_call_target="tpu_custom_call" | custom-call | flops 973078528 | bytes 4194304 | tf_op jit(solution)/shard_map/pallas_call | solution.py:94
  53.5 2.2 %shard_map.183 = (bf16[512,512]{1,0:T(8,128)(2,1)}, bf16[320,512]{1,0:T(8,128)(2,1)}, bf16[2048,512]{1,0:T(8,128)(2,1)}) custom-call(bf16[512,512]{1,0:T(8,128)(2,1)S(1)} %get-tuple-element.53.e_ref, f32[512,512]{1,0:T(8,128)S(1)} %get-tuple-element.63.pre_ref, bf16[512,256]{1,0:T(8,128)(2,1)S(1)} %get-tuple-element.64.far_hot_ref, ...), custom_call_target="tpu_custom_call" | custom-call | flops 872415232 | bytes 4194304 | tf_op jit(solution)/shard_map/pallas_call | solution.py:94
  (61 shorter events, 0.2 us)
Async XLA Ops:
  0.6 13.5 %copy-start.2 = (bf16[2,512,512]{2,1,0:T(8,128)(2,1)S(1)}, bf16[2,512,512]{2,1,0:T(8,128)(2,1)}, u32[]{:S(2)}) copy-start(bf16[2,512,512]{2,1,0:T(8,128)(2,1)} %second_ref.3) | copy-start | bytes 3145732
  1.7 12.4 %copy-start = (bf16[2,1536,512]{2,1,0:T(8,128)(2,1)S(1)}, bf16[2,1536,512]{2,1,0:T(8,128)(2,1)}, u32[]{:S(2)}) copy-start(bf16[2,1536,512]{2,1,0:T(8,128)(2,1)} %first_ref.15) | copy-start | bytes 9437188
  1.7 12.4 %copy-start.5 = (bf16[320,512]{1,0:T(8,128)(2,1)S(1)}, bf16[320,512]{1,0:T(8,128)(2,1)}, u32[]{:S(2)}) copy-start(bf16[320,512]{1,0:T(8,128)(2,1)} %h_ref.7) | copy-start | bytes 983044
  1.7 12.4 %copy-start.8 = (f32[2,512]{1,0:T(2,128)S(1)}, f32[2,512]{1,0:T(2,128)}, u32[]{:S(2)}) copy-start(f32[2,512]{1,0:T(2,128)} %bias_ref.7) | copy-start | bytes 12292
  1.9 8.8 %collective-permute-start.2 = (bf16[16,512]{1,0:T(8,128)(2,1)S(1)}, bf16[16,512]{1,0:T(8,128)(2,1)S(1)}, u32[]{:S(2)}, u32[]{:S(2)}) collective-permute-start(bf16[16,512]{1,0:T(8,128)(2,1)S(1)} %get-tuple-element.38), channel_id=1, source_target_pairs={{0,25},{1,24},{2,27},{3,26},{4,29},{5,28},{6,31},{7,30},{8,17},{9,... | collective-permute-start | bytes 49160 | tf_op jit(solution)/shard_map/ppermute | solution.py:314
  6.5 4.2 %collective-permute-start.1 = (bf16[16,512]{1,0:T(8,128)(2,1)S(1)}, bf16[16,512]{1,0:T(8,128)(2,1)S(1)}, u32[]{:S(2)}, u32[]{:S(2)}) collective-permute-start(bf16[16,512]{1,0:T(8,128)(2,1)S(1)} %get-tuple-element.38), channel_id=1, source_target_pairs={{0,17},{1,16},{2,19},{3,18},{4,21},{5,20},{6,23},{7,22},{8,25},{9,... | collective-permute-start | bytes 49160 | tf_op jit(solution)/shard_map/ppermute | solution.py:314
  6.5 3.2 %collective-permute-start = (bf16[16,512]{1,0:T(8,128)(2,1)S(1)}, bf16[16,512]{1,0:T(8,128)(2,1)S(1)}, u32[]{:S(2)}, u32[]{:S(2)}) collective-permute-start(bf16[16,512]{1,0:T(8,128)(2,1)S(1)} %get-tuple-element.38), channel_id=1, source_target_pairs={{0,9},{1,8},{2,11},{3,10},{4,13},{5,12},{6,15},{7,14},{8,1},{9,0},... | collective-permute-start | bytes 49160 | tf_op jit(solution)/shard_map/ppermute | solution.py:314
  10.7 5.8 %collective-permute-start.3 = (bf16[64,512]{1,0:T(8,128)(2,1)S(1)}, bf16[64,512]{1,0:T(8,128)(2,1)S(1)}, u32[]{:S(2)}, u32[]{:S(2)}) collective-permute-start(bf16[64,512]{1,0:T(8,128)(2,1)S(1)} %get-tuple-element.81), channel_id=1, source_target_pairs={{0,3},{1,2},{2,1},{3,0},{4,7},{5,6},{6,5},{7,4},{8,11},{9,10},{10,... | collective-permute-start | bytes 196616 | tf_op jit(solution)/shard_map/ppermute | solution.py:314
  12.4 8.4 %collective-permute-start.6 = (bf16[64,512]{1,0:T(8,128)(2,1)S(1)}, bf16[64,512]{1,0:T(8,128)(2,1)S(1)}, u32[]{:S(2)}, u32[]{:S(2)}) collective-permute-start(bf16[64,512]{1,0:T(8,128)(2,1)S(1)} %get-tuple-element.43), channel_id=1, source_target_pairs={{0,1},{1,0},{2,3},{3,2},{4,5},{5,4},{6,7},{7,6},{8,9},{9,8},{10,11... | collective-permute-start | bytes 196616 | tf_op jit(solution)/shard_map/ppermute | solution.py:314
  12.4 8.4 %copy-start.9 = (f32[2,512]{1,0:T(2,128)S(1)}, f32[2,512]{1,0:T(2,128)}, u32[]{:S(2)}) copy-start(f32[2,512]{1,0:T(2,128)} %gain_ref.7) | copy-start | bytes 12292
  12.4 8.4 %copy-start.14 = (bf16[2048,512]{1,0:T(8,128)(2,1)S(1)}, bf16[2048,512]{1,0:T(8,128)(2,1)}, u32[]{:S(2)}) copy-start(bf16[2048,512]{1,0:T(8,128)(2,1)} %e_ref.3) | copy-start | bytes 6291460
  12.4 8.4 %copy-start.15 = (s32[2048]{0:T(1024)S(1)}, s32[2048]{0:T(1024)}, u32[]{:S(2)}) copy-start(s32[2048]{0:T(1024)} %param.19) | copy-start | bytes 24580
  12.4 8.4 %copy-start.16 = (s32[2048]{0:T(1024)S(1)}, s32[2048]{0:T(1024)}, u32[]{:S(2)}) copy-start(s32[2048]{0:T(1024)} %param.20) | copy-start | bytes 24580
  12.5 8.3 %collective-permute-start.7 = (bf16[64,512]{1,0:T(8,128)(2,1)S(1)}, bf16[64,512]{1,0:T(8,128)(2,1)S(1)}, u32[]{:S(2)}, u32[]{:S(2)}) collective-permute-start(bf16[64,512]{1,0:T(8,128)(2,1)S(1)} %get-tuple-element.44), channel_id=1, source_target_pairs={{0,7},{1,2},{2,1},{3,4},{4,3},{5,6},{6,5},{7,0},{8,15},{9,10},{10,... | collective-permute-start | bytes 196616 | tf_op jit(solution)/shard_map/ppermute | solution.py:325
  14.7 5.9 %collective-permute-start.5 = (bf16[64,512]{1,0:T(8,128)(2,1)S(1)}, bf16[64,512]{1,0:T(8,128)(2,1)S(1)}, u32[]{:S(2)}, u32[]{:S(2)}) collective-permute-start(bf16[64,512]{1,0:T(8,128)(2,1)S(1)} %get-tuple-element.81), channel_id=1, source_target_pairs={{0,7},{1,6},{2,5},{3,4},{4,3},{5,2},{6,1},{7,0},{8,15},{9,14},{10,... | collective-permute-start | bytes 196616 | tf_op jit(solution)/shard_map/ppermute | solution.py:314
  15.8 4.8 %collective-permute-start.4 = (bf16[64,512]{1,0:T(8,128)(2,1)S(1)}, bf16[64,512]{1,0:T(8,128)(2,1)S(1)}, u32[]{:S(2)}, u32[]{:S(2)}) collective-permute-start(bf16[64,512]{1,0:T(8,128)(2,1)S(1)} %get-tuple-element.81), channel_id=1, source_target_pairs={{0,5},{1,4},{2,7},{3,6},{4,1},{5,0},{6,3},{7,2},{8,13},{9,12},{10,... | collective-permute-start | bytes 196616 | tf_op jit(solution)/shard_map/ppermute | solution.py:314
  20.6 7.7 %collective-permute-start.8 = (bf16[256,512]{1,0:T(8,128)(2,1)S(1)}, bf16[256,512]{1,0:T(8,128)(2,1)S(1)}, u32[]{:S(2)}, u32[]{:S(2)}) collective-permute-start(bf16[256,512]{1,0:T(8,128)(2,1)S(1)} %constant_dynamic-update-slice_fusion.4.near_ref), channel_id=1, source_target_pairs={{0,1},{1,0},{2,3},{3,2},{4,5},{5,4},{6,7},{7,6},{8,9},{9,8},{10,11... | collective-permute-start | bytes 786440 | tf_op jit(solution)/shard_map/ppermute | solution.py:314
  20.8 5.6 %copy-start.1 = (bf16[2,1024,512]{2,1,0:T(8,128)(2,1)S(1)}, bf16[2,1024,512]{2,1,0:T(8,128)(2,1)}, u32[]{:S(2)}) copy-start(bf16[2,1024,512]{2,1,0:T(8,128)(2,1)} %node_first_ref.7) | copy-start | bytes 6291460
  20.8 5.6 %copy-start.3 = (bf16[2,512,512]{2,1,0:T(8,128)(2,1)S(1)}, bf16[2,512,512]{2,1,0:T(8,128)(2,1)}, u32[]{:S(2)}) copy-start(bf16[2,512,512]{2,1,0:T(8,128)(2,1)} %node_second_ref.3) | copy-start | bytes 3145732
  20.8 5.6 %copy-start.6 = (bf16[512,512]{1,0:T(8,128)(2,1)S(1)}, bf16[512,512]{1,0:T(8,128)(2,1)}, u32[]{:S(2)}) copy-start(bf16[512,512]{1,0:T(8,128)(2,1)} %e_ref.5) | copy-start | bytes 1572868
  20.9 5.6 %copy-start.7 = (f32[2,512]{1,0:T(2,128)S(1)}, f32[2,512]{1,0:T(2,128)}, u32[]{:S(2)}) copy-start(f32[2,512]{1,0:T(2,128)} %node_gain_ref.7) | copy-start | bytes 12292
  20.9 5.6 %copy-start.10 = (f32[2,512]{1,0:T(2,128)S(1)}, f32[2,512]{1,0:T(2,128)}, u32[]{:S(2)}) copy-start(f32[2,512]{1,0:T(2,128)} %node_bias_ref.3) | copy-start | bytes 12292
  20.9 5.6 %copy-start.11 = (s32[512,1]{0,1:T(1,128)S(1)}, s32[512,1]{0,1:T(1,128)}, u32[]{:S(2)}) copy-start(s32[512,1]{0,1:T(1,128)} %param.21) | copy-start | bytes 6148
  29.9 6.2 %collective-permute-start.11 = (bf16[16,512]{1,0:T(8,128)(2,1)S(1)}, bf16[16,512]{1,0:T(8,128)(2,1)S(1)}, u32[]{:S(2)}, u32[]{:S(2)}) collective-permute-start(bf16[16,512]{1,0:T(8,128)(2,1)S(1)} %get-tuple-element.54), channel_id=1, source_target_pairs={{0,25},{1,24},{2,27},{3,26},{4,29},{5,28},{6,31},{7,30},{8,17},{9,... | collective-permute-start | bytes 49160 | tf_op jit(solution)/shard_map/ppermute | solution.py:314
  31.6 4.5 %collective-permute-start.10 = (bf16[16,512]{1,0:T(8,128)(2,1)S(1)}, bf16[16,512]{1,0:T(8,128)(2,1)S(1)}, u32[]{:S(2)}, u32[]{:S(2)}) collective-permute-start(bf16[16,512]{1,0:T(8,128)(2,1)S(1)} %get-tuple-element.54), channel_id=1, source_target_pairs={{0,17},{1,16},{2,19},{3,18},{4,21},{5,20},{6,23},{7,22},{8,25},{9,... | collective-permute-start | bytes 49160 | tf_op jit(solution)/shard_map/ppermute | solution.py:314
  32.4 3.7 %collective-permute-start.9 = (bf16[16,512]{1,0:T(8,128)(2,1)S(1)}, bf16[16,512]{1,0:T(8,128)(2,1)S(1)}, u32[]{:S(2)}, u32[]{:S(2)}) collective-permute-start(bf16[16,512]{1,0:T(8,128)(2,1)S(1)} %get-tuple-element.54), channel_id=1, source_target_pairs={{0,9},{1,8},{2,11},{3,10},{4,13},{5,12},{6,15},{7,14},{8,1},{9,0},... | collective-permute-start | bytes 49160 | tf_op jit(solution)/shard_map/ppermute | solution.py:314
  36.1 5.1 %collective-permute-start.12 = (bf16[64,512]{1,0:T(8,128)(2,1)S(1)}, bf16[64,512]{1,0:T(8,128)(2,1)S(1)}, u32[]{:S(2)}, u32[]{:S(2)}) collective-permute-start(bf16[64,512]{1,0:T(8,128)(2,1)S(1)} %get-tuple-element.73), channel_id=1, source_target_pairs={{0,3},{1,2},{2,1},{3,0},{4,7},{5,6},{6,5},{7,4},{8,11},{9,10},{10,... | collective-permute-start | bytes 196616 | tf_op jit(solution)/shard_map/ppermute | solution.py:314
  37.3 8.8 %collective-permute-start.15 = (bf16[64,512]{1,0:T(8,128)(2,1)S(1)}, bf16[64,512]{1,0:T(8,128)(2,1)S(1)}, u32[]{:S(2)}, u32[]{:S(2)}) collective-permute-start(bf16[64,512]{1,0:T(8,128)(2,1)S(1)} %get-tuple-element.60), channel_id=1, source_target_pairs={{0,1},{1,0},{2,3},{3,2},{4,5},{5,4},{6,7},{7,6},{8,9},{9,8},{10,11... | collective-permute-start | bytes 196616 | tf_op jit(solution)/shard_map/ppermute | solution.py:314
  37.7 8.4 %collective-permute-start.16 = (bf16[64,512]{1,0:T(8,128)(2,1)S(1)}, bf16[64,512]{1,0:T(8,128)(2,1)S(1)}, u32[]{:S(2)}, u32[]{:S(2)}) collective-permute-start(bf16[64,512]{1,0:T(8,128)(2,1)S(1)} %get-tuple-element.61), channel_id=1, source_target_pairs={{0,7},{1,2},{2,1},{3,4},{4,3},{5,6},{6,5},{7,0},{8,15},{9,10},{10,... | collective-permute-start | bytes 196616 | tf_op jit(solution)/shard_map/ppermute | solution.py:325
  39.4 6.5 %collective-permute-start.14 = (bf16[64,512]{1,0:T(8,128)(2,1)S(1)}, bf16[64,512]{1,0:T(8,128)(2,1)S(1)}, u32[]{:S(2)}, u32[]{:S(2)}) collective-permute-start(bf16[64,512]{1,0:T(8,128)(2,1)S(1)} %get-tuple-element.73), channel_id=1, source_target_pairs={{0,7},{1,6},{2,5},{3,4},{4,3},{5,2},{6,1},{7,0},{8,15},{9,14},{10,... | collective-permute-start | bytes 196616 | tf_op jit(solution)/shard_map/ppermute | solution.py:314
  40.9 5.0 %collective-permute-start.13 = (bf16[64,512]{1,0:T(8,128)(2,1)S(1)}, bf16[64,512]{1,0:T(8,128)(2,1)S(1)}, u32[]{:S(2)}, u32[]{:S(2)}) collective-permute-start(bf16[64,512]{1,0:T(8,128)(2,1)S(1)} %get-tuple-element.73), channel_id=1, source_target_pairs={{0,5},{1,4},{2,7},{3,6},{4,1},{5,0},{6,3},{7,2},{8,13},{9,12},{10,... | collective-permute-start | bytes 196616 | tf_op jit(solution)/shard_map/ppermute | solution.py:314
  45.9 7.6 %collective-permute-start.17 = (bf16[256,512]{1,0:T(8,128)(2,1)S(1)}, bf16[256,512]{1,0:T(8,128)(2,1)S(1)}, u32[]{:S(2)}, u32[]{:S(2)}) collective-permute-start(bf16[256,512]{1,0:T(8,128)(2,1)S(1)} %constant_dynamic-update-slice_fusion.15.near_ref), channel_id=1, source_target_pairs={{0,1},{1,0},{2,3},{3,2},{4,5},{5,4},{6,7},{7,6},{8,9},{9,8},{10,11... | collective-permute-start | bytes 786440 | tf_op jit(solution)/shard_map/ppermute | solution.py:314
  (3 other events, 12.2 us)
